TPU v7x, 128 devices: a whole 4x4x4 slice. The times are simulated.
128 devices in a mesh: seq: 32 (over y, z, core), head: 4 (over x).
Axes of the slice: x: 4, y: 4, z: 4, core: 2. Of those that a mesh axis runs over, the one named last changes fastest.
Arguments:
- queries: bfloat16 [2, 64, 64, 128], P(None, 'head'), may hold values from -9 to 9
- cache_keys: bfloat16 [2, 8, 32768, 128], P(None, 'head', 'seq'), may hold values from -10 to 10
- cache_values: bfloat16 [2, 8, 32768, 128], P(None, 'head', 'seq'), may hold values from -6 to 6
- new_keys: bfloat16 [2, 8, 64, 128], P(None, 'head'), may hold values from -20 to 20
- new_values: bfloat16 [2, 8, 64, 128], P(None, 'head'), may hold values from -6 to 6
- parents: int32 [2, 64], replicated, may hold values from 0 to 62, as said below
- path: int32 [2, 6], replicated, may hold values from 0 to 63, as said below
- lengths: int32 [2], replicated, may hold values from 8192 to 32768, as said below
- draft_tokens: int32 [2, 64], replicated, may hold values from 0 to 65535
- residual: bfloat16 [2, 64, 8192], P(None, None, 'seq'), may hold values from -8 to 8
- out_weight: bfloat16 [8192, 8192], P('head', 'seq'), may hold values from -0.0625 to 0.0625
- norm_gain: bfloat16 [8192], P('seq'), may hold values from 0.5 to 1.5
- vocab_weight: bfloat16 [8192, 65536], P(None, ('seq', 'head')), may hold values from -3 to 3
Outputs:
- path_logits: float32 [2, 6, 65536], P(None, None, ('seq', 'head'))
- draft_logprob: float32 [2, 64], replicated
Inputs may be any that keep to these rules, and one draw needn't show every extreme that they name: parents[b, 0] is 0; for every other node n, parents[b, n] is a smaller node number. path[b] lists 6 different nodes: node 0 first, and each later entry is a child (by parents) of the entry before it. `lengths`: at least one sequence uses all 32768 cache positions.
All inputs are finite; a program needn't handle non-finite values.
Results may differ from a plain program's by a relative error of at most 0.006.
Values may be sent and summed in bfloat16 or wider, within the bound.
No kernel may reach another device: no remote copies, remote signals or barrier semaphores. Data moves between devices by JAX's collectives and lax.ppermute only.
A program may use at most 64 MiB of HBM per device.

v0:
```python
import math

import jax
import jax.numpy as jnp
from jax import lax
from jax.sharding import Mesh
from jax.sharding import PartitionSpec as P

D = 8192
SEQ = ("seq_0", "seq_1", "seq_2")
SEQ_HEAD = ("seq_0", "seq_1", "seq_2", "head")


lowest = -1e30
epsilon = 1e-05


def from_everyone(x, axis):
    size = lax.axis_size(axis)
    return lax.all_to_all(jnp.broadcast_to(x[None], (size, *x.shape)), axis, 0, 0, tiled=True)


def over_copies(x, axis):
    return from_everyone(x, axis).max(axis=0)


def split_up(x, dim, size):
    lengths = x.shape
    parts = x.reshape(*lengths[:dim], size, lengths[dim] // size, *lengths[dim + 1 :])
    return jnp.moveaxis(parts, dim, 0)


def sum_at_owner(x, axis, dim):
    size = lax.axis_size(axis)
    parts = lax.all_to_all(split_up(x, dim, size), axis, 0, 0, tiled=True)
    return jnp.sum(parts, axis=0)


def sent_together(arrays, axis, dim, along):
    widths = [math.prod(a.shape[along:]) for a in arrays]
    both = jnp.concatenate(
        [a.reshape(*a.shape[:along], w) for a, w in zip(arrays, widths)], axis=along
    )
    result = sum_at_owner(both, axis, dim)
    parts = jnp.split(result, [sum(widths[:k]) for k in range(1, len(widths))], axis=along)
    return tuple(
        (b.reshape(*result.shape[:along], *a.shape[along:]) for a, b in zip(arrays, parts))
    )


def laid_out(parts, dim):
    parts = jnp.moveaxis(parts, 0, dim)
    lengths = parts.shape
    return parts.reshape(*lengths[:dim], lengths[dim] * lengths[dim + 1], *lengths[dim + 2 :])


def collect(x, axis, dim):
    parts = from_everyone(x, axis)
    return laid_out(parts, dim)


def over_copies_2(x, axis):
    return from_everyone(x, axis).sum(axis=0)


def gathered_once(x, axis):
    leaves = jax.tree.leaves(x)
    turns = sorted(range(len(leaves)), key=lambda k: -leaves[k].size)
    width = (1, *leaves[turns[0]].shape)[-1]
    lines = [
        jnp.pad(leaves[k].reshape(-1), (0, -leaves[k].size % width)).reshape(-1, width)
        for k in turns
    ]
    both, at, found = (lax.all_gather(jnp.concatenate(lines), axis), 0, {})
    for k, line in zip(turns, lines):
        section = both[:, at : at + len(line)].reshape(len(both), -1)
        found[k] = section[:, : leaves[k].size].reshape(-1, *leaves[k].shape)
        at += len(line)
    numbers = iter(range(len(leaves)))
    return jax.tree.map(lambda _: found[next(numbers)], x)


def merged_by_axis(x, axes, combine):
    for axis in axes:
        pieces = gathered_once(x, axis)
        x = jax.tree.map(lambda part: part[0], pieces)
        for k in range(1, lax.axis_size(axis)):
            x = combine(x, jax.tree.map(lambda part: part[k], pieces))
    return x


def ancestors(parents):
    node_count = parents.shape[-1]
    node_ids = jnp.arange(node_count, dtype=jnp.int32)
    linked = (parents[..., :, None] == node_ids[None, None, :]).astype(jnp.float32)
    reached = jnp.maximum(linked, jnp.eye(node_count, dtype=jnp.float32)[None])
    for _ in range(node_count.bit_length()):
        reached = jnp.minimum(jnp.einsum("bij,bjk->bik", reached, reached), 1.0)
    return reached > 0.5


def block_state(scores, visible, values):
    masked = jnp.where(visible, scores, lowest)
    block_max = jnp.max(masked, axis=-1)
    weights = jnp.where(visible, jnp.exp(masked - block_max[..., None]), 0.0).astype(jnp.bfloat16)
    block_total = jnp.sum(weights.astype(jnp.float32), axis=-1)
    block_out = jnp.einsum("kqc,kcd->kqd", weights, values, preferred_element_type=jnp.float32)
    return (block_max, block_total, block_out)


def join_states(earlier, later):
    summit = jnp.maximum(earlier[0], later[0])
    damp_early = jnp.exp(earlier[0] - summit)
    damp_later = jnp.exp(later[0] - summit)
    total_joined = earlier[1] * damp_early + later[1] * damp_later
    out_joined = earlier[2] * damp_early[..., None] + later[2] * damp_later[..., None]
    return (summit, total_joined, out_joined)


def join_sums(earlier, later):
    summit = jnp.maximum(earlier[0], later[0])
    exp_joined = earlier[1] * jnp.exp(earlier[0] - summit) + later[1] * jnp.exp(later[0] - summit)
    return (summit, exp_joined, earlier[2] + later[2])


def on_device(
    queries,
    cache_keys,
    cache_values,
    new_keys,
    new_values,
    parents,
    path,
    lengths,
    draft_tokens,
    residual,
    out_weight,
    norm_gain,
    vocab_weight,
):
    batch_size, heads_local, node_count, head_dim = queries.shape
    kv_local = cache_keys.shape[1]
    span_local = cache_keys.shape[2]
    group_size = heads_local // kv_local
    score_scale = head_dim ** (-0.5)
    seq_index = lax.axis_index(SEQ)
    reached = ancestors(parents)
    is_owner = seq_index == 0
    offsets = seq_index * span_local + jnp.arange(span_local, dtype=jnp.int32)

    def per_sequence(entries):
        query_block, key_block, value_block, tree_keys, tree_values, reach_row, length = entries
        grouped = query_block.reshape(kv_local, group_size * node_count, head_dim)
        scores = (
            jnp.einsum("kqd,kcd->kqc", grouped, key_block, preferred_element_type=jnp.float32)
            * score_scale
        )
        live_keys = (offsets < length)[None, None, :]
        cache_state = block_state(scores, live_keys, value_block)
        tree_scores = (
            jnp.einsum("kqd,kcd->kqc", grouped, tree_keys, preferred_element_type=jnp.float32)
            * score_scale
        )
        tree_seen = jnp.logical_and(jnp.tile(reach_row, (group_size, 1))[None], is_owner)
        tree_state = block_state(tree_scores, tree_seen, tree_values)
        return join_states(cache_state, tree_state)

    maxima, totals, outputs = lax.map(
        per_sequence, (queries, cache_keys, cache_values, new_keys, new_values, reached, lengths)
    )
    weight_heads = out_weight.reshape(heads_local, head_dim, -1)
    highest = over_copies(maxima, SEQ)
    factors = jnp.exp(maxima - highest)
    scaled = (outputs * factors[..., None]).reshape(batch_size, heads_local, node_count, head_dim)
    summed = (totals * factors).reshape(batch_size, heads_local, node_count)
    share_out, share_total = sent_together((scaled, summed), SEQ, 2, 3)
    attention = (share_out / share_total[..., None]).astype(jnp.bfloat16)
    projected = jnp.einsum(
        "bhnd,hdc->bnc",
        collect(attention, SEQ, 2),
        weight_heads,
        preferred_element_type=jnp.float32,
    )
    vocab_local = vocab_weight.shape[1]
    projected = over_copies_2(projected, "head")
    stream = residual.astype(jnp.float32) + projected
    gain_part = norm_gain.astype(jnp.float32)
    square_sum = over_copies_2(jnp.sum(stream * stream, axis=-1), SEQ)
    normed = (stream * lax.rsqrt(square_sum / D + epsilon)[..., None] * gain_part).astype(
        jnp.bfloat16
    )
    portion = collect(normed, SEQ, 2)
    flat_part = portion.reshape(batch_size * node_count, portion.shape[2])
    logits = jnp.dot(flat_part, vocab_weight, preferred_element_type=jnp.float32)
    logits = logits.reshape(batch_size, node_count, vocab_local)
    vocab_first = lax.axis_index(SEQ_HEAD) * vocab_local
    vocab_ids = jnp.arange(vocab_local, dtype=jnp.int32) + vocab_first
    picked = jnp.sum(jnp.where(draft_tokens[..., None] == vocab_ids, logits, 0.0), axis=-1)
    local_max = jnp.max(logits, axis=-1)
    local_sum = jnp.sum(jnp.exp(logits - local_max[..., None]), axis=-1)
    vocab_top, exp_sums, picked = merged_by_axis(
        (local_max, local_sum, picked), SEQ_HEAD, join_sums
    )
    draft_logprob = picked - (vocab_top + jnp.log(exp_sums))
    path_logits = jnp.take_along_axis(logits, path[:, :, None], axis=1)
    return (path_logits, draft_logprob)


def solution(mesh):
    torus = Mesh(
        mesh.devices.reshape(4, 4, 2, mesh.shape["head"]), ("seq_0", "seq_1", "seq_2", "head")
    )
    in_specs = (
        P(None, "head", None, None),
        P(None, "head", SEQ, None),
        P(None, "head", SEQ, None),
        P(None, "head", None, None),
        P(None, "head", None, None),
        P(),
        P(),
        P(),
        P(),
        P(None, None, SEQ),
        P("head", SEQ),
        P(SEQ),
        P(None, SEQ_HEAD),
    )
    out_specs = (P(None, None, SEQ_HEAD), P())
    return jax.shard_map(
        on_device, mesh=torus, in_specs=in_specs, out_specs=out_specs, check_vma=False
    )
```

profile of v0, /device:TPU:1, one launch (start us, length us, event | category | flops | bytes accessed | tf_op | source)
XLA Modules:
  0.0 197.1 jit_solution(6454780422807597039)
XLA Ops:
  0.7 1.0 convolution_minimum_fusion.6
  2.0 0.3 convolution_minimum_fusion.2
  2.2 0.3 fusion.30
  2.5 17.6 %while.15 = (s32[]{:T(128)}, f32[2,2,512]{2,1,0:T(2,128)S(1)}, f32[2,2,512]{2,1,0:T(2,128)S(1)}, f32[2,2,512,128]{3,2,1,0:T(8,128)S(1)}, s32[2]{0:T(128)}, /*ind...) while((s32[]{:T(128)}, f32[2,2,512]{2,1,0:T(2,128)S(1)}, ...), condition=%wide.region_5.6_spmd.clone, body=%wide.region_0.5_spmd.clone.sunk | while | flops 587279360 | bytes 21873904 | solution.py:168
  2.6 1.0 constant_dynamic-slice_fusion.4
  3.9 1.0 fusion.120
  4.9 1.2 dynamic_slice.68
  6.2 0.6 add_compare_fusion.2
  6.8 2.0 fusion.121
  8.7 1.2 convert_reduce_fusion.5
  9.9 0.3 convolution_multiply_fusion.4
  10.3 1.1 fusion.124
  11.4 1.0 constant_dynamic-slice_fusion.4
  12.7 1.0 fusion.120
  13.7 1.2 dynamic_slice.68
  15.0 0.6 add_compare_fusion.2
  15.6 2.0 fusion.121
  17.5 1.2 convert_reduce_fusion.5
  18.8 0.3 convolution_multiply_fusion.4
  19.1 1.1 fusion.124
  20.3 18.3 %all_to_all.30 = f32[32,2,2,512]{3,2,1,0:T(2,128)S(1)} all-to-all(f32[32,2,2,512]{3,2,1,0:T(2,128)S(1)} %broadcast_in_dim.105), channel_id=1, replica_groups=mesh['seq_0'=4,'seq_1'=4,'seq_2'=2,'head'=4] {'seq_0','seq_1','seq_2'}, dimensions={0} | all-to-all | bytes 524288 | tf_op jit(solution)/shard_map/all_to_all | solution.py:20
  38.7 1.6 concatenate.30
  40.3 0.3 broadcast_multiply_fusion
  40.6 1.1 maximum_bitcast_fusion
  41.7 1.2 copy.53
  42.9 31.6 %all_to_all.31 = f32[32,2,16,2,129]{4,3,2,1,0:T(2,128)S(1)} all-to-all(f32[32,2,16,2,129]{4,3,2,1,0:T(2,128)S(1)} %copy.53), channel_id=1, replica_groups=mesh['seq_0'=4,'seq_1'=4,'seq_2'=2,'head'=4] {'seq_0','seq_1','seq_2'}, dimensions={0} | all-to-all | bytes 2113536 | tf_op jit(solution)/shard_map/all_to_all | solution.py:35
  74.6 1.0 reduce_sum.76
  75.9 0.5 broadcast_in_dim.106
  76.3 15.3 %all_to_all.32 = bf16[32,2,16,2,128]{4,3,2,1,0:T(2,128)(2,1)S(1)} all-to-all(bf16[32,2,16,2,128]{4,3,2,1,0:T(2,128)(2,1)S(1)} %broadcast_in_dim.106), channel_id=1, replica_groups=mesh['seq_0'=4,'seq_1'=4,'seq_2'=2,'head'=4] {'seq_0','seq_1','seq_2'}, dimensions={0} | all-to-all | bytes 1048576 | tf_op jit(solution)/shard_map/all_to_all | solution.py:20
  91.7 0.5 copy.57
  92.2 0.3 convolution_bitcast_fusion
  92.6 13.1 %all_to_all.33 = f32[4,2,64,256]{3,2,1,0:T(8,128)S(1)} all-to-all(f32[4,2,64,256]{3,2,1,0:T(8,128)S(1)} %broadcast_in_dim.107), channel_id=1, replica_groups=mesh['seq_0'=4,'seq_1'=4,'seq_2'=2,'head'=4] {'head'}, dimensions={0} | all-to-all | bytes 1048576 | tf_op jit(solution)/shard_map/all_to_all | solution.py:20
  105.9 0.7 reshape.209
  106.6 4.6 %all-to-all-start.4 = ((f32[32,1,128]{2,1,0:T(1,128)}), f32[32,1,128]{2,1,0:T(1,128)S(1)}, u32[]{:S(2)}, u32[]{:S(2)}) async-start(f32[32,1,128]{2,1,0:T(1,128)} %reshape.209), calls=%async_computation.4 | async-start | bytes 32768 | tf_op jit(solution)/shard_map/all_to_all | solution.py:20
  111.2 7.0 %all-to-all-done.4 = f32[32,1,128]{2,1,0:T(1,128)S(1)} async-done(((f32[32,1,128]{2,1,0:T(1,128)}), f32[32,1,128]{2,1,0:T(1,128)S(1)}, u32[]{:S(2)}, u32[]{:S(2)}) %all-to-all-start.4) | async-done | bytes 16416 | tf_op jit(solution)/shard_map/all_to_all | solution.py:20
  118.2 0.5 broadcast.111
  118.7 0.7 reduce
  119.7 1.6 broadcast_in_dim.109
  121.3 4.5 %all-to-all-start.5 = ((bf16[32,2,64,256]{3,2,1,0:T(8,128)(2,1)}), bf16[32,2,64,256]{3,2,1,0:T(8,128)(2,1)S(1)}, u32[]{:S(2)}, u32[]{:S(2)}) async-start(bf16[32,2,64,256]{3,2,1,0:T(8,128)(2,1)} %broadcast_in_dim.109), calls=%async_computation.5 | async-start | bytes 4194304 | tf_op jit(solution)/shard_map/all_to_all | solution.py:20
  125.9 28.3 %all-to-all-done.5 = bf16[32,2,64,256]{3,2,1,0:T(8,128)(2,1)S(1)} async-done(((bf16[32,2,64,256]{3,2,1,0:T(8,128)(2,1)}), bf16[32,2,64,256]{3,2,1,0:T(8,128)(2,1)S(1)}, u32[]{:S(2)}, u32[]{:S(2)}) %all-to-all-start.5) | async-done | bytes 2097184 | tf_op jit(solution)/shard_map/all_to_all | solution.py:20
  154.4 4.8 %fusion.95 = (f32[2,64]{1,0:T(2,128)S(1)}, f32[2,64,512]{2,1,0:T(8,128)S(1)}) fusion(bf16[2,64,8192]{2,1,0:T(8,128)(2,1)S(1)} %bitcast.366, bf16[8192,512]{1,0:T(8,128)(2,1)} %param.27), kind=kOutput, calls=%fused_computation.181 | convolution fusion | flops 1073807232 | bytes 10748416 | tf_op jit(solution)/shard_map/dot_general | solution.py:194
  159.5 9.1 %all-gather.4 = f32[4,6,64]{2,1,0:T(8,128)S(1)} all-gather(f32[1,6,64]{2,1,0:T(8,128)S(1)} %maximum_bitcast_fusion.1), channel_id=2, replica_groups=mesh['seq_0'=4,'seq_1'=4,'seq_2'=2,'head'=4] {'seq_0'}, dimensions={0}, use_global_device_ids=true | all-gather | bytes 7680 | tf_op jit(solution)/shard_map/all_gather | solution.py:74
  168.7 9.1 %all-gather.5 = f32[4,6,64]{2,1,0:T(8,128)S(1)} all-gather(f32[1,6,64]{2,1,0:T(8,128)S(1)} %maximum_bitcast_fusion.2), channel_id=3, replica_groups=mesh['seq_0'=4,'seq_1'=4,'seq_2'=2,'head'=4] {'seq_1'}, dimensions={0}, use_global_device_ids=true | all-gather | bytes 7680 | tf_op jit(solution)/shard_map/all_gather | solution.py:74
  177.9 8.1 %all-gather.6 = f32[2,6,64]{2,1,0:T(8,128)S(1)} all-gather(f32[1,6,64]{2,1,0:T(8,128)S(1)} %maximum_bitcast_fusion.3), channel_id=4, replica_groups=mesh['seq_0'=4,'seq_1'=4,'seq_2'=2,'head'=4] {'seq_2'}, dimensions={0}, use_global_device_ids=true | all-gather | bytes 4608 | tf_op jit(solution)/shard_map/all_gather | solution.py:74
  185.9 0.7 gather_fusion
  186.7 0.6 copy.60
  187.4 9.1 %all-gather.7 = f32[4,6,64]{2,1,0:T(8,128)S(1)} all-gather(f32[1,6,64]{2,1,0:T(8,128)S(1)} %maximum_bitcast_fusion.4), channel_id=5, replica_groups=mesh['seq_0'=4,'seq_1'=4,'seq_2'=2,'head'=4] {'head'}, dimensions={0}, use_global_device_ids=true | all-gather | bytes 7680 | tf_op jit(solution)/shard_map/all_gather | solution.py:74
  196.5 0.6 fusion.44
  (73 shorter events, 2.8 us)
Async XLA Ops:
  0.6 91.6 %copy-start = (bf16[2048,256]{1,0:T(8,128)(2,1)S(1)}, bf16[2048,256]{1,0:T(8,128)(2,1)}, u32[]{:S(2)}) copy-start(bf16[2048,256]{1,0:T(8,128)(2,1)} %param.25) | copy-start | bytes 3145732
  6.7 3.2 %copy-start.1 = (bf16[2,2,64,128]{3,2,1,0:T(8,128)(2,1)S(1)}, bf16[2,2,64,128]{3,2,1,0:T(8,128)(2,1)}, u32[]{:S(2)}) copy-start(bf16[2,2,64,128]{3,2,1,0:T(8,128)(2,1)} %get-tuple-element.371) | copy-start | bytes 196612 | tf_op jit(solution)/shard_map/while
  6.7 3.5 %copy-start.5 = (bf16[2,2,1024,128]{3,2,1,0:T(8,128)(2,1)S(1)}, bf16[2,2,1024,128]{3,2,1,0:T(8,128)(2,1)}, u32[]{:S(2)}) copy-start(bf16[2,2,1024,128]{3,2,1,0:T(8,128)(2,1)} %get-tuple-element.370) | copy-start | bytes 3145732 | tf_op jit(solution)/shard_map/while
  15.5 3.2 %copy-start.1 = (bf16[2,2,64,128]{3,2,1,0:T(8,128)(2,1)S(1)}, bf16[2,2,64,128]{3,2,1,0:T(8,128)(2,1)}, u32[]{:S(2)}) copy-start(bf16[2,2,64,128]{3,2,1,0:T(8,128)(2,1)} %get-tuple-element.371) | copy-start | bytes 196612 | tf_op jit(solution)/shard_map/while
  15.6 3.5 %copy-start.5 = (bf16[2,2,1024,128]{3,2,1,0:T(8,128)(2,1)S(1)}, bf16[2,2,1024,128]{3,2,1,0:T(8,128)(2,1)}, u32[]{:S(2)}) copy-start(bf16[2,2,1024,128]{3,2,1,0:T(8,128)(2,1)} %get-tuple-element.370) | copy-start | bytes 3145732 | tf_op jit(solution)/shard_map/while
  74.6 31.2 %copy-start.2 = (bf16[2,64,256]{2,1,0:T(8,128)(2,1)S(1)}, bf16[2,64,256]{2,1,0:T(8,128)(2,1)}, u32[]{:S(2)}) copy-start(bf16[2,64,256]{2,1,0:T(8,128)(2,1)} %param.24) | copy-start | bytes 196612
  74.6 36.7 %copy-start.6 = (bf16[256]{0:T(256)(128)(2,1)S(1)}, bf16[256]{0:T(256)(128)(2,1)}, u32[]{:S(2)}) copy-start(bf16[256]{0:T(256)(128)(2,1)} %param.26) | copy-start | bytes 1540
  92.6 33.2 %copy-start.4 = (s32[2,6]{1,0:T(2,128)S(1)}, s32[2,6]{1,0:T(2,128)}, u32[]{:S(2)}) copy-start(s32[2,6]{1,0:T(2,128)} %param.21) | copy-start | bytes 148
  106.6 11.6 %all-to-all-start.4 = ((f32[32,1,128]{2,1,0:T(1,128)}), f32[32,1,128]{2,1,0:T(1,128)S(1)}, u32[]{:S(2)}, u32[]{:S(2)}) async-start(f32[32,1,128]{2,1,0:T(1,128)} %reshape.209), calls=%async_computation.4 | async-start | bytes 32768 | tf_op jit(solution)/shard_map/all_to_all | solution.py:20
  121.3 32.9 %all-to-all-start.5 = ((bf16[32,2,64,256]{3,2,1,0:T(8,128)(2,1)}), bf16[32,2,64,256]{3,2,1,0:T(8,128)(2,1)S(1)}, u32[]{:S(2)}, u32[]{:S(2)}) async-start(bf16[32,2,64,256]{3,2,1,0:T(8,128)(2,1)} %broadcast_in_dim.109), calls=%async_computation.5 | async-start | bytes 4194304 | tf_op jit(solution)/shard_map/all_to_all | solution.py:20
  154.4 4.9 %copy-start.3 = (s32[2,64]{1,0:T(2,128)S(1)}, s32[2,64]{1,0:T(2,128)}, u32[]{:S(2)}) copy-start(s32[2,64]{1,0:T(2,128)} %param.23) | copy-start | bytes 1540
where the time goes:
time: 200 us; the launch traced here: 197 us
  blocking collectives  114 us (57%)
  waiting for transfers between devices  35.3 us (18%)
  matrix products  15.6 us (8%)
  local copies, waits for them, and re-layouts  13.6 us (7%)
  starting transfers between devices  9.12 us (5%)
  other arithmetic  8.36 us (4%)
    all_to_all x3, blocking collectives, from_everyone(): lax.all_to_all(jnp.broadcast_to(x[None], (size, *x.shape)), axis, 0, 0, t...  46.8 us
    all_gather x4, blocking collectives, gathered_once(): both, at, found = (lax.all_gather(jnp.concatenate(lines), axis), 0, {})  35.5 us
    all_to_all x2, waiting for transfers between devices, from_everyone(): lax.all_to_all(jnp.broadcast_to(x[None], (size, *x.shape)), axis, 0, 0, t...  35.3 us
    all_to_all x1, blocking collectives, sum_at_owner(): parts = lax.all_to_all(split_up(x, dim, size), axis, 0, 0, tiled=True)  31.6 us
    all_to_all x2, starting transfers between devices, from_everyone(): lax.all_to_all(jnp.broadcast_to(x[None], (size, *x.shape)), axis, 0, 0, t...  9.12 us
    dot_general x1, matrix products, on_device(): jnp.dot(flat_part, vocab_weight, preferred_element_type=jnp.float32)  4.85 us
    dynamic_slice x8, local copies, waits for them, and re-layouts, on_device(): lax.map(per_sequence, (queries, cache_keys, cache_values, new_keys, new_v...  4.63 us
  transfers between devices with their start and end apart: 2, of which 2 were waited for; matrix products, arithmetic and copies ran while one was open for 0% of the time, Pallas kernels for 0%

commit v1 on v0

v1 whole, which is shorter than its diff:
```python
import functools

import jax
import jax.numpy as jnp
from jax import lax
from jax.experimental import pallas as pl
from jax.experimental.pallas import tpu as pltpu
from jax.sharding import Mesh
from jax.sharding import PartitionSpec as P

D = 8192
SEQ = ("seq_0", "seq_1", "seq_2")
CHIPS = ("seq_0", "seq_1")
SEQ_HEAD = ("seq_0", "seq_1", "seq_2", "head")

HIDDEN = -1e30
FLOOR = -1e25
EPSILON = 1e-5
LOG2E = 1.4426950408889634
ROWS = 256

f32 = jnp.float32
bf16 = jnp.bfloat16


def rows_dot(a, b):
    return lax.dot_general(a, b, (((1,), (1,)), ((), ())), preferred_element_type=f32)


def plain_dot(a, b):
    return lax.dot_general(a, b, (((1,), (0,)), ((), ())), preferred_element_type=f32)


def high_low(x):
    high = x.astype(bf16)
    return high, (x - high.astype(f32)).astype(bf16)


def attention_kernel(lengths_ref, parents_ref, q_ref, k_ref, v_ref, nk_ref, nv_ref, out_ref):
    heads, nodes, width = q_ref.shape[1:]
    span = k_ref.shape[2]
    scale = width**-0.5
    step = scale * LOG2E
    seq = lax.axis_index(SEQ)
    live = lengths_ref[pl.program_id(0)] - seq * span
    column = lax.broadcasted_iota(jnp.int32, (nodes, nodes), 1)
    row = lax.broadcasted_iota(jnp.int32, (nodes, nodes), 0)
    linked = jnp.logical_or(parents_ref[0] == column, row == column)
    reached = jnp.where(linked, 1.0, 0.0).astype(bf16)
    for _ in range((nodes - 1).bit_length()):
        reached = jnp.minimum(plain_dot(reached, reached), 1.0).astype(bf16)
    owner = jnp.where(seq == 0, 1.0, 0.0)
    tree_bias = jnp.where(reached.astype(f32) * owner > 0.5, 0.0, HIDDEN)
    keys, tree_keys = k_ref[0, 0], nk_ref[0, 0]
    ones = jnp.ones((span, width), bf16)
    values = jnp.concatenate([v_ref[0, 0], ones], axis=1)
    tree_values = jnp.concatenate([nv_ref[0, 0], ones[:nodes]], axis=1)
    dead = lax.broadcasted_iota(jnp.int32, (1, span), 1) >= live
    bias = jnp.where(dead, HIDDEN, 0.0)
    group = ROWS // nodes
    lane = lax.broadcasted_iota(jnp.int32, (ROWS, width), 1)
    tiled = jnp.concatenate([tree_bias] * group, axis=0)
    for part in range(heads // group):
        at = part * group
        query = q_ref[0, at : at + group].reshape(ROWS, width)
        scores = rows_dot(query, keys) + bias
        tree_scores = rows_dot(query, tree_keys) + tiled
        highest = jnp.maximum(
            jnp.max(scores, axis=1, keepdims=True), jnp.max(tree_scores, axis=1, keepdims=True)
        )
        top = jnp.maximum((highest * scale).astype(bf16).astype(f32), FLOOR)
        shift = top * LOG2E
        weights = jnp.exp2(scores * step - shift).astype(bf16)
        tree_weights = jnp.exp2(tree_scores * step - shift).astype(bf16)
        result = plain_dot(weights, values) + plain_dot(tree_weights, tree_values)
        out_ref[at : at + group, :nodes] = (
            result[:, :width].astype(bf16).reshape(group, nodes, width)
        )
        both = jnp.where(lane == 0, top, result[:, width:])
        turned = jnp.transpose(both)[:8]
        for h in range(group):
            section = turned[:, h * nodes : (h + 1) * nodes]
            high, low = high_low(section[1:2])
            out_ref[at + h, nodes : nodes + 1, :nodes] = section[0:1].astype(bf16)
            out_ref[at + h, nodes + 1 : nodes + 2, :nodes] = high
            out_ref[at + h, nodes + 2 : nodes + 3, :nodes] = low


def local_attention(queries, cache_keys, cache_values, new_keys, new_values, parents, lengths):
    batch, heads, nodes, width = queries.shape
    kv, span = cache_keys.shape[1:3]
    group = heads // kv
    whole = lambda b, g, *_: (b, g, 0, 0)
    return pl.pallas_call(
        attention_kernel,
        grid_spec=pltpu.PrefetchScalarGridSpec(
            num_scalar_prefetch=1,
            grid=(batch, kv),
            in_specs=[
                pl.BlockSpec((1, nodes, 1), lambda b, g, *_: (b, 0, 0)),
                pl.BlockSpec((1, group, nodes, width), whole),
                pl.BlockSpec((1, 1, span, width), whole),
                pl.BlockSpec((1, 1, span, width), whole),
                pl.BlockSpec((1, 1, nodes, width), whole),
                pl.BlockSpec((1, 1, nodes, width), whole),
            ],
            out_specs=pl.BlockSpec((group, nodes + 8, width), lambda b, g, *_: (b * kv + g, 0, 0)),
        ),
        out_shape=jax.ShapeDtypeStruct((batch * heads, nodes + 8, width), bf16),
        name="attend",
    )(lengths, parents[:, :, None], queries, cache_keys, cache_values, new_keys, new_values)


def join_kernel(parts_ref, out_ref):
    count, rows, width = parts_ref.shape
    nodes = rows - 8
    tops = parts_ref[:, nodes, :].astype(f32)
    totals = parts_ref[:, nodes + 1, :].astype(f32) + parts_ref[:, nodes + 2, :].astype(f32)
    used = lax.broadcasted_iota(jnp.int32, (count, width), 1) < nodes
    tops = jnp.where(used, tops, 0.0)
    totals = jnp.where(used, totals, 1.0)
    factors = jnp.exp(tops - jnp.max(tops, axis=0, keepdims=True))
    share = factors / jnp.sum(factors * totals, axis=0, keepdims=True)
    square = jnp.concatenate([share, jnp.zeros((width - count, width), f32)], axis=0)
    turned = jnp.transpose(square)[:nodes]
    total = parts_ref[0, :nodes].astype(f32) * turned[:, 0:1]
    for k in range(1, count):
        total = total + parts_ref[k, :nodes].astype(f32) * turned[:, k : k + 1]
    block = total.astype(bf16)
    for k in range(out_ref.shape[0]):
        out_ref[k] = block


def join_shares(parts, copies):
    rows, width = parts.shape[1:]
    return pl.pallas_call(
        join_kernel,
        out_shape=jax.ShapeDtypeStruct((copies, rows - 8, width), bf16),
        name="join",
    )(parts)


def project_kernel(mine_ref, other_ref, weight_ref, out_ref):
    chips, nodes, width = mine_ref.shape
    first = lax.axis_index("seq_2") == 0
    mine, other = mine_ref[...], other_ref[...]
    even = jnp.where(first, mine, other)
    odd = jnp.where(first, other, mine)
    half = chips // 2
    lines = []
    for b in range(2):
        blocks = []
        for k in range(half):
            blocks += [even[b * half + k], odd[b * half + k]]
        lines.append(jnp.concatenate(blocks, axis=1))
    result = plain_dot(jnp.concatenate(lines, axis=0), weight_ref[...]).astype(bf16)
    for k in range(out_ref.shape[0]):
        out_ref[k] = result


def project(mine, other, weight, copies):
    rows = 2 * mine.shape[1]
    return pl.pallas_call(
        project_kernel,
        out_shape=jax.ShapeDtypeStruct((copies, rows, weight.shape[1]), bf16),
        name="project",
    )(mine, other, weight)


def stream_kernel(parts_ref, residual_ref, gain_ref, out_ref):
    rows, columns = residual_ref.shape
    stream = residual_ref[...].astype(f32)
    for k in range(parts_ref.shape[0]):
        stream = stream + parts_ref[k].astype(f32)
    scaled = (stream * gain_ref[...].astype(f32)).astype(bf16)
    squares = stream * stream
    folded = squares[:, :128]
    for at in range(128, columns, 128):
        folded = folded + squares[:, at : at + 128]
    sums = jnp.sum(jnp.transpose(folded), axis=0, keepdims=True)
    high, low = high_low(sums)
    for k in range(out_ref.shape[0]):
        out_ref[k, :rows] = scaled
        out_ref[k, rows : rows + 1, :128] = high
        out_ref[k, rows + 1 : rows + 2, :128] = low


def make_stream(parts, residual, gain, copies):
    rows, columns = residual.shape
    return pl.pallas_call(
        stream_kernel,
        out_shape=jax.ShapeDtypeStruct((copies, rows + 8, columns), bf16),
        name="stream",
    )(parts, residual, gain)


def logits_kernel(path_ref, mine_ref, other_ref, weight_ref, tokens_ref, picked_ref, stats_ref, acc):
    chips, padded, columns = mine_ref.shape
    rows = padded - 8
    width = weight_ref.shape[1]
    group = weight_ref.shape[0] // (2 * columns)
    first = lax.axis_index("seq_2") == 0
    at = pl.program_id(0)

    def half(which):
        blocks = []
        for k in range(group):
            mine = mine_ref[at * group + k, :rows]
            other = other_ref[at * group + k, :rows]
            blocks += [jnp.where(first, mine, other), jnp.where(first, other, mine)]
        return jnp.concatenate(blocks, axis=1)

    part = plain_dot(half(0), weight_ref[...])

    @pl.when(at == 0)
    def _():
        acc[...] = part

    @pl.when(at > 0)
    def _():
        acc[...] += part

    @pl.when(at == pl.num_programs(0) - 1)
    def _():
        sums = jnp.zeros((1, 128), f32)
        for ref in (mine_ref, other_ref):
            for k in range(chips):
                sums += ref[k, rows : rows + 1, :128].astype(f32)
                sums += ref[k, rows + 1 : rows + 2, :128].astype(f32)
        scale = lax.rsqrt(sums / D + EPSILON)
        square = jnp.broadcast_to(scale, (rows, 128))
        logits = acc[...] * jnp.transpose(square)[:, 0:1]
        acc[...] = logits
        top = jnp.max(logits, axis=1, keepdims=True)
        total = jnp.sum(jnp.exp(logits - top), axis=1, keepdims=True)
        ids = lax.broadcasted_iota(jnp.int32, (rows, width), 1) + lax.axis_index(SEQ_HEAD) * width
        hit = jnp.sum(jnp.where(ids == tokens_ref[...], logits, 0.0), axis=1, keepdims=True)
        lane = lax.broadcasted_iota(jnp.int32, (rows, 128), 1)
        both = jnp.where(lane == 0, top + jnp.log(total), hit)
        pair = jnp.transpose(both)[:2]
        for k in range(stats_ref.shape[0]):
            stats_ref[k] = pair
        for b in range(picked_ref.shape[0]):
            for k in range(picked_ref.shape[1]):
                n = path_ref[b, k] + b * (rows // picked_ref.shape[0])
                picked_ref[b, k : k + 1] = acc[pl.ds(n, 1)]


def make_logits(mine, other, weight, path, tokens, copies):
    chips, padded, columns = mine.shape
    rows = padded - 8
    width = weight.shape[1]
    steps = 8
    depth = weight.shape[0] // steps
    fixed = lambda *_: (0, 0, 0)
    return pl.pallas_call(
        logits_kernel,
        grid_spec=pltpu.PrefetchScalarGridSpec(
            num_scalar_prefetch=1,
            grid=(steps,),
            in_specs=[
                pl.BlockSpec((chips, padded, columns), fixed),
                pl.BlockSpec((chips, padded, columns), fixed),
                pl.BlockSpec((depth, width), lambda k, *_: (k, 0)),
                pl.BlockSpec((rows, 1), lambda *_: (0, 0)),
            ],
            out_specs=[
                pl.BlockSpec((*path.shape, width), fixed),
                pl.BlockSpec((copies, 2, 128), fixed),
            ],
            scratch_shapes=[pltpu.VMEM((rows, width), f32)],
        ),
        out_shape=[
            jax.ShapeDtypeStruct((*path.shape, width), f32),
            jax.ShapeDtypeStruct((copies, 2, 128), f32),
        ],
        name="logits",
    )(path, mine, other, weight, tokens)


def to_each(x, axes):
    return lax.all_to_all(x, axes, 0, 0, tiled=True)


def across(x):
    return lax.ppermute(x, "seq_2", [(0, 1), (1, 0)])


def on_device(
    queries,
    cache_keys,
    cache_values,
    new_keys,
    new_values,
    parents,
    path,
    lengths,
    draft_tokens,
    residual,
    out_weight,
    norm_gain,
    vocab_weight,
):
    batch, nodes = parents.shape
    rows = batch * nodes
    chips = lax.axis_size(CHIPS)
    shares = local_attention(
        queries, cache_keys, cache_values, new_keys, new_values, parents, lengths
    )
    block = join_shares(to_each(shares, SEQ), chips)
    mine = to_each(block, CHIPS)
    partial = project(mine, across(mine), out_weight, lax.axis_size("head"))
    partial = to_each(partial, "head")
    stream = make_stream(partial, residual.reshape(rows, -1), norm_gain[None], chips)
    mine = to_each(stream, CHIPS)
    path_logits, stats = make_logits(
        mine,
        across(mine),
        vocab_weight,
        path,
        draft_tokens.reshape(rows, 1),
        lax.axis_size(SEQ_HEAD),
    )
    stats = to_each(stats, SEQ_HEAD)
    sums, hits = stats[:, 0], stats[:, 1]
    top = jnp.max(sums, axis=0)
    total = top + jnp.log(jnp.sum(jnp.exp(sums - top), axis=0))
    logprob = (jnp.sum(hits, axis=0) - total).reshape(batch, nodes)
    return (path_logits, logprob)


def solution(mesh):
    torus = Mesh(
        mesh.devices.reshape(4, 4, 2, mesh.shape["head"]), ("seq_0", "seq_1", "seq_2", "head")
    )
    in_specs = (
        P(None, "head", None, None),
        P(None, "head", SEQ, None),
        P(None, "head", SEQ, None),
        P(None, "head", None, None),
        P(None, "head", None, None),
        P(),
        P(),
        P(),
        P(),
        P(None, None, SEQ),
        P("head", SEQ),
        P(SEQ),
        P(None, SEQ_HEAD),
    )
    out_specs = (P(None, None, SEQ_HEAD), P())
    return jax.shard_map(
        on_device, mesh=torus, in_specs=in_specs, out_specs=out_specs, check_vma=False
    )
```

time: 200 us -> 119 us (0.59); the launches traced: 197 us -> 118 us
  blocking collectives: 114 us -> 53 us
  Pallas kernels: 0 us -> 28 us
  waiting for transfers between devices: 35.3 us -> 16.7 us
  matrix products: 15.6 us -> 0 us
  other arithmetic: 8.36 us -> 0.22 us
  local copies, waits for them, and re-layouts: 13.6 us -> 7.22 us
  starting transfers between devices: 9.12 us -> 12.3 us
    all_gather x4 -> x0, blocking collectives: 35.5 us -> none  [gathered_once(): both, at, found = (lax.all_gather(jnp.concatenate(lines), axis), 0, {})]
    pallas_call x0 -> x5, Pallas kernels: none -> 28 us  [the longest x1 11.7 us: local_attention(): pl.pallas_call(attention_kernel, grid_spec=pltpu.PrefetchScalarGridSpec(n...]
    all_to_all x4 -> x3, blocking collectives: 78.4 us -> 53 us  [to_each(): return lax.all_to_all(x, axes, 0, 0, tiled=True)]
    all_to_all x2, waiting for transfers between devices: 35.3 us -> 13.9 us  [to_each(): return lax.all_to_all(x, axes, 0, 0, tiled=True)]
    dot_general x14 -> x0, matrix products: 15.6 us -> none  [the longest x1 4.85 us: on_device(): jnp.dot(flat_part, vocab_weight, preferred_element_type=jnp.float32)]
    dynamic_slice x8 -> x0, local copies, waits for them, and re-layouts: 4.63 us -> none  [on_device(): lax.map(per_sequence, (queries, cache_keys, cache_values, new_keys, new_v...]
    ppermute x0 -> x2, starting transfers between devices: none -> 4.42 us  [across(): return lax.ppermute(x, 'seq_2', [(0, 1), (1, 0)])]
    reduce_sum x9 -> x1, other arithmetic: 3.86 us -> 0.04 us  [on_device(): total = top + jnp.log(jnp.sum(jnp.exp(sums - top), axis=0))]
  transfers between devices with their start and end apart: 2 -> 4, of which waited for: 2 -> 4; matrix products, arithmetic and copies ran while one was open for 0% -> 2% of each run, Pallas kernels for 0% -> 0%
where the time goes in v1:
time: 119 us; the launch traced here: 118 us
  blocking collectives  53 us (45%)
  Pallas kernels  28 us (24%)
  waiting for transfers between devices  16.7 us (14%)
  starting transfers between devices  12.3 us (10%)
  local copies, waits for them, and re-layouts  7.22 us (6%)
    all_to_all x3, blocking collectives, to_each(): return lax.all_to_all(x, axes, 0, 0, tiled=True)  53 us
    all_to_all x2, waiting for transfers between devices, to_each(): return lax.all_to_all(x, axes, 0, 0, tiled=True)  13.9 us
    pallas_call x1, Pallas kernels, local_attention(): pl.pallas_call(attention_kernel, grid_spec=pltpu.PrefetchScalarGridSpec(n...  11.7 us
    pallas_call x1, Pallas kernels, make_logits(): pl.pallas_call(logits_kernel, grid_spec=pltpu.PrefetchScalarGridSpec(num_...  9.43 us
    all_to_all x2, starting transfers between devices, to_each(): return lax.all_to_all(x, axes, 0, 0, tiled=True)  7.92 us
    ppermute x2, starting transfers between devices, across(): return lax.ppermute(x, 'seq_2', [(0, 1), (1, 0)])  4.42 us
    unnamed x15, local copies, waits for them, and re-layouts  3.84 us
    ppermute x2, waiting for transfers between devices, across(): return lax.ppermute(x, 'seq_2', [(0, 1), (1, 0)])  2.78 us
  transfers between devices with their start and end apart: 4, of which 4 were waited for; matrix products, arithmetic and copies ran while one was open for 2% of the time, Pallas kernels for 0%

profile of v1, /device:TPU:1, one launch (start us, length us, event | category | flops | bytes accessed | tf_op | source)
XLA Modules:
  0.0 118.1 jit_solution(17881844540693859540)
XLA Ops:
  0.6 1.4 %copy.15.parents_ref = s32[2,64,1]{2,1,0:T(8,128)} copy(s32[2,64,1]{1,0,2:T(2,128)} %bitcast.5) | data formatting | bytes 1024 | tf_op jit(solution)/shard_map/broadcast_in_dim | solution.py:111
  2.0 11.7 %attend.1 = bf16[32,72,128]{2,1,0:T(8,128)(2,1)} custom-call(s32[2]{0:T(128)} %lengths_ref.1, s32[2,64,1]{2,1,0:T(8,128)} %copy.15.parents_ref, bf16[2,16,64,128]{3,2,1,0:T(8,128)(2,1)} %q_ref.1, bf16[2,2,1024,128]{3,2,1,0:T(8,128)(2,1)} %k_ref.1, bf16[2,2,1024,128]{3,2,1,0:T(8,128)(2,1)} %v_ref.1, bf16[2,2,64,128]{3,2,1,0:T(8,128)(2,1)} %nk_ref.1, ...), custom_call_target="tpu_custom_call" | custom-call | tf_op jit(solution)/shard_map/attend/pallas_call | solution.py:94
  13.7 21.9 %all_to_all.25.parts_ref = bf16[32,72,128]{2,1,0:T(8,128)(2,1)} all-to-all(bf16[32,72,128]{2,1,0:T(8,128)(2,1)} %attend.1), channel_id=1, replica_groups=mesh['seq_0'=4,'seq_1'=4,'seq_2'=2,'head'=4] {'seq_0','seq_1','seq_2'}, dimensions={0} | all-to-all | bytes 1179648 | tf_op jit(solution)/shard_map/all_to_all | solution.py:282
  35.7 2.4 %join.1 = bf16[16,64,128]{2,1,0:T(8,128)(2,1)} custom-call(bf16[32,72,128]{2,1,0:T(8,128)(2,1)} %all_to_all.25.parts_ref), custom_call_target="tpu_custom_call" | custom-call | tf_op jit(solution)/shard_map/join/pallas_call | solution.py:136
  38.0 11.4 %all_to_all.26.mine_ref = bf16[16,64,128]{2,1,0:T(8,128)(2,1)S(1)} all-to-all(bf16[16,64,128]{2,1,0:T(8,128)(2,1)} %join.1), channel_id=1, replica_groups=mesh['seq_0'=4,'seq_1'=4,'seq_2'=2,'head'=4] {'seq_0','seq_1'}, dimensions={0} | all-to-all | bytes 524288 | tf_op jit(solution)/shard_map/all_to_all | solution.py:282
  49.4 0.0 copy-start.3
  49.4 0.0 copy-start.6
  49.4 1.5 %collective-permute-start = (bf16[16,64,128]{2,1,0:T(8,128)(2,1)S(1)}, bf16[16,64,128]{2,1,0:T(8,128)(2,1)S(1)}, u32[]{:S(2)}, u32[]{:S(2)}) collective-permute-start(bf16[16,64,128]{2,1,0:T(8,128)(2,1)S(1)} %all_to_all.26.mine_ref), channel_id=1, source_target_pairs={{0,4},{4,0},{1,5},{5,1},{2,6},{6,2},{3,7},{7,3},{8,12},{12,8},{9,1... | collective-permute-start | bytes 786440 | tf_op jit(solution)/shard_map/ppermute | solution.py:286
  51.0 1.2 collective-permute-done.other_ref
  52.1 0.0 copy-done.3
  52.1 0.0 copy-start.4
  52.1 0.7 copy-done.4
  52.8 2.4 %project.1 = bf16[4,128,256]{2,1,0:T(8,128)(2,1)} custom-call(bf16[16,64,128]{2,1,0:T(8,128)(2,1)} %copy-done.3, bf16[16,64,128]{2,1,0:T(8,128)(2,1)} %copy-done.4, bf16[2048,256]{1,0:T(8,128)(2,1)} %weight_ref.2), custom_call_target="tpu_custom_call" | custom-call | tf_op jit(solution)/shard_map/project/pallas_call | solution.py:163
  55.2 4.0 %all-to-all-start.2 = ((bf16[4,128,256]{2,1,0:T(8,128)(2,1)}), bf16[4,128,256]{2,1,0:T(8,128)(2,1)S(1)}, u32[]{:S(2)}, u32[]{:S(2)}) async-start(bf16[4,128,256]{2,1,0:T(8,128)(2,1)} %project.1), calls=%async_computation.2 | async-start | bytes 524288 | tf_op jit(solution)/shard_map/all_to_all | solution.py:282
  59.2 0.0 copy-done.6
  59.2 0.6 broadcast_in_dim.8.gain_ref
  59.8 5.2 %all-to-all-done.2.parts_ref = bf16[4,128,256]{2,1,0:T(8,128)(2,1)S(1)} async-done(((bf16[4,128,256]{2,1,0:T(8,128)(2,1)}), bf16[4,128,256]{2,1,0:T(8,128)(2,1)S(1)}, u32[]{:S(2)}, u32[]{:S(2)}) %all-to-all-start.2) | async-done | bytes 262176 | tf_op jit(solution)/shard_map/all_to_all | solution.py:282
  65.0 0.0 copy-start.2
  65.0 0.7 copy-done.2
  65.8 2.1 %stream.1 = bf16[16,136,256]{2,1,0:T(8,128)(2,1)} custom-call(bf16[4,128,256]{2,1,0:T(8,128)(2,1)} %copy-done.2, bf16[128,256]{1,0:T(8,128)(2,1)} %bitcast.4, bf16[1,256]{1,0:T(2,128)(2,1)} %broadcast_in_dim.8.gain_ref), custom_call_target="tpu_custom_call" | custom-call | tf_op jit(solution)/shard_map/stream/pallas_call | solution.py:190
  67.9 0.0 copy-start.5
  67.9 19.7 %all_to_all.27.mine_ref = bf16[16,136,256]{2,1,0:T(8,128)(2,1)S(1)} all-to-all(bf16[16,136,256]{2,1,0:T(8,128)(2,1)} %stream.1), channel_id=1, replica_groups=mesh['seq_0'=4,'seq_1'=4,'seq_2'=2,'head'=4] {'seq_0','seq_1'}, dimensions={0} | all-to-all | bytes 2228224 | tf_op jit(solution)/shard_map/all_to_all | solution.py:282
  87.6 0.0 copy-start
  87.6 2.9 %collective-permute-start.1 = (bf16[16,136,256]{2,1,0:T(8,128)(2,1)S(1)}, bf16[16,136,256]{2,1,0:T(8,128)(2,1)S(1)}, u32[]{:S(2)}, u32[]{:S(2)}) collective-permute-start(bf16[16,136,256]{2,1,0:T(8,128)(2,1)S(1)} %all_to_all.27.mine_ref), channel_id=1, source_target_pairs={{0,4},{4,0},{1,5},{5,1},{2,6},{6,2},{3,7},{7,3},{8,12},{12,8},{9,1... | collective-permute-start | bytes 3342344 | tf_op jit(solution)/shard_map/ppermute | solution.py:286
  90.5 0.0 copy-done.5
  90.5 0.8 reshape.20.tokens_ref
  91.2 1.6 %collective-permute-done.1.other_ref = bf16[16,136,256]{2,1,0:T(8,128)(2,1)S(1)} collective-permute-done((bf16[16,136,256]{2,1,0:T(8,128)(2,1)S(1)}, bf16[16,136,256]{2,1,0:T(8,128)(2,1)S(1)}, u32[]{:S(2)}, u32[]{:S(2)}) %collective-permute-start.1) | collective-permute-done | bytes 1114144 | tf_op jit(solution)/shard_map/ppermute | solution.py:286
  92.8 0.0 copy-done
  92.8 0.0 copy-start.1
  92.8 1.0 copy-done.1
  93.9 9.4 %logits.1 = (f32[2,6,512]{2,1,0:T(8,128)}, f32[128,2,128]{2,1,0:T(2,128)}) custom-call(s32[2,6]{1,0:T(2,128)} %path_ref.1, bf16[16,136,256]{2,1,0:T(8,128)(2,1)} %copy-done, bf16[16,136,256]{2,1,0:T(8,128)(2,1)} %copy-done.1, bf16[8192,512]{1,0:T(8,128)(2,1)} %weight_ref.3, s32[128,1]{1,0:T(8,128)} %reshape.20.tokens_ref), custom_call_target="tpu_custom_call" | custom-call | tf_op jit(solution)/shard_map/logits/pallas_call | solution.py:256
  103.3 3.9 %all-to-all-start.4 = ((f32[128,2,128]{2,1,0:T(2,128)}), f32[128,2,128]{2,1,0:T(2,128)S(1)}, u32[]{:S(2)}, u32[]{:S(2)}) async-start(f32[128,2,128]{2,1,0:T(2,128)} %get-tuple-element.5), calls=%async_computation.4 | async-start | bytes 262144 | tf_op jit(solution)/shard_map/all_to_all | solution.py:282
  107.2 1.4 %copy.17 = f32[2,6,512]{2,0,1:T(2,128)} copy(f32[2,6,512]{2,1,0:T(8,128)} %get-tuple-element.6) | data formatting | bytes 49152
  108.6 8.7 %all-to-all-done.4 = f32[128,2,128]{2,1,0:T(2,128)S(1)} async-done(((f32[128,2,128]{2,1,0:T(2,128)}), f32[128,2,128]{2,1,0:T(2,128)S(1)}, u32[]{:S(2)}, u32[]{:S(2)}) %all-to-all-start.4) | async-done | bytes 131104 | tf_op jit(solution)/shard_map/all_to_all | solution.py:282
  117.3 0.2 slice_reduce_fusion.1
  117.5 0.6 sub.18
  (2 shorter events, 0.1 us)
Async XLA Ops:
  49.4 2.7 %copy-start.3 = (bf16[16,64,128]{2,1,0:T(8,128)(2,1)}, bf16[16,64,128]{2,1,0:T(8,128)(2,1)S(1)}, u32[]{:S(2)}) copy-start(bf16[16,64,128]{2,1,0:T(8,128)(2,1)S(1)} %all_to_all.26.mine_ref) | copy-start | bytes 786436
  49.4 9.8 %copy-start.6 = (bf16[256]{0:T(256)(128)(2,1)S(1)}, bf16[256]{0:T(256)(128)(2,1)}, u32[]{:S(2)}) copy-start(bf16[256]{0:T(256)(128)(2,1)} %param.24) | copy-start | bytes 1540
  49.4 2.7 %collective-permute-start = (bf16[16,64,128]{2,1,0:T(8,128)(2,1)S(1)}, bf16[16,64,128]{2,1,0:T(8,128)(2,1)S(1)}, u32[]{:S(2)}, u32[]{:S(2)}) collective-permute-start(bf16[16,64,128]{2,1,0:T(8,128)(2,1)S(1)} %all_to_all.26.mine_ref), channel_id=1, source_target_pairs={{0,4},{4,0},{1,5},{5,1},{2,6},{6,2},{3,7},{7,3},{8,12},{12,8},{9,1... | collective-permute-start | bytes 786440 | tf_op jit(solution)/shard_map/ppermute | solution.py:286
  52.1 0.7 copy-start.4
  55.2 9.8 %all-to-all-start.2 = ((bf16[4,128,256]{2,1,0:T(8,128)(2,1)}), bf16[4,128,256]{2,1,0:T(8,128)(2,1)S(1)}, u32[]{:S(2)}, u32[]{:S(2)}) async-start(bf16[4,128,256]{2,1,0:T(8,128)(2,1)} %project.1), calls=%async_computation.2 | async-start | bytes 524288 | tf_op jit(solution)/shard_map/all_to_all | solution.py:282
  65.0 0.7 copy-start.2
  67.9 22.6 %copy-start.5 = (s32[2,64]{1,0:T(2,128)S(1)}, s32[2,64]{1,0:T(2,128)}, u32[]{:S(2)}) copy-start(s32[2,64]{1,0:T(2,128)} %param.21) | copy-start | bytes 1540
  87.6 5.3 %copy-start = (bf16[16,136,256]{2,1,0:T(8,128)(2,1)}, bf16[16,136,256]{2,1,0:T(8,128)(2,1)S(1)}, u32[]{:S(2)}) copy-start(bf16[16,136,256]{2,1,0:T(8,128)(2,1)S(1)} %all_to_all.27.mine_ref) | copy-start | bytes 3342340
  87.6 5.3 %collective-permute-start.1 = (bf16[16,136,256]{2,1,0:T(8,128)(2,1)S(1)}, bf16[16,136,256]{2,1,0:T(8,128)(2,1)S(1)}, u32[]{:S(2)}, u32[]{:S(2)}) collective-permute-start(bf16[16,136,256]{2,1,0:T(8,128)(2,1)S(1)} %all_to_all.27.mine_ref), channel_id=1, source_target_pairs={{0,4},{4,0},{1,5},{5,1},{2,6},{6,2},{3,7},{7,3},{8,12},{12,8},{9,1... | collective-permute-start | bytes 3342344 | tf_op jit(solution)/shard_map/ppermute | solution.py:286
  92.8 1.0 copy-start.1
  103.3 14.0 %all-to-all-start.4 = ((f32[128,2,128]{2,1,0:T(2,128)}), f32[128,2,128]{2,1,0:T(2,128)S(1)}, u32[]{:S(2)}, u32[]{:S(2)}) async-start(f32[128,2,128]{2,1,0:T(2,128)} %get-tuple-element.5), calls=%async_computation.4 | async-start | bytes 262144 | tf_op jit(solution)/shard_map/all_to_all | solution.py:282

commit v2 on v1

--- a/solution.py
+++ b/solution.py
@@ -31,53 +31,48 @@
     return lax.dot_general(a, b, (((1,), (0,)), ((), ())), preferred_element_type=f32)
 
 
+def room(mib):
+    return pltpu.CompilerParams(vmem_limit_bytes=mib << 20)
+
+
 def high_low(x):
     high = x.astype(bf16)
     return high, (x - high.astype(f32)).astype(bf16)
 
 
+def tree_bias(parents):
+    nodes = parents.shape[1]
+    column = lax.broadcasted_iota(jnp.int32, (nodes, nodes), 1)
+    row = lax.broadcasted_iota(jnp.int32, (nodes, nodes), 0)
+    eye = row == column
+    linked = jnp.where(jnp.logical_or(parents == row, eye), 1.0, 0.0).astype(bf16)
+    reached = rows_dot(jnp.where(eye, 1.0, 0.0).astype(bf16), linked).astype(bf16)
+    for _ in range((nodes - 1).bit_length()):
+        reached = jnp.minimum(plain_dot(reached, reached), 1.0).astype(bf16)
+    return jnp.where(reached.astype(f32) > 0.5, 0.0, HIDDEN)
+
+
 def attention_kernel(lengths_ref, parents_ref, q_ref, k_ref, v_ref, nk_ref, nv_ref, out_ref):
     heads, nodes, width = q_ref.shape[1:]
-    span = k_ref.shape[2]
+    kv, span = k_ref.shape[1:3]
     scale = width**-0.5
     step = scale * LOG2E
     seq = lax.axis_index(SEQ)
     live = lengths_ref[pl.program_id(0)] - seq * span
-    column = lax.broadcasted_iota(jnp.int32, (nodes, nodes), 1)
-    row = lax.broadcasted_iota(jnp.int32, (nodes, nodes), 0)
-    linked = jnp.logical_or(parents_ref[0] == column, row == column)
-    reached = jnp.where(linked, 1.0, 0.0).astype(bf16)
-    for _ in range((nodes - 1).bit_length()):
-        reached = jnp.minimum(plain_dot(reached, reached), 1.0).astype(bf16)
-    owner = jnp.where(seq == 0, 1.0, 0.0)
-    tree_bias = jnp.where(reached.astype(f32) * owner > 0.5, 0.0, HIDDEN)
-    keys, tree_keys = k_ref[0, 0], nk_ref[0, 0]
+    owner = seq == lax.axis_size(SEQ) - 1
+    group = ROWS // nodes
+    turns = range(heads // group)
+    of_group = heads // group // kv
     ones = jnp.ones((span, width), bf16)
-    values = jnp.concatenate([v_ref[0, 0], ones], axis=1)
-    tree_values = jnp.concatenate([nv_ref[0, 0], ones[:nodes]], axis=1)
-    dead = lax.broadcasted_iota(jnp.int32, (1, span), 1) >= live
-    bias = jnp.where(dead, HIDDEN, 0.0)
-    group = ROWS // nodes
-    lane = lax.broadcasted_iota(jnp.int32, (ROWS, width), 1)
-    tiled = jnp.concatenate([tree_bias] * group, axis=0)
-    for part in range(heads // group):
+
+    def query(part):
+        return q_ref[0, part * group : (part + 1) * group].reshape(ROWS, width)
+
+    def write(part, out, top, total):
         at = part * group
-        query = q_ref[0, at : at + group].reshape(ROWS, width)
-        scores = rows_dot(query, keys) + bias
-        tree_scores = rows_dot(query, tree_keys) + tiled
-        highest = jnp.maximum(
-            jnp.max(scores, axis=1, keepdims=True), jnp.max(tree_scores, axis=1, keepdims=True)
-        )
-        top = jnp.maximum((highest * scale).astype(bf16).astype(f32), FLOOR)
-        shift = top * LOG2E
-        weights = jnp.exp2(scores * step - shift).astype(bf16)
-        tree_weights = jnp.exp2(tree_scores * step - shift).astype(bf16)
-        result = plain_dot(weights, values) + plain_dot(tree_weights, tree_values)
-        out_ref[at : at + group, :nodes] = (
-            result[:, :width].astype(bf16).reshape(group, nodes, width)
-        )
-        both = jnp.where(lane == 0, top, result[:, width:])
-        turned = jnp.transpose(both)[:8]
+        out_ref[at : at + group, :nodes] = out.astype(bf16).reshape(group, nodes, width)
+        lane = lax.broadcasted_iota(jnp.int32, (ROWS, width), 1)
+        turned = jnp.transpose(jnp.where(lane == 0, top, total))[:8]
         for h in range(group):
             section = turned[:, h * nodes : (h + 1) * nodes]
             high, low = high_low(section[1:2])
@@ -85,30 +80,82 @@
             out_ref[at + h, nodes + 1 : nodes + 2, :nodes] = high
             out_ref[at + h, nodes + 2 : nodes + 3, :nodes] = low
 
+    def sweep(with_cache, with_tree):
+        streams = []
+        if with_cache:
+            dead = lax.broadcasted_iota(jnp.int32, (1, span), 1) >= live
+            values = [jnp.concatenate([v_ref[0, g], ones], axis=1) for g in range(kv)]
+            streams.append((k_ref, jnp.where(dead, HIDDEN, 0.0), values))
+        if with_tree:
+            bias = tree_bias(parents_ref[pl.ds(pl.program_id(0), 1)])
+            values = [jnp.concatenate([nv_ref[0, g], ones[:nodes]], axis=1) for g in range(kv)]
+            streams.append((nk_ref, jnp.concatenate([bias] * group, axis=0), values))
+
+        def products(part):
+            rows = query(part)
+            return [rows_dot(rows, ref[0, part // of_group]) for ref, _, _ in streams]
+
+        ahead = products(0)
+        for part in turns:
+            scores = [s + bias for s, (_, bias, _) in zip(ahead, streams)]
+            if part + 1 < len(turns):
+                ahead = products(part + 1)
+            highest = functools.reduce(
+                jnp.maximum, [jnp.max(s, axis=1, keepdims=True) for s in scores]
+            )
+            top = jnp.maximum((highest * scale).astype(bf16).astype(f32), FLOOR)
+            shift = top * LOG2E
+            result = 0.0
+            for s, (_, _, values) in zip(scores, streams):
+                weights = jnp.exp2(s * step - shift).astype(bf16)
+                result = result + plain_dot(weights, values[part // of_group])
+            write(part, result[:, :width], top, result[:, width:])
+
+    has_cache = live > 0
+    other = jnp.logical_not(owner)
+
+    @pl.when(jnp.logical_and(has_cache, other))
+    def _():
+        sweep(True, False)
+
+    @pl.when(jnp.logical_and(has_cache, owner))
+    def _():
+        sweep(True, True)
+
+    @pl.when(jnp.logical_and(jnp.logical_not(has_cache), owner))
+    def _():
+        sweep(False, True)
+
+    @pl.when(jnp.logical_and(jnp.logical_not(has_cache), other))
+    def _():
+        for part in turns:
+            nothing = jnp.zeros((ROWS, width), f32)
+            write(part, nothing, jnp.full((ROWS, 1), FLOOR), nothing)
+
 
 def local_attention(queries, cache_keys, cache_values, new_keys, new_values, parents, lengths):
     batch, heads, nodes, width = queries.shape
     kv, span = cache_keys.shape[1:3]
-    group = heads // kv
-    whole = lambda b, g, *_: (b, g, 0, 0)
+    whole = lambda b, *_: (b, 0, 0, 0)
     return pl.pallas_call(
         attention_kernel,
         grid_spec=pltpu.PrefetchScalarGridSpec(
             num_scalar_prefetch=1,
-            grid=(batch, kv),
+            grid=(batch,),
             in_specs=[
-                pl.BlockSpec((1, nodes, 1), lambda b, g, *_: (b, 0, 0)),
-                pl.BlockSpec((1, group, nodes, width), whole),
-                pl.BlockSpec((1, 1, span, width), whole),
-                pl.BlockSpec((1, 1, span, width), whole),
-                pl.BlockSpec((1, 1, nodes, width), whole),
-                pl.BlockSpec((1, 1, nodes, width), whole),
+                pl.BlockSpec(parents.shape, lambda b, *_: (0, 0)),
+                pl.BlockSpec((1, heads, nodes, width), whole),
+                pl.BlockSpec((1, kv, span, width), whole),
+                pl.BlockSpec((1, kv, span, width), whole),
+                pl.BlockSpec((1, kv, nodes, width), whole),
+                pl.BlockSpec((1, kv, nodes, width), whole),
             ],
-            out_specs=pl.BlockSpec((group, nodes + 8, width), lambda b, g, *_: (b * kv + g, 0, 0)),
+            out_specs=pl.BlockSpec((heads, nodes + 8, width), lambda b, *_: (b, 0, 0)),
         ),
         out_shape=jax.ShapeDtypeStruct((batch * heads, nodes + 8, width), bf16),
+        compiler_params=room(24),
         name="attend",
-    )(lengths, parents[:, :, None], queries, cache_keys, cache_values, new_keys, new_values)
+    )(lengths, parents, queries, cache_keys, cache_values, new_keys, new_values)
 
 
 def join_kernel(parts_ref, out_ref):
@@ -136,6 +183,7 @@
     return pl.pallas_call(
         join_kernel,
         out_shape=jax.ShapeDtypeStruct((copies, rows - 8, width), bf16),
+        compiler_params=room(8),
         name="join",
     )(parts)
 
@@ -163,6 +211,7 @@
     return pl.pallas_call(
         project_kernel,
         out_shape=jax.ShapeDtypeStruct((copies, rows, weight.shape[1]), bf16),
+        compiler_params=room(8),
         name="project",
     )(mine, other, weight)
 
@@ -172,7 +221,7 @@
     stream = residual_ref[...].astype(f32)
     for k in range(parts_ref.shape[0]):
         stream = stream + parts_ref[k].astype(f32)
-    scaled = (stream * gain_ref[...].astype(f32)).astype(bf16)
+    scaled = (stream * gain_ref[...].astype(f32)[None]).astype(bf16)
     squares = stream * stream
     folded = squares[:, :128]
     for at in range(128, columns, 128):
@@ -190,6 +239,7 @@
     return pl.pallas_call(
         stream_kernel,
         out_shape=jax.ShapeDtypeStruct((copies, rows + 8, columns), bf16),
+        compiler_params=room(8),
         name="stream",
     )(parts, residual, gain)
 
@@ -234,16 +284,19 @@
         top = jnp.max(logits, axis=1, keepdims=True)
         total = jnp.sum(jnp.exp(logits - top), axis=1, keepdims=True)
         ids = lax.broadcasted_iota(jnp.int32, (rows, width), 1) + lax.axis_index(SEQ_HEAD) * width
-        hit = jnp.sum(jnp.where(ids == tokens_ref[...], logits, 0.0), axis=1, keepdims=True)
+        lines = [tokens_ref[b : b + 1].astype(f32) for b in range(tokens_ref.shape[0])]
+        line = jnp.broadcast_to(jnp.concatenate(lines, axis=1), (128, rows))
+        tokens = jnp.transpose(line)[:, 0:1].astype(jnp.int32)
+        hit = jnp.sum(jnp.where(ids == tokens, logits, 0.0), axis=1, keepdims=True)
         lane = lax.broadcasted_iota(jnp.int32, (rows, 128), 1)
         both = jnp.where(lane == 0, top + jnp.log(total), hit)
         pair = jnp.transpose(both)[:2]
         for k in range(stats_ref.shape[0]):
             stats_ref[k] = pair
-        for b in range(picked_ref.shape[0]):
-            for k in range(picked_ref.shape[1]):
-                n = path_ref[b, k] + b * (rows // picked_ref.shape[0])
-                picked_ref[b, k : k + 1] = acc[pl.ds(n, 1)]
+        for b in range(path_ref.shape[0]):
+            for k in range(path_ref.shape[1]):
+                n = path_ref[b, k] + b * (rows // path_ref.shape[0])
+                picked_ref[k, b : b + 1] = acc[pl.ds(n, 1)]
 
 
 def make_logits(mine, other, weight, path, tokens, copies):
@@ -262,20 +315,40 @@
                 pl.BlockSpec((chips, padded, columns), fixed),
                 pl.BlockSpec((chips, padded, columns), fixed),
                 pl.BlockSpec((depth, width), lambda k, *_: (k, 0)),
-                pl.BlockSpec((rows, 1), lambda *_: (0, 0)),
+                pl.BlockSpec(tokens.shape, lambda *_: (0, 0)),
             ],
             out_specs=[
-                pl.BlockSpec((*path.shape, width), fixed),
+                pl.BlockSpec((*path.shape[::-1], width), fixed),
                 pl.BlockSpec((copies, 2, 128), fixed),
             ],
             scratch_shapes=[pltpu.VMEM((rows, width), f32)],
         ),
         out_shape=[
-            jax.ShapeDtypeStruct((*path.shape, width), f32),
+            jax.ShapeDtypeStruct((*path.shape[::-1], width), f32),
             jax.ShapeDtypeStruct((copies, 2, 128), f32),
         ],
+        compiler_params=room(16),
         name="logits",
     )(path, mine, other, weight, tokens)
+
+
+def final_kernel(stats_ref, out_ref):
+    sums, hits = stats_ref[:, 0], stats_ref[:, 1]
+    top = jnp.max(sums, axis=0, keepdims=True)
+    total = top + jnp.log(jnp.sum(jnp.exp(sums - top), axis=0, keepdims=True))
+    result = jnp.sum(hits, axis=0, keepdims=True) - total
+    nodes = out_ref.shape[1]
+    for b in range(out_ref.shape[0]):
+        out_ref[b : b + 1] = result[:, b * nodes : (b + 1) * nodes]
+
+
+def log_probabilities(stats, batch):
+    return pl.pallas_call(
+        final_kernel,
+        out_shape=jax.ShapeDtypeStruct((batch, stats.shape[2] // batch), f32),
+        compiler_params=room(4),
+        name="final",
+    )(stats)
 
 
 def to_each(x, axes):
@@ -311,22 +384,19 @@
     mine = to_each(block, CHIPS)
     partial = project(mine, across(mine), out_weight, lax.axis_size("head"))
     partial = to_each(partial, "head")
-    stream = make_stream(partial, residual.reshape(rows, -1), norm_gain[None], chips)
+    stream = make_stream(partial, residual.reshape(rows, -1), norm_gain, chips)
     mine = to_each(stream, CHIPS)
     path_logits, stats = make_logits(
         mine,
         across(mine),
         vocab_weight,
         path,
-        draft_tokens.reshape(rows, 1),
+        draft_tokens,
         lax.axis_size(SEQ_HEAD),
     )
     stats = to_each(stats, SEQ_HEAD)
-    sums, hits = stats[:, 0], stats[:, 1]
-    top = jnp.max(sums, axis=0)
-    total = top + jnp.log(jnp.sum(jnp.exp(sums - top), axis=0))
-    logprob = (jnp.sum(hits, axis=0) - total).reshape(batch, nodes)
-    return (path_logits, logprob)
+    logprob = log_probabilities(stats, batch)
+    return (jnp.transpose(path_logits, (1, 0, 2)), logprob)
 
 
 def solution(mesh):

time: 119 us -> 103 us (0.87)
  blocking collectives: 53 us -> 75.3 us
  Pallas kernels: 28 us -> 11 us
  waiting for transfers between devices: 16.7 us -> 3.54 us
  starting transfers between devices: 12.3 us -> 4.96 us
    all_to_all x3 -> x5, blocking collectives: 53 us -> 75.3 us  [to_each(): return lax.all_to_all(x, axes, 0, 0, tiled=True)]
    all_to_all x2 -> x0, waiting for transfers between devices: 13.9 us -> none  [to_each(): return lax.all_to_all(x, axes, 0, 0, tiled=True)]
    all_to_all x2 -> x0, starting transfers between devices: 7.92 us -> none  [to_each(): return lax.all_to_all(x, axes, 0, 0, tiled=True)]
    pallas_call x1, Pallas kernels: 11.7 us -> 4.59 us  [local_attention(): pl.pallas_call(attention_kernel, grid_spec=pltpu.PrefetchScalarGridSpec(n...]
    pallas_call x1, Pallas kernels: 9.43 us -> 4.64 us  [make_logits(): pl.pallas_call(logits_kernel, grid_spec=pltpu.PrefetchScalarGridSpec(num_...]
    unnamed x15 -> x26, local copies, waits for them, and re-layouts: 3.84 us -> 6.52 us
    pallas_call x1, Pallas kernels: 2.4 us -> 0.32 us  [project(): pl.pallas_call(project_kernel, out_shape=jax.ShapeDtypeStruct((copies, ro...]
    pallas_call x1, Pallas kernels: 2.14 us -> 0.15 us  [make_stream(): pl.pallas_call(stream_kernel, out_shape=jax.ShapeDtypeStruct((copies, row...]
  transfers between devices with their start and end apart: 4 -> 2, of which waited for: 4 -> 2; matrix products, arithmetic and copies ran while one was open for 2% -> 0% of each run, Pallas kernels for 0% -> 0%
where the time goes in v2:
time: 103 us; the launch traced here: 102 us
  blocking collectives  75.3 us (73%)
  Pallas kernels  11 us (11%)
  local copies, waits for them, and re-layouts  6.52 us (6%)
  starting transfers between devices  4.96 us (5%)
  waiting for transfers between devices  3.54 us (3%)
    all_to_all x5, blocking collectives, to_each(): return lax.all_to_all(x, axes, 0, 0, tiled=True)  75.3 us
    unnamed x26, local copies, waits for them, and re-layouts  6.52 us
    ppermute x2, starting transfers between devices, across(): return lax.ppermute(x, 'seq_2', [(0, 1), (1, 0)])  4.96 us
    pallas_call x1, Pallas kernels, make_logits(): pl.pallas_call(logits_kernel, grid_spec=pltpu.PrefetchScalarGridSpec(num_...  4.64 us
    pallas_call x1, Pallas kernels, local_attention(): pl.pallas_call(attention_kernel, grid_spec=pltpu.PrefetchScalarGridSpec(n...  4.59 us
    ppermute x2, waiting for transfers between devices, across(): return lax.ppermute(x, 'seq_2', [(0, 1), (1, 0)])  3.54 us
  transfers between devices with their start and end apart: 2, of which 2 were waited for; matrix products, arithmetic and copies ran while one was open for 0% of the time, Pallas kernels for 0%

profile of v2, /device:TPU:1, one launch (start us, length us, event | category | flops | bytes accessed | tf_op | source)
XLA Modules:
  0.0 102.0 jit_solution(9906763080357565745)
XLA Ops:
  0.6 0.0 copy-start.2
  0.6 1.2 %copy-done.2 = bf16[2,2,1024,128]{3,2,1,0:T(8,128)(2,1)S(1)} copy-done((bf16[2,2,1024,128]{3,2,1,0:T(8,128)(2,1)S(1)}, bf16[2,2,1024,128]{3,2,1,0:T(8,128)(2,1)}, u32[]{:S(2)}) %copy-start.2) | copy-done | bytes 1048600
  1.9 0.0 copy-start.3
  1.9 1.2 %copy-done.3 = bf16[2,2,1024,128]{3,2,1,0:T(8,128)(2,1)S(1)} copy-done((bf16[2,2,1024,128]{3,2,1,0:T(8,128)(2,1)S(1)}, bf16[2,2,1024,128]{3,2,1,0:T(8,128)(2,1)}, u32[]{:S(2)}) %copy-start.3) | copy-done | bytes 1048600
  3.1 0.0 copy-start.4
  3.1 1.0 %copy-done.4 = bf16[2,16,64,128]{3,2,1,0:T(8,128)(2,1)S(1)} copy-done((bf16[2,16,64,128]{3,2,1,0:T(8,128)(2,1)S(1)}, bf16[2,16,64,128]{3,2,1,0:T(8,128)(2,1)}, u32[]{:S(2)}) %copy-start.4) | copy-done | bytes 524312
  4.1 0.0 copy-start.6
  4.1 0.8 copy-done.6
  5.0 0.0 copy-start.7
  5.0 0.8 copy-done.7
  5.8 0.0 copy-start.8
  5.8 0.7 copy-done.8
  6.5 0.0 copy-start.12
  6.5 0.7 copy-done.12
  7.1 0.0 copy-start.1
  7.1 0.0 copy-start.5
  7.1 0.0 copy-start.11
  7.1 4.6 %attend.1 = bf16[32,72,128]{2,1,0:T(8,128)(2,1)S(1)} custom-call(s32[2]{0:T(128)S(1)} %copy-done.12, s32[2,64]{1,0:T(2,128)S(1)} %copy-done.8, bf16[2,16,64,128]{3,2,1,0:T(8,128)(2,1)S(1)} %copy-done.4, bf16[2,2,1024,128]{3,2,1,0:T(8,128)(2,1)S(1)} %copy-done.2, bf16[2,2,1024,128]{3,2,1,0:T(8,128)(2,1)S(1)} %copy-done.3, ...), custom_call_target="tpu_custom_call" | custom-call | tf_op jit(solution)/shard_map/attend/pallas_call | solution.py:140
  11.7 0.0 copy-start
  11.8 22.4 %all_to_all.25.parts_ref = bf16[32,72,128]{2,1,0:T(8,128)(2,1)S(1)} all-to-all(bf16[32,72,128]{2,1,0:T(8,128)(2,1)S(1)} %attend.1), channel_id=1, replica_groups=mesh['seq_0'=4,'seq_1'=4,'seq_2'=2,'head'=4] {'seq_0','seq_1','seq_2'}, dimensions={0} | all-to-all | bytes 1179648 | tf_op jit(solution)/shard_map/all_to_all | solution.py:355
  34.1 0.6 join.1
  34.7 10.5 %all_to_all.26.mine_ref = bf16[16,64,128]{2,1,0:T(8,128)(2,1)S(1)} all-to-all(bf16[16,64,128]{2,1,0:T(8,128)(2,1)S(1)} %join.1), channel_id=1, replica_groups=mesh['seq_0'=4,'seq_1'=4,'seq_2'=2,'head'=4] {'seq_0','seq_1'}, dimensions={0} | all-to-all | bytes 524288 | tf_op jit(solution)/shard_map/all_to_all | solution.py:355
  45.2 1.8 %collective-permute-start = (bf16[16,64,128]{2,1,0:T(8,128)(2,1)S(1)}, bf16[16,64,128]{2,1,0:T(8,128)(2,1)S(1)}, u32[]{:S(2)}, u32[]{:S(2)}) collective-permute-start(bf16[16,64,128]{2,1,0:T(8,128)(2,1)S(1)} %all_to_all.26.mine_ref), channel_id=1, source_target_pairs={{0,4},{4,0},{1,5},{5,1},{2,6},{6,2},{3,7},{7,3},{8,12},{12,8},{9,1... | collective-permute-start | bytes 786440 | tf_op jit(solution)/shard_map/ppermute | solution.py:359
  47.0 1.2 %collective-permute-done.other_ref = bf16[16,64,128]{2,1,0:T(8,128)(2,1)S(1)} collective-permute-done((bf16[16,64,128]{2,1,0:T(8,128)(2,1)S(1)}, bf16[16,64,128]{2,1,0:T(8,128)(2,1)S(1)}, u32[]{:S(2)}, u32[]{:S(2)}) %collective-permute-start) | collective-permute-done | bytes 262176 | tf_op jit(solution)/shard_map/ppermute | solution.py:359
  48.2 0.0 copy-done.1
  48.2 0.3 project.1
  48.5 9.6 %all_to_all.27.parts_ref = bf16[4,128,256]{2,1,0:T(8,128)(2,1)S(1)} all-to-all(bf16[4,128,256]{2,1,0:T(8,128)(2,1)S(1)} %project.1), channel_id=1, replica_groups=mesh['seq_0'=4,'seq_1'=4,'seq_2'=2,'head'=4] {'head'}, dimensions={0} | all-to-all | bytes 524288 | tf_op jit(solution)/shard_map/all_to_all | solution.py:355
  58.2 0.0 copy-done.5
  58.2 0.0 copy-done.11
  58.2 0.2 stream.1
  58.3 0.0 copy-start.9
  58.3 0.0 copy-start.10
  58.3 18.8 %all_to_all.28.mine_ref = bf16[16,136,256]{2,1,0:T(8,128)(2,1)S(1)} all-to-all(bf16[16,136,256]{2,1,0:T(8,128)(2,1)S(1)} %stream.1), channel_id=1, replica_groups=mesh['seq_0'=4,'seq_1'=4,'seq_2'=2,'head'=4] {'seq_0','seq_1'}, dimensions={0} | all-to-all | bytes 2228224 | tf_op jit(solution)/shard_map/all_to_all | solution.py:355
  77.2 3.1 %collective-permute-start.1 = (bf16[16,136,256]{2,1,0:T(8,128)(2,1)S(1)}, bf16[16,136,256]{2,1,0:T(8,128)(2,1)S(1)}, u32[]{:S(2)}, u32[]{:S(2)}) collective-permute-start(bf16[16,136,256]{2,1,0:T(8,128)(2,1)S(1)} %all_to_all.28.mine_ref), channel_id=1, source_target_pairs={{0,4},{4,0},{1,5},{5,1},{2,6},{6,2},{3,7},{7,3},{8,12},{12,8},{9,1... | collective-permute-start | bytes 3342344 | tf_op jit(solution)/shard_map/ppermute | solution.py:359
  80.3 2.4 %collective-permute-done.1.other_ref = bf16[16,136,256]{2,1,0:T(8,128)(2,1)S(1)} collective-permute-done((bf16[16,136,256]{2,1,0:T(8,128)(2,1)S(1)}, bf16[16,136,256]{2,1,0:T(8,128)(2,1)S(1)}, u32[]{:S(2)}, u32[]{:S(2)}) %collective-permute-start.1) | collective-permute-done | bytes 1114144 | tf_op jit(solution)/shard_map/ppermute | solution.py:359
  82.7 0.0 copy-done
  82.7 0.0 copy-done.9
  82.7 0.0 copy-done.10
  82.7 4.6 %logits.1 = (f32[6,2,512]{2,1,0:T(2,128)}, f32[128,2,128]{2,1,0:T(2,128)S(1)}) custom-call(s32[2,6]{1,0:T(2,128)S(1)} %copy-done.9, bf16[16,136,256]{2,1,0:T(8,128)(2,1)S(1)} %all_to_all.28.mine_ref, bf16[16,136,256]{2,1,0:T(8,128)(2,1)S(1)} %collective-permute-done.1.other_ref, bf16[8192,512]{1,0:T(8,128)(2,1)S(1)} %copy-done, s32[2,64]{1,0:T(2,128)S(1)} %copy-done.10), custom_call_target="tpu_custom_call" | custom-call | tf_op jit(solution)/shard_map/logits/pallas_call | solution.py:309
  87.3 14.0 %all_to_all.29.stats_ref = f32[128,2,128]{2,1,0:T(2,128)S(1)} all-to-all(f32[128,2,128]{2,1,0:T(2,128)S(1)} %get-tuple-element.5), channel_id=1, replica_groups=mesh['seq_0'=4,'seq_1'=4,'seq_2'=2,'head'=4] {'seq_0','seq_1','seq_2','h..., dimensions={0} | all-to-all | bytes 262144 | tf_op jit(solution)/shard_map/all_to_all | solution.py:355
  101.3 0.8 final.1
Async XLA Ops:
  0.6 1.2 %copy-start.2 = (bf16[2,2,1024,128]{3,2,1,0:T(8,128)(2,1)S(1)}, bf16[2,2,1024,128]{3,2,1,0:T(8,128)(2,1)}, u32[]{:S(2)}) copy-start(bf16[2,2,1024,128]{3,2,1,0:T(8,128)(2,1)} %k_ref.1) | copy-start | bytes 3145732
  1.9 1.2 %copy-start.3 = (bf16[2,2,1024,128]{3,2,1,0:T(8,128)(2,1)S(1)}, bf16[2,2,1024,128]{3,2,1,0:T(8,128)(2,1)}, u32[]{:S(2)}) copy-start(bf16[2,2,1024,128]{3,2,1,0:T(8,128)(2,1)} %v_ref.1) | copy-start | bytes 3145732
  3.1 1.0 %copy-start.4 = (bf16[2,16,64,128]{3,2,1,0:T(8,128)(2,1)S(1)}, bf16[2,16,64,128]{3,2,1,0:T(8,128)(2,1)}, u32[]{:S(2)}) copy-start(bf16[2,16,64,128]{3,2,1,0:T(8,128)(2,1)} %q_ref.1) | copy-start | bytes 1572868
  4.1 0.8 copy-start.6
  5.0 0.8 copy-start.7
  5.8 0.7 copy-start.8
  6.5 0.7 copy-start.12
  7.1 41.1 %copy-start.1 = (bf16[2048,256]{1,0:T(8,128)(2,1)S(1)}, bf16[2048,256]{1,0:T(8,128)(2,1)}, u32[]{:S(2)}) copy-start(bf16[2048,256]{1,0:T(8,128)(2,1)} %weight_ref.2) | copy-start | bytes 3145732
  7.1 51.0 %copy-start.5 = (bf16[2,64,256]{2,1,0:T(8,128)(2,1)S(1)}, bf16[2,64,256]{2,1,0:T(8,128)(2,1)}, u32[]{:S(2)}) copy-start(bf16[2,64,256]{2,1,0:T(8,128)(2,1)} %param.22) | copy-start | bytes 196612
  7.1 51.0 %copy-start.11 = (bf16[256]{0:T(256)(128)(2,1)S(1)}, bf16[256]{0:T(256)(128)(2,1)}, u32[]{:S(2)}) copy-start(bf16[256]{0:T(256)(128)(2,1)} %gain_ref.1) | copy-start | bytes 1540
  11.7 70.9 %copy-start = (bf16[8192,512]{1,0:T(8,128)(2,1)S(1)}, bf16[8192,512]{1,0:T(8,128)(2,1)}, u32[]{:S(2)}) copy-start(bf16[8192,512]{1,0:T(8,128)(2,1)} %weight_ref.3) | copy-start | bytes 25165828
  45.2 3.0 %collective-permute-start = (bf16[16,64,128]{2,1,0:T(8,128)(2,1)S(1)}, bf16[16,64,128]{2,1,0:T(8,128)(2,1)S(1)}, u32[]{:S(2)}, u32[]{:S(2)}) collective-permute-start(bf16[16,64,128]{2,1,0:T(8,128)(2,1)S(1)} %all_to_all.26.mine_ref), channel_id=1, source_target_pairs={{0,4},{4,0},{1,5},{5,1},{2,6},{6,2},{3,7},{7,3},{8,12},{12,8},{9,1... | collective-permute-start | bytes 786440 | tf_op jit(solution)/shard_map/ppermute | solution.py:359
  58.3 24.4 %copy-start.9 = (s32[2,6]{1,0:T(2,128)S(1)}, s32[2,6]{1,0:T(2,128)}, u32[]{:S(2)}) copy-start(s32[2,6]{1,0:T(2,128)} %path_ref.1) | copy-start | bytes 148
  58.3 24.4 %copy-start.10 = (s32[2,64]{1,0:T(2,128)S(1)}, s32[2,64]{1,0:T(2,128)}, u32[]{:S(2)}) copy-start(s32[2,64]{1,0:T(2,128)} %tokens_ref.1) | copy-start | bytes 1540
  77.2 5.5 %collective-permute-start.1 = (bf16[16,136,256]{2,1,0:T(8,128)(2,1)S(1)}, bf16[16,136,256]{2,1,0:T(8,128)(2,1)S(1)}, u32[]{:S(2)}, u32[]{:S(2)}) collective-permute-start(bf16[16,136,256]{2,1,0:T(8,128)(2,1)S(1)} %all_to_all.28.mine_ref), channel_id=1, source_target_pairs={{0,4},{4,0},{1,5},{5,1},{2,6},{6,2},{3,7},{7,3},{8,12},{12,8},{9,1... | collective-permute-start | bytes 3342344 | tf_op jit(solution)/shard_map/ppermute | solution.py:359

commit v3 on v2

v3 whole, which is shorter than its diff:
```python
import functools

import jax
import jax.numpy as jnp
from jax import lax
from jax.experimental import pallas as pl
from jax.experimental.pallas import tpu as pltpu
from jax.sharding import Mesh
from jax.sharding import PartitionSpec as P

D = 8192
SEQ = ("seq_0", "seq_1", "seq_2")
CHIPS = ("seq_0", "seq_1")
SEQ_HEAD = ("seq_0", "seq_1", "seq_2", "head")

HIDDEN = -1e30
FLOOR = -1e25
EPSILON = 1e-5
LOG2E = 1.4426950408889634
ROWS = 256

f32 = jnp.float32
bf16 = jnp.bfloat16


def rows_dot(a, b):
    return lax.dot_general(a, b, (((1,), (1,)), ((), ())), preferred_element_type=f32)


def plain_dot(a, b):
    return lax.dot_general(a, b, (((1,), (0,)), ((), ())), preferred_element_type=f32)


def room(mib):
    return pltpu.CompilerParams(vmem_limit_bytes=mib << 20)


def rows_dot(a, b):
    return lax.dot_general(a, b, (((1,), (1,)), ((), ())), preferred_element_type=f32)


def plain_dot(a, b):
    return lax.dot_general(a, b, (((1,), (0,)), ((), ())), preferred_element_type=f32)


def room(mib):
    return pltpu.CompilerParams(vmem_limit_bytes=mib << 20)


def high_low(x):
    high = x.astype(bf16)
    return high, (x - high.astype(f32)).astype(bf16)


def tree_bias(parents):
    nodes = parents.shape[1]
    column = lax.broadcasted_iota(jnp.int32, (nodes, nodes), 1)
    row = lax.broadcasted_iota(jnp.int32, (nodes, nodes), 0)
    eye = row == column
    linked = jnp.where(jnp.logical_or(parents == row, eye), 1.0, 0.0).astype(bf16)
    reached = rows_dot(jnp.where(eye, 1.0, 0.0).astype(bf16), linked).astype(bf16)
    for _ in range((nodes - 1).bit_length()):
        reached = jnp.minimum(plain_dot(reached, reached), 1.0).astype(bf16)
    return jnp.where(reached.astype(f32) > 0.5, 0.0, HIDDEN)


def attention_kernel(
    lengths_hbm,
    parents_hbm,
    q_hbm,
    k_hbm,
    v_hbm,
    nk_hbm,
    nv_hbm,
    out_ref,
    lengths_ref,
    parents_ref,
    q_ref,
    k_ref,
    v_ref,
    nk_ref,
    nv_ref,
    block_sems,
    tree_sems,
    length_sem,
):
    batch, heads, nodes, width = q_ref.shape
    kv, span = k_ref.shape[1:3]
    scale = width**-0.5
    step = scale * LOG2E
    seq = lax.axis_index(SEQ)
    owner = seq == lax.axis_size(SEQ) - 1
    other = jnp.logical_not(owner)
    group = ROWS // nodes
    turns = range(heads // group)
    of_group = heads // group // kv
    ones = jnp.ones((span, width), bf16)

    lengths_copy = pltpu.make_async_copy(lengths_hbm, lengths_ref, length_sem)
    lengths_copy.start()

    def block_copy(b, g, n):
        own = pl.ds(g * (heads // kv), heads // kv)
        source, target, place = (
            (q_hbm, q_ref, (b, own)),
            (k_hbm, k_ref, (b, g)),
            (v_hbm, v_ref, (b, g)),
        )[n]
        return pltpu.make_async_copy(source.at[place], target.at[place], block_sems.at[b, g, n])

    for b in range(batch):
        for g in range(kv):
            for n in range(3):
                block_copy(b, g, n).start()
    trees = [
        pltpu.make_async_copy(source, target, tree_sems.at[n])
        for n, (source, target) in enumerate(
            ((parents_hbm, parents_ref), (nk_hbm, nk_ref), (nv_hbm, nv_ref))
        )
    ]

    @pl.when(owner)
    def _():
        for copy in trees:
            copy.start()
        for copy in trees:
            copy.wait()

    lengths_copy.wait()

    def write(b, part, out, top, total):
        at = b * heads + part * group
        out_ref[pl.ds(at, group), :nodes] = out.astype(bf16).reshape(group, nodes, width)
        lane = lax.broadcasted_iota(jnp.int32, (ROWS, width), 1)
        turned = jnp.transpose(jnp.where(lane == 0, top, total))[:8]
        for h in range(group):
            section = turned[:, h * nodes : (h + 1) * nodes]
            total = section[1:2]
            high = total.astype(bf16).astype(f32)
            row = lax.broadcasted_iota(jnp.int32, section.shape, 0)
            tail = jnp.where(row == 0, section[0:1], jnp.where(row == 1, high, total - high))
            out_ref[at + h, nodes:, :nodes] = tail.astype(bf16)

    def sweep(b, live, with_cache, with_tree):
        biases = []
        if with_cache:
            dead = lax.broadcasted_iota(jnp.int32, (1, span), 1) >= live
            biases.append(jnp.where(dead, HIDDEN, 0.0))
        if with_tree:
            bias = tree_bias(parents_ref[pl.ds(b, 1)])
            biases.append(jnp.concatenate([bias] * group, axis=0))

        def products(part):
            g = part // of_group
            rows = q_ref[b, part * group : (part + 1) * group].reshape(ROWS, width)
            found = [rows_dot(rows, k_ref[b, g])] if with_cache else []
            return found + ([rows_dot(rows, nk_ref[b, g])] if with_tree else [])

        ahead = products(0)
        for part in turns:
            g = part // of_group
            scores = [s + bias for s, bias in zip(ahead, biases)]
            if part + 1 < len(turns):
                ahead = products(part + 1)
            if part % of_group == 0:
                values = [jnp.concatenate([v_ref[b, g], ones], axis=1)] if with_cache else []
                if with_tree:
                    values.append(jnp.concatenate([nv_ref[b, g], ones[:nodes]], axis=1))
            highest = functools.reduce(
                jnp.maximum, [jnp.max(s, axis=1, keepdims=True) for s in scores]
            )
            top = jnp.maximum((highest * scale).astype(bf16).astype(f32), FLOOR)
            shift = top * LOG2E
            result = 0.0
            for s, value in zip(scores, values):
                weights = jnp.exp2(s * step - shift).astype(bf16)
                result = result + plain_dot(weights, value)
            write(b, part, result[:, :width], top, result[:, width:])

    def nothing(b):
        for part in turns:
            zeros = jnp.zeros((ROWS, width), f32)
            write(b, part, zeros, jnp.full((ROWS, 1), FLOOR), zeros)

    @pl.loop(0, batch)
    def _(b):
        live = lengths_ref[b] - seq * span
        for g in range(kv):
            for n in range(3):
                block_copy(b, g, n).wait()
        filled = live > 0
        empty = jnp.logical_not(filled)
        pl.when(jnp.logical_and(filled, other))(functools.partial(sweep, b, live, True, False))
        pl.when(jnp.logical_and(filled, owner))(functools.partial(sweep, b, live, True, True))
        pl.when(jnp.logical_and(empty, owner))(functools.partial(sweep, b, live, False, True))
        pl.when(jnp.logical_and(empty, other))(functools.partial(nothing, b))


def local_attention(queries, cache_keys, cache_values, new_keys, new_values, parents, lengths):
    batch, heads, nodes, width = queries.shape
    kv = cache_keys.shape[1]
    operands = (lengths, parents, queries, cache_keys, cache_values, new_keys, new_values)
    scratch = [pltpu.SMEM(lengths.shape, lengths.dtype)]
    scratch += [pltpu.VMEM(x.shape, x.dtype) for x in operands[1:]]
    scratch += [
        pltpu.SemaphoreType.DMA((batch, kv, 3)),
        pltpu.SemaphoreType.DMA((3,)),
        pltpu.SemaphoreType.DMA,
    ]
    return pl.pallas_call(
        attention_kernel,
        in_specs=[pl.BlockSpec(memory_space=pltpu.HBM)] * len(operands),
        out_specs=pl.BlockSpec(memory_space=pltpu.VMEM),
        out_shape=jax.ShapeDtypeStruct((batch * heads, nodes + 8, width), bf16),
        scratch_shapes=scratch,
        compiler_params=room(62),
        name="attend",
    )(*operands)


def join_kernel(parts_ref, gain_ref, out_ref):
    count, rows, width = parts_ref.shape
    nodes = rows - 8
    tops = parts_ref[:, nodes, :].astype(f32)
    totals = parts_ref[:, nodes + 1, :].astype(f32) + parts_ref[:, nodes + 2, :].astype(f32)
    used = lax.broadcasted_iota(jnp.int32, (count, width), 1) < nodes
    tops = jnp.where(used, tops, 0.0)
    totals = jnp.where(used, totals, 1.0)
    factors = jnp.exp(tops - jnp.max(tops, axis=0, keepdims=True))
    share = factors / jnp.sum(factors * totals, axis=0, keepdims=True)
    square = jnp.concatenate([share, jnp.zeros((width - count, width), f32)], axis=0)
    turned = jnp.transpose(square)[:nodes]
    total = parts_ref[0, :nodes].astype(f32) * turned[:, 0:1]
    for k in range(1, count):
        total = total + parts_ref[k, :nodes].astype(f32) * turned[:, k : k + 1]
    block = total.astype(bf16)
    gain = gain_ref[...].astype(f32)[None]
    lines = [gain[:, :width], gain[:, width:], jnp.ones((6, width), f32)]
    tail = jnp.concatenate(lines, axis=0).astype(bf16)
    for k in range(out_ref.shape[0]):
        out_ref[k, :nodes] = block
        out_ref[k, nodes:] = tail


def join_shares(parts, gain, copies):
    rows, width = parts.shape[1:]
    return pl.pallas_call(
        join_kernel,
        out_shape=jax.ShapeDtypeStruct((copies, rows, width), bf16),
        compiler_params=room(8),
        name="join",
    )(parts, gain)


def project_kernel(mine_ref, other_ref, weight_ref, out_ref):
    chips, padded, width = mine_ref.shape
    nodes = padded - 8
    first = lax.axis_index("seq_2") == 0
    mine, other = mine_ref[:, :nodes], other_ref[:, :nodes]
    even = jnp.where(first, mine, other)
    odd = jnp.where(first, other, mine)
    half = chips // 2
    lines = []
    for b in range(2):
        blocks = []
        for k in range(half):
            blocks += [even[b * half + k], odd[b * half + k]]
        lines.append(jnp.concatenate(blocks, axis=1))
    result = plain_dot(jnp.concatenate(lines, axis=0), weight_ref[...]).astype(bf16)
    for k in range(out_ref.shape[0]):
        out_ref[k] = result


def project(mine, other, weight, copies):
    rows = 2 * (mine.shape[1] - 8)
    return pl.pallas_call(
        project_kernel,
        out_shape=jax.ShapeDtypeStruct((copies, rows, weight.shape[1]), bf16),
        compiler_params=room(8),
        name="project",
    )(mine, other, weight)


def stream_kernel(parts_ref, residual_ref, gain_ref, out_ref):
    stream = residual_ref[...].astype(f32)
    for k in range(parts_ref.shape[0]):
        stream = stream + parts_ref[k].astype(f32)
    scaled = (stream * gain_ref[...].astype(f32)[None]).astype(bf16)
    for k in range(out_ref.shape[0]):
        out_ref[k] = scaled


def make_stream(parts, residual, gain, copies):
    rows, columns = residual.shape
    return pl.pallas_call(
        stream_kernel,
        out_shape=jax.ShapeDtypeStruct((copies, rows, columns), bf16),
        compiler_params=room(8),
        name="stream",
    )(parts, residual, gain)


def gathered_product(blocks_ref, gains_ref, weight_ref, core):
    chips, rows, columns = blocks_ref.shape
    nodes = gains_ref.shape[1] - 8
    blocks, sections, squares = [], [], 0.0
    for k in range(chips):
        block = blocks_ref[k]
        blocks.append(block)
        start = pl.multiple_of((2 * k + core) * columns, columns)
        sections.append(weight_ref[pl.ds(start, columns)])
        inverse = 1.0 / gains_ref[k, nodes:].astype(f32)
        for n in range(2):
            plain = block[:, n * 128 : (n + 1) * 128].astype(f32) * inverse[n : n + 1]
            squares = squares + plain * plain
    product = plain_dot(jnp.concatenate(blocks, axis=1), jnp.concatenate(sections, axis=0))
    return product, squares


def first_kernel(blocks_ref, gains_ref, weight_ref, product_ref, squares_ref):
    core = lax.axis_index("seq_2")
    product_ref[...], squares_ref[...] = gathered_product(
        blocks_ref, gains_ref, weight_ref, core
    )


def first_half(blocks, gains, weight):
    chips, rows, columns = blocks.shape
    width = weight.shape[1]
    return pl.pallas_call(
        first_kernel,
        out_shape=[
            jax.ShapeDtypeStruct((rows, width), f32),
            jax.ShapeDtypeStruct((rows, 128), f32),
        ],
        cost_estimate=pl.CostEstimate(
            flops=2 * rows * chips * columns * width,
            bytes_accessed=2 * chips * columns * (rows + width),
            transcendentals=0,
        ),
        compiler_params=room(16),
        name="logits_first",
    )(blocks, gains, weight)


def second_kernel(
    path_ref,
    blocks_ref,
    gains_ref,
    weight_ref,
    product_ref,
    squares_ref,
    tokens_ref,
    picked_ref,
    stats_ref,
    acc,
):
    rows, width = product_ref.shape
    core = 1 - lax.axis_index("seq_2")
    product, squares = gathered_product(blocks_ref, gains_ref, weight_ref, core)
    total = jnp.sum(squares + squares_ref[...], axis=1, keepdims=True)
    logits = (product + product_ref[...]) * lax.rsqrt(total / D + EPSILON)
    acc[...] = logits
    top = jnp.max(logits, axis=1, keepdims=True)
    sums = jnp.sum(jnp.exp(logits - top), axis=1, keepdims=True)
    ids = lax.broadcasted_iota(jnp.int32, (rows, width), 1) + lax.axis_index(SEQ_HEAD) * width
    lines = [tokens_ref[b : b + 1].astype(f32) for b in range(tokens_ref.shape[0])]
    line = jnp.broadcast_to(jnp.concatenate(lines, axis=1), (128, rows))
    tokens = jnp.transpose(line)[:, 0:1].astype(jnp.int32)
    hit = jnp.sum(jnp.where(ids == tokens, logits, 0.0), axis=1, keepdims=True)
    lane = lax.broadcasted_iota(jnp.int32, (rows, 128), 1)
    pair = jnp.transpose(jnp.where(lane == 0, top + jnp.log(sums), hit))[:2]
    for k in range(stats_ref.shape[0]):
        stats_ref[k] = pair
    for b in range(path_ref.shape[0]):
        for k in range(path_ref.shape[1]):
            n = path_ref[b, k] + b * (rows // path_ref.shape[0])
            picked_ref[k, b : b + 1] = acc[pl.ds(n, 1)]


def second_half(blocks, gains, weight, product, squares, path, tokens, copies):
    rows, width = product.shape
    specs = [pl.BlockSpec(memory_space=pltpu.VMEM)] * 6
    return pl.pallas_call(
        second_kernel,
        in_specs=[pl.BlockSpec(memory_space=pltpu.SMEM)] + specs,
        out_shape=[
            jax.ShapeDtypeStruct((*path.shape[::-1], width), f32),
            jax.ShapeDtypeStruct((copies, 2, 128), f32),
        ],
        scratch_shapes=[pltpu.VMEM((rows, width), f32)],
        compiler_params=room(16),
        name="logits_second",
    )(path, blocks, gains, weight, product, squares, tokens)


def final_kernel(stats_ref, out_ref):
    sums, hits = stats_ref[:, 0], stats_ref[:, 1]
    top = jnp.max(sums, axis=0, keepdims=True)
    total = top + jnp.log(jnp.sum(jnp.exp(sums - top), axis=0, keepdims=True))
    result = jnp.sum(hits, axis=0, keepdims=True) - total
    nodes = out_ref.shape[1]
    for b in range(out_ref.shape[0]):
        out_ref[b : b + 1] = result[:, b * nodes : (b + 1) * nodes]


def log_probabilities(stats, batch):
    return pl.pallas_call(
        final_kernel,
        out_shape=jax.ShapeDtypeStruct((batch, stats.shape[2] // batch), f32),
        compiler_params=room(4),
        name="final",
    )(stats)


def to_each(x, axes):
    return lax.all_to_all(x, axes, 0, 0, tiled=True)


def across(x):
    return lax.ppermute(x, "seq_2", [(0, 1), (1, 0)])


def on_device(
    queries,
    cache_keys,
    cache_values,
    new_keys,
    new_values,
    parents,
    path,
    lengths,
    draft_tokens,
    residual,
    out_weight,
    norm_gain,
    vocab_weight,
):
    batch, nodes = parents.shape
    rows = batch * nodes
    chips = lax.axis_size(CHIPS)
    shares = local_attention(
        queries, cache_keys, cache_values, new_keys, new_values, parents, lengths
    )
    heads = to_each(join_shares(to_each(shares, SEQ), norm_gain, chips), CHIPS)
    other_heads = across(heads)
    partial = project(heads, other_heads, out_weight, lax.axis_size("head"))
    partial = to_each(partial, "head")
    stream = make_stream(partial, residual.reshape(rows, -1), norm_gain, chips)
    mine = to_each(stream, CHIPS)
    other = across(mine)
    product, squares = first_half(mine, heads, vocab_weight)
    path_logits, stats = second_half(
        other,
        other_heads,
        vocab_weight,
        product,
        squares,
        path,
        draft_tokens,
        lax.axis_size(SEQ_HEAD),
    )
    stats = to_each(stats, SEQ_HEAD)
    logprob = log_probabilities(stats, batch)
    return (jnp.transpose(path_logits, (1, 0, 2)), logprob)


def solution(mesh):
    torus = Mesh(
        mesh.devices.reshape(4, 4, 2, mesh.shape["head"]), ("seq_0", "seq_1", "seq_2", "head")
    )
    in_specs = (
        P(None, "head", None, None),
        P(None, "head", SEQ, None),
        P(None, "head", SEQ, None),
        P(None, "head", None, None),
        P(None, "head", None, None),
        P(),
        P(),
        P(),
        P(),
        P(None, None, SEQ),
        P("head", SEQ),
        P(SEQ),
        P(None, SEQ_HEAD),
    )
    out_specs = (P(None, None, SEQ_HEAD), P())
    return jax.shard_map(
        on_device, mesh=torus, in_specs=in_specs, out_specs=out_specs, check_vma=False
    )
```

time: 103 us -> 96.8 us (0.940)
  local copies, waits for them, and re-layouts: 6.52 us -> 1.9 us
    unnamed x26 -> x14, local copies, waits for them, and re-layouts: 6.52 us -> 1.9 us
    pallas_call x3 -> x4, Pallas kernels: 9.8 us -> 9.39 us  [the longest x1 6.15 us: local_attention(): pl.pallas_call(attention_kernel, in_specs=[pl.BlockSpec(memory_space=pltp...]
  transfers between devices with their start and end apart: 2 -> 2, of which waited for: 2 -> 2; matrix products, arithmetic and copies ran while one was open for 0% -> 0% of each run, Pallas kernels for 0% -> 1%
where the time goes in v3:
time: 96.8 us; the launch traced here: 96.5 us
  blocking collectives  75.6 us (78%)
  Pallas kernels  10.6 us (11%)
  starting transfers between devices  4.92 us (5%)
  waiting for transfers between devices  2.76 us (3%)
  local copies, waits for them, and re-layouts  1.9 us (2%)
    all_to_all x5, blocking collectives, to_each(): return lax.all_to_all(x, axes, 0, 0, tiled=True)  75.6 us
    pallas_call x1, Pallas kernels, local_attention(): pl.pallas_call(attention_kernel, in_specs=[pl.BlockSpec(memory_space=pltp...  6.15 us
    ppermute x2, starting transfers between devices, across(): return lax.ppermute(x, 'seq_2', [(0, 1), (1, 0)])  4.92 us
    ppermute x2, waiting for transfers between devices, across(): return lax.ppermute(x, 'seq_2', [(0, 1), (1, 0)])  2.76 us
  transfers between devices with their start and end apart: 2, of which 2 were waited for; matrix products, arithmetic and copies ran while one was open for 0% of the time, Pallas kernels for 1%

profile of v3, /device:TPU:1, one launch (start us, length us, event | category | flops | bytes accessed | tf_op | source)
XLA Modules:
  0.0 96.5 jit_solution(14046353060092568535)
XLA Ops:
  0.6 0.0 copy-start.4
  0.6 0.0 copy-start.2
  0.7 0.0 copy-start.5
  0.7 0.0 copy-start.6
  0.7 6.2 %attend.1 = bf16[32,72,128]{2,1,0:T(8,128)(2,1)} custom-call(s32[2]{0:T(128)} %lengths_hbm.1, s32[2,64]{1,0:T(2,128)} %parents_hbm.1, bf16[2,16,64,128]{3,2,1,0:T(8,128)(2,1)} %q_hbm.1, bf16[2,2,1024,128]{3,2,1,0:T(8,128)(2,1)} %k_hbm.1, bf16[2,2,1024,128]{3,2,1,0:T(8,128)(2,1)} %v_hbm.1, bf16[2,2,64,128]{3,2,1,0:T(8,128)(2,1)} %nk_hbm.1, ...), custom_call_target="tpu_custom_call" | custom-call | tf_op jit(solution)/shard_map/attend/pallas_call | solution.py:210
  6.8 0.0 copy-start
  6.8 23.1 %all_to_all.25.parts_ref = bf16[32,72,128]{2,1,0:T(8,128)(2,1)S(1)} all-to-all(bf16[32,72,128]{2,1,0:T(8,128)(2,1)} %attend.1), channel_id=1, replica_groups=mesh['seq_0'=4,'seq_1'=4,'seq_2'=2,'head'=4] {'seq_0','seq_1','seq_2'}, dimensions={0} | all-to-all | bytes 1179648 | tf_op jit(solution)/shard_map/all_to_all | solution.py:417
  29.9 0.0 copy-start.3
  29.9 0.7 copy-done.3
  30.6 0.6 join.1
  31.2 10.8 %all_to_all.26.mine_ref.gains_ref = bf16[16,72,128]{2,1,0:T(8,128)(2,1)S(1)} all-to-all(bf16[16,72,128]{2,1,0:T(8,128)(2,1)S(1)} %join.1), channel_id=1, replica_groups=mesh['seq_0'=4,'seq_1'=4,'seq_2'=2,'head'=4] {'seq_0','seq_1'}, dimensions={0} | all-to-all | bytes 589824 | tf_op jit(solution)/shard_map/all_to_all | solution.py:417
  41.9 1.9 %collective-permute-start = (bf16[16,72,128]{2,1,0:T(8,128)(2,1)S(1)}, bf16[16,72,128]{2,1,0:T(8,128)(2,1)S(1)}, u32[]{:S(2)}, u32[]{:S(2)}) collective-permute-start(bf16[16,72,128]{2,1,0:T(8,128)(2,1)S(1)} %all_to_all.26.mine_ref.gains_ref), channel_id=1, source_target_pairs={{0,4},{4,0},{1,5},{5,1},{2,6},{6,2},{3,7},{7,3},{8,12},{12,8},{9,1... | collective-permute-start | bytes 884744 | tf_op jit(solution)/shard_map/ppermute | solution.py:421
  43.8 1.2 %collective-permute-done.other_ref.gains_ref = bf16[16,72,128]{2,1,0:T(8,128)(2,1)S(1)} collective-permute-done((bf16[16,72,128]{2,1,0:T(8,128)(2,1)S(1)}, bf16[16,72,128]{2,1,0:T(8,128)(2,1)S(1)}, u32[]{:S(2)}, u32[]{:S(2)}) %collective-permute-start) | collective-permute-done | bytes 294944 | tf_op jit(solution)/shard_map/ppermute | solution.py:421
  45.0 0.0 copy-start.1
  45.0 1.2 %copy-done.1 = bf16[2048,256]{1,0:T(8,128)(2,1)S(1)} copy-done((bf16[2048,256]{1,0:T(8,128)(2,1)S(1)}, bf16[2048,256]{1,0:T(8,128)(2,1)}, u32[]{:S(2)}) %copy-start.1) | copy-done | bytes 1048600
  46.2 0.3 project.1
  46.5 9.6 %all_to_all.27.parts_ref = bf16[4,128,256]{2,1,0:T(8,128)(2,1)S(1)} all-to-all(bf16[4,128,256]{2,1,0:T(8,128)(2,1)S(1)} %project.1), channel_id=1, replica_groups=mesh['seq_0'=4,'seq_1'=4,'seq_2'=2,'head'=4] {'head'}, dimensions={0} | all-to-all | bytes 524288 | tf_op jit(solution)/shard_map/all_to_all | solution.py:417
  56.2 0.0 copy-done.4
  56.2 0.0 copy-done.2
  56.2 0.1 stream.1
  56.3 18.2 %all_to_all.28.blocks_ref = bf16[16,128,256]{2,1,0:T(8,128)(2,1)S(1)} all-to-all(bf16[16,128,256]{2,1,0:T(8,128)(2,1)S(1)} %stream.1), channel_id=1, replica_groups=mesh['seq_0'=4,'seq_1'=4,'seq_2'=2,'head'=4] {'seq_0','seq_1'}, dimensions={0} | all-to-all | bytes 2097152 | tf_op jit(solution)/shard_map/all_to_all | solution.py:417
  74.5 3.0 %collective-permute-start.1 = (bf16[16,128,256]{2,1,0:T(8,128)(2,1)S(1)}, bf16[16,128,256]{2,1,0:T(8,128)(2,1)S(1)}, u32[]{:S(2)}, u32[]{:S(2)}) collective-permute-start(bf16[16,128,256]{2,1,0:T(8,128)(2,1)S(1)} %all_to_all.28.blocks_ref), channel_id=1, source_target_pairs={{0,4},{4,0},{1,5},{5,1},{2,6},{6,2},{3,7},{7,3},{8,12},{12,8},{9,1... | collective-permute-start | bytes 3145736 | tf_op jit(solution)/shard_map/ppermute | solution.py:421
  77.5 0.0 copy-done
  77.5 0.7 logits_first.1
  78.3 1.5 %collective-permute-done.1.blocks_ref = bf16[16,128,256]{2,1,0:T(8,128)(2,1)S(1)} collective-permute-done((bf16[16,128,256]{2,1,0:T(8,128)(2,1)S(1)}, bf16[16,128,256]{2,1,0:T(8,128)(2,1)S(1)}, u32[]{:S(2)}, u32[]{:S(2)}) %collective-permute-start.1) | collective-permute-done | bytes 1048608 | tf_op jit(solution)/shard_map/ppermute | solution.py:421
  79.8 0.0 copy-done.5
  79.8 0.0 copy-done.6
  79.8 1.9 %logits_second.1 = (f32[6,2,512]{2,1,0:T(2,128)}, f32[128,2,128]{2,1,0:T(2,128)S(1)}) custom-call(s32[2,6]{1,0:T(2,128)S(1)} %copy-done.5, bf16[16,128,256]{2,1,0:T(8,128)(2,1)S(1)} %collective-permute-done.1.blocks_ref, bf16[16,72,128]{2,1,0:T(8,128)(2,1)S(1)} %collective-permute-done.other_ref.gains_ref, bf16[8192,512]{1,0:T(8,128)(2,1)S(1)} %copy-done, ...), custom_call_target="tpu_custom_call" | custom-call | tf_op jit(solution)/shard_map/logits_second/pallas_call | solution.py:384
  81.8 14.0 %all_to_all.29.stats_ref = f32[128,2,128]{2,1,0:T(2,128)S(1)} all-to-all(f32[128,2,128]{2,1,0:T(2,128)S(1)} %get-tuple-element.9), channel_id=1, replica_groups=mesh['seq_0'=4,'seq_1'=4,'seq_2'=2,'head'=4] {'seq_0','seq_1','seq_2','h..., dimensions={0} | all-to-all | bytes 262144 | tf_op jit(solution)/shard_map/all_to_all | solution.py:417
  95.7 0.8 final.1
Async XLA Ops:
  0.6 55.5 %copy-start.4 = (bf16[256]{0:T(256)(128)(2,1)S(1)}, bf16[256]{0:T(256)(128)(2,1)}, u32[]{:S(2)}) copy-start(bf16[256]{0:T(256)(128)(2,1)} %gain_ref.3) | copy-start | bytes 1540
  0.6 55.5 %copy-start.2 = (bf16[2,64,256]{2,1,0:T(8,128)(2,1)S(1)}, bf16[2,64,256]{2,1,0:T(8,128)(2,1)}, u32[]{:S(2)}) copy-start(bf16[2,64,256]{2,1,0:T(8,128)(2,1)} %param.22) | copy-start | bytes 196612
  0.7 79.2 %copy-start.5 = (s32[2,6]{1,0:T(2,128)S(1)}, s32[2,6]{1,0:T(2,128)}, u32[]{:S(2)}) copy-start(s32[2,6]{1,0:T(2,128)} %path_ref.1) | copy-start | bytes 148
  0.7 79.2 %copy-start.6 = (s32[2,64]{1,0:T(2,128)S(1)}, s32[2,64]{1,0:T(2,128)}, u32[]{:S(2)}) copy-start(s32[2,64]{1,0:T(2,128)} %tokens_ref.1) | copy-start | bytes 1540
  6.8 70.7 %copy-start = (bf16[8192,512]{1,0:T(8,128)(2,1)S(1)}, bf16[8192,512]{1,0:T(8,128)(2,1)}, u32[]{:S(2)}) copy-start(bf16[8192,512]{1,0:T(8,128)(2,1)} %weight_ref.5) | copy-start | bytes 25165828
  29.9 0.7 copy-start.3
  41.9 3.1 %collective-permute-start = (bf16[16,72,128]{2,1,0:T(8,128)(2,1)S(1)}, bf16[16,72,128]{2,1,0:T(8,128)(2,1)S(1)}, u32[]{:S(2)}, u32[]{:S(2)}) collective-permute-start(bf16[16,72,128]{2,1,0:T(8,128)(2,1)S(1)} %all_to_all.26.mine_ref.gains_ref), channel_id=1, source_target_pairs={{0,4},{4,0},{1,5},{5,1},{2,6},{6,2},{3,7},{7,3},{8,12},{12,8},{9,1... | collective-permute-start | bytes 884744 | tf_op jit(solution)/shard_map/ppermute | solution.py:421
  45.0 1.2 %copy-start.1 = (bf16[2048,256]{1,0:T(8,128)(2,1)S(1)}, bf16[2048,256]{1,0:T(8,128)(2,1)}, u32[]{:S(2)}) copy-start(bf16[2048,256]{1,0:T(8,128)(2,1)} %weight_ref.3) | copy-start | bytes 3145732
  74.5 5.3 %collective-permute-start.1 = (bf16[16,128,256]{2,1,0:T(8,128)(2,1)S(1)}, bf16[16,128,256]{2,1,0:T(8,128)(2,1)S(1)}, u32[]{:S(2)}, u32[]{:S(2)}) collective-permute-start(bf16[16,128,256]{2,1,0:T(8,128)(2,1)S(1)} %all_to_all.28.blocks_ref), channel_id=1, source_target_pairs={{0,4},{4,0},{1,5},{5,1},{2,6},{6,2},{3,7},{7,3},{8,12},{12,8},{9,1... | collective-permute-start | bytes 3145736 | tf_op jit(solution)/shard_map/ppermute | solution.py:421

commit v4 on v3

--- a/solution.py
+++ b/solution.py
@@ -72,6 +72,7 @@
     v_hbm,
     nk_hbm,
     nv_hbm,
+    gain_hbm,
     out_ref,
     lengths_ref,
     parents_ref,
@@ -80,9 +81,10 @@
     v_ref,
     nk_ref,
     nv_ref,
+    gain_ref,
     block_sems,
     tree_sems,
-    length_sem,
+    small_sems,
 ):
     batch, heads, nodes, width = q_ref.shape
     kv, span = k_ref.shape[1:3]
@@ -96,8 +98,10 @@
     of_group = heads // group // kv
     ones = jnp.ones((span, width), bf16)
 
-    lengths_copy = pltpu.make_async_copy(lengths_hbm, lengths_ref, length_sem)
+    lengths_copy = pltpu.make_async_copy(lengths_hbm, lengths_ref, small_sems.at[0])
     lengths_copy.start()
+    gain_copy = pltpu.make_async_copy(gain_hbm, gain_ref, small_sems.at[1])
+    gain_copy.start()
 
     def block_copy(b, g, n):
         own = pl.ds(g * (heads // kv), heads // kv)
@@ -127,6 +131,10 @@
             copy.wait()
 
     lengths_copy.wait()
+    gain_copy.wait()
+    gain = gain_ref[...].astype(f32)[None]
+    gains = gain[:, :width], gain[:, width:]
+    row = lax.broadcasted_iota(jnp.int32, (8, width), 0)
 
     def write(b, part, out, top, total):
         at = b * heads + part * group
@@ -137,9 +145,12 @@
             section = turned[:, h * nodes : (h + 1) * nodes]
             total = section[1:2]
             high = total.astype(bf16).astype(f32)
-            row = lax.broadcasted_iota(jnp.int32, section.shape, 0)
-            tail = jnp.where(row == 0, section[0:1], jnp.where(row == 1, high, total - high))
-            out_ref[at + h, nodes:, :nodes] = tail.astype(bf16)
+            lines = jnp.where(row[:, :nodes] == 1, high, total - high)
+            lines = jnp.where(row[:, :nodes] == 0, section[0:1], lines)
+            tail = jnp.concatenate([lines, jnp.zeros((8, width - nodes), f32)], axis=1)
+            for n in range(2):
+                tail = jnp.where(row == 3 + n, gains[n], tail)
+            out_ref[at + h, nodes:] = tail.astype(bf16)
 
     def sweep(b, live, with_cache, with_tree):
         biases = []
@@ -196,16 +207,18 @@
         pl.when(jnp.logical_and(empty, other))(functools.partial(nothing, b))
 
 
-def local_attention(queries, cache_keys, cache_values, new_keys, new_values, parents, lengths):
+def local_attention(
+    queries, cache_keys, cache_values, new_keys, new_values, parents, lengths, gain
+):
     batch, heads, nodes, width = queries.shape
     kv = cache_keys.shape[1]
-    operands = (lengths, parents, queries, cache_keys, cache_values, new_keys, new_values)
+    operands = (lengths, parents, queries, cache_keys, cache_values, new_keys, new_values, gain)
     scratch = [pltpu.SMEM(lengths.shape, lengths.dtype)]
     scratch += [pltpu.VMEM(x.shape, x.dtype) for x in operands[1:]]
     scratch += [
         pltpu.SemaphoreType.DMA((batch, kv, 3)),
         pltpu.SemaphoreType.DMA((3,)),
-        pltpu.SemaphoreType.DMA,
+        pltpu.SemaphoreType.DMA((2,)),
     ]
     return pl.pallas_call(
         attention_kernel,
@@ -218,7 +231,7 @@
     )(*operands)
 
 
-def join_kernel(parts_ref, gain_ref, out_ref):
+def join_kernel(parts_ref, out_ref):
     count, rows, width = parts_ref.shape
     nodes = rows - 8
     tops = parts_ref[:, nodes, :].astype(f32)
@@ -234,51 +247,71 @@
     for k in range(1, count):
         total = total + parts_ref[k, :nodes].astype(f32) * turned[:, k : k + 1]
     block = total.astype(bf16)
-    gain = gain_ref[...].astype(f32)[None]
-    lines = [gain[:, :width], gain[:, width:], jnp.ones((6, width), f32)]
-    tail = jnp.concatenate(lines, axis=0).astype(bf16)
     for k in range(out_ref.shape[0]):
-        out_ref[k, :nodes] = block
-        out_ref[k, nodes:] = tail
-
-
-def join_shares(parts, gain, copies):
+        out_ref[k] = block
+
+
+def join_shares(parts, copies):
     rows, width = parts.shape[1:]
     return pl.pallas_call(
         join_kernel,
-        out_shape=jax.ShapeDtypeStruct((copies, rows, width), bf16),
+        out_shape=jax.ShapeDtypeStruct((copies, rows - 8, width), bf16),
         compiler_params=room(8),
         name="join",
-    )(parts, gain)
-
-
-def project_kernel(mine_ref, other_ref, weight_ref, out_ref):
-    chips, padded, width = mine_ref.shape
-    nodes = padded - 8
-    first = lax.axis_index("seq_2") == 0
-    mine, other = mine_ref[:, :nodes], other_ref[:, :nodes]
-    even = jnp.where(first, mine, other)
-    odd = jnp.where(first, other, mine)
-    half = chips // 2
-    lines = []
-    for b in range(2):
-        blocks = []
-        for k in range(half):
-            blocks += [even[b * half + k], odd[b * half + k]]
-        lines.append(jnp.concatenate(blocks, axis=1))
-    result = plain_dot(jnp.concatenate(lines, axis=0), weight_ref[...]).astype(bf16)
+    )(parts)
+
+
+def head_lines(blocks_ref):
+    half = blocks_ref.shape[0] // 2
+    lines = [
+        jnp.concatenate([blocks_ref[b * half + k] for k in range(half)], axis=1) for b in range(2)
+    ]
+    return jnp.concatenate(lines, axis=0)
+
+
+def project_first_kernel(blocks_ref, weight_ref, out_ref, rest_ref):
+    chips, nodes, width = blocks_ref.shape
+    core = lax.axis_index("seq_2")
+    sections = []
+    for k in range(chips // 2):
+        own = pl.multiple_of((2 * k + core) * width, width)
+        other = pl.multiple_of((2 * k + 1 - core) * width, width)
+        sections.append(weight_ref[pl.ds(own, width)])
+        rest_ref[k * width : (k + 1) * width] = weight_ref[pl.ds(other, width)]
+    out_ref[...] = plain_dot(head_lines(blocks_ref), jnp.concatenate(sections, axis=0))
+
+
+def project_second_kernel(blocks_ref, weight_ref, first_ref, out_ref):
+    result = first_ref[...] + plain_dot(head_lines(blocks_ref), weight_ref[...])
+    result = result.astype(bf16)
     for k in range(out_ref.shape[0]):
         out_ref[k] = result
 
 
-def project(mine, other, weight, copies):
-    rows = 2 * (mine.shape[1] - 8)
-    return pl.pallas_call(
-        project_kernel,
-        out_shape=jax.ShapeDtypeStruct((copies, rows, weight.shape[1]), bf16),
+def project_first(blocks, weight):
+    rows = 2 * blocks.shape[1]
+    depth, columns = weight.shape
+    return pl.pallas_call(
+        project_first_kernel,
+        out_shape=[
+            jax.ShapeDtypeStruct((rows, columns), f32),
+            jax.ShapeDtypeStruct((depth // 2, columns), weight.dtype),
+        ],
+        cost_estimate=pl.CostEstimate(
+            flops=rows * weight.size, bytes_accessed=3 * weight.size, transcendentals=0
+        ),
         compiler_params=room(8),
-        name="project",
-    )(mine, other, weight)
+        name="project_first",
+    )(blocks, weight)
+
+
+def project_second(blocks, weight, first, copies):
+    return pl.pallas_call(
+        project_second_kernel,
+        out_shape=jax.ShapeDtypeStruct((copies, *first.shape), bf16),
+        compiler_params=room(8),
+        name="project_second",
+    )(blocks, weight, first)
 
 
 def stream_kernel(parts_ref, residual_ref, gain_ref, out_ref):
@@ -300,31 +333,32 @@
     )(parts, residual, gain)
 
 
-def gathered_product(blocks_ref, gains_ref, weight_ref, core):
+def gathered_product(blocks_ref, shares_ref, weight_ref, core):
     chips, rows, columns = blocks_ref.shape
-    nodes = gains_ref.shape[1] - 8
+    nodes = shares_ref.shape[1] - 8
     blocks, sections, squares = [], [], 0.0
     for k in range(chips):
         block = blocks_ref[k]
         blocks.append(block)
-        start = pl.multiple_of((2 * k + core) * columns, columns)
-        sections.append(weight_ref[pl.ds(start, columns)])
-        inverse = 1.0 / gains_ref[k, nodes:].astype(f32)
+        source = 2 * k + core
+        sections.append(weight_ref[pl.ds(pl.multiple_of(source * columns, columns), columns)])
+        gains = shares_ref[source, nodes:].astype(f32)
         for n in range(2):
-            plain = block[:, n * 128 : (n + 1) * 128].astype(f32) * inverse[n : n + 1]
+            inverse = 1.0 / gains[3 + n : 4 + n]
+            plain = block[:, n * 128 : (n + 1) * 128].astype(f32) * inverse
             squares = squares + plain * plain
     product = plain_dot(jnp.concatenate(blocks, axis=1), jnp.concatenate(sections, axis=0))
     return product, squares
 
 
-def first_kernel(blocks_ref, gains_ref, weight_ref, product_ref, squares_ref):
+def first_kernel(blocks_ref, shares_ref, weight_ref, product_ref, squares_ref):
     core = lax.axis_index("seq_2")
     product_ref[...], squares_ref[...] = gathered_product(
-        blocks_ref, gains_ref, weight_ref, core
+        blocks_ref, shares_ref, weight_ref, core
     )
 
 
-def first_half(blocks, gains, weight):
+def first_half(blocks, shares, weight):
     chips, rows, columns = blocks.shape
     width = weight.shape[1]
     return pl.pallas_call(
@@ -340,27 +374,27 @@
         ),
         compiler_params=room(16),
         name="logits_first",
-    )(blocks, gains, weight)
+    )(blocks, shares, weight)
 
 
 def second_kernel(
     path_ref,
     blocks_ref,
-    gains_ref,
+    shares_ref,
     weight_ref,
     product_ref,
     squares_ref,
     tokens_ref,
     picked_ref,
     stats_ref,
-    acc,
+    logits_ref,
 ):
     rows, width = product_ref.shape
     core = 1 - lax.axis_index("seq_2")
-    product, squares = gathered_product(blocks_ref, gains_ref, weight_ref, core)
+    product, squares = gathered_product(blocks_ref, shares_ref, weight_ref, core)
     total = jnp.sum(squares + squares_ref[...], axis=1, keepdims=True)
     logits = (product + product_ref[...]) * lax.rsqrt(total / D + EPSILON)
-    acc[...] = logits
+    logits_ref[...] = logits
     top = jnp.max(logits, axis=1, keepdims=True)
     sums = jnp.sum(jnp.exp(logits - top), axis=1, keepdims=True)
     ids = lax.broadcasted_iota(jnp.int32, (rows, width), 1) + lax.axis_index(SEQ_HEAD) * width
@@ -375,15 +409,15 @@
     for b in range(path_ref.shape[0]):
         for k in range(path_ref.shape[1]):
             n = path_ref[b, k] + b * (rows // path_ref.shape[0])
-            picked_ref[k, b : b + 1] = acc[pl.ds(n, 1)]
-
-
-def second_half(blocks, gains, weight, product, squares, path, tokens, copies):
+            picked_ref[k, b : b + 1] = logits_ref[pl.ds(n, 1)]
+
+
+def second_half(blocks, shares, weight, product, squares, path, tokens, copies):
     rows, width = product.shape
-    specs = [pl.BlockSpec(memory_space=pltpu.VMEM)] * 6
     return pl.pallas_call(
         second_kernel,
-        in_specs=[pl.BlockSpec(memory_space=pltpu.SMEM)] + specs,
+        in_specs=[pl.BlockSpec(memory_space=pltpu.SMEM)]
+        + [pl.BlockSpec(memory_space=pltpu.VMEM)] * 6,
         out_shape=[
             jax.ShapeDtypeStruct((*path.shape[::-1], width), f32),
             jax.ShapeDtypeStruct((copies, 2, 128), f32),
@@ -391,14 +425,14 @@
         scratch_shapes=[pltpu.VMEM((rows, width), f32)],
         compiler_params=room(16),
         name="logits_second",
-    )(path, blocks, gains, weight, product, squares, tokens)
+    )(path, blocks, shares, weight, product, squares, tokens)
 
 
 def final_kernel(stats_ref, out_ref):
-    sums, hits = stats_ref[:, 0], stats_ref[:, 1]
-    top = jnp.max(sums, axis=0, keepdims=True)
-    total = top + jnp.log(jnp.sum(jnp.exp(sums - top), axis=0, keepdims=True))
-    result = jnp.sum(hits, axis=0, keepdims=True) - total
+    stats = stats_ref[...]
+    top = jnp.max(stats, axis=0)
+    total = top + jnp.log(jnp.sum(jnp.exp(stats - top[None]), axis=0))
+    result = jnp.sum(stats, axis=0)[1:2] - total[0:1]
     nodes = out_ref.shape[1]
     for b in range(out_ref.shape[0]):
         out_ref[b : b + 1] = result[:, b * nodes : (b + 1) * nodes]
@@ -440,25 +474,21 @@
     rows = batch * nodes
     chips = lax.axis_size(CHIPS)
     shares = local_attention(
-        queries, cache_keys, cache_values, new_keys, new_values, parents, lengths
+        queries, cache_keys, cache_values, new_keys, new_values, parents, lengths, norm_gain
     )
-    heads = to_each(join_shares(to_each(shares, SEQ), norm_gain, chips), CHIPS)
+    shares = to_each(shares, SEQ)
+    heads = to_each(join_shares(shares, chips), CHIPS)
     other_heads = across(heads)
-    partial = project(heads, other_heads, out_weight, lax.axis_size("head"))
+    partial, rest = project_first(heads, out_weight)
+    partial = project_second(other_heads, rest, partial, lax.axis_size("head"))
     partial = to_each(partial, "head")
     stream = make_stream(partial, residual.reshape(rows, -1), norm_gain, chips)
     mine = to_each(stream, CHIPS)
     other = across(mine)
-    product, squares = first_half(mine, heads, vocab_weight)
+    product, squares = first_half(mine, shares, vocab_weight)
+    copies = lax.axis_size(SEQ_HEAD)
     path_logits, stats = second_half(
-        other,
-        other_heads,
-        vocab_weight,
-        product,
-        squares,
-        path,
-        draft_tokens,
-        lax.axis_size(SEQ_HEAD),
+        other, shares, vocab_weight, product, squares, path, draft_tokens, copies
     )
     stats = to_each(stats, SEQ_HEAD)
     logprob = log_probabilities(stats, batch)

time: 96.8 us -> 95.6 us (0.988)
  waiting for transfers between devices: 2.76 us -> 1.56 us
    ppermute x2, waiting for transfers between devices: 2.76 us -> 1.56 us  [across(): return lax.ppermute(x, 'seq_2', [(0, 1), (1, 0)])]
  transfers between devices with their start and end apart: 2 -> 2, of which waited for: 2 -> 1; matrix products, arithmetic and copies ran while one was open for 0% -> 0% of each run, Pallas kernels for 1% -> 1%
where the time goes in v4:
time: 95.6 us; the launch traced here: 95.3 us
  blocking collectives  75.5 us (79%)
  Pallas kernels  11 us (12%)
  starting transfers between devices  5.26 us (6%)
  waiting for transfers between devices  1.56 us (2%)
  local copies, waits for them, and re-layouts  1.25 us (1%)
    all_to_all x5, blocking collectives, to_each(): return lax.all_to_all(x, axes, 0, 0, tiled=True)  75.5 us
    pallas_call x1, Pallas kernels, local_attention(): pl.pallas_call(attention_kernel, in_specs=[pl.BlockSpec(memory_space=pltp...  6.33 us
    ppermute x2, starting transfers between devices, across(): return lax.ppermute(x, 'seq_2', [(0, 1), (1, 0)])  5.26 us
    pallas_call x1, Pallas kernels, second_half(): pl.pallas_call(second_kernel, in_specs=[pl.BlockSpec(memory_space=pltpu.S...  1.93 us
  transfers between devices with their start and end apart: 2, of which 1 were waited for; matrix products, arithmetic and copies ran while one was open for 0% of the time, Pallas kernels for 1%

profile of v4, /device:TPU:1, one launch (start us, length us, event | category | flops | bytes accessed | tf_op | source)
XLA Modules:
  0.0 95.3 jit_solution(17933628807956076272)
XLA Ops:
  0.6 0.0 copy-start.3
  0.6 0.0 copy-start.2
  0.7 6.3 %attend.1 = bf16[32,72,128]{2,1,0:T(8,128)(2,1)} custom-call(s32[2]{0:T(128)} %lengths_hbm.1, s32[2,64]{1,0:T(2,128)} %parents_hbm.1, bf16[2,16,64,128]{3,2,1,0:T(8,128)(2,1)} %q_hbm.1, bf16[2,2,1024,128]{3,2,1,0:T(8,128)(2,1)} %k_hbm.1, bf16[2,2,1024,128]{3,2,1,0:T(8,128)(2,1)} %v_hbm.1, bf16[2,2,64,128]{3,2,1,0:T(8,128)(2,1)} %nk_hbm.1, ...), custom_call_target="tpu_custom_call" | custom-call | tf_op jit(solution)/shard_map/attend/pallas_call | solution.py:223
  7.0 0.0 copy-start
  7.0 22.9 %all_to_all.25.parts_ref.shares_ref = bf16[32,72,128]{2,1,0:T(8,128)(2,1)S(1)} all-to-all(bf16[32,72,128]{2,1,0:T(8,128)(2,1)} %attend.1), channel_id=1, replica_groups=mesh['seq_0'=4,'seq_1'=4,'seq_2'=2,'head'=4] {'seq_0','seq_1','seq_2'}, dimensions={0} | all-to-all | bytes 1179648 | tf_op jit(solution)/shard_map/all_to_all | solution.py:451
  30.0 0.6 join.1
  30.5 10.5 %all_to_all.26.blocks_ref = bf16[16,64,128]{2,1,0:T(8,128)(2,1)S(1)} all-to-all(bf16[16,64,128]{2,1,0:T(8,128)(2,1)S(1)} %join.1), channel_id=1, replica_groups=mesh['seq_0'=4,'seq_1'=4,'seq_2'=2,'head'=4] {'seq_0','seq_1'}, dimensions={0} | all-to-all | bytes 524288 | tf_op jit(solution)/shard_map/all_to_all | solution.py:451
  41.0 1.8 %collective-permute-start = (bf16[16,64,128]{2,1,0:T(8,128)(2,1)S(1)}, bf16[16,64,128]{2,1,0:T(8,128)(2,1)S(1)}, u32[]{:S(2)}, u32[]{:S(2)}) collective-permute-start(bf16[16,64,128]{2,1,0:T(8,128)(2,1)S(1)} %all_to_all.26.blocks_ref), channel_id=1, source_target_pairs={{0,4},{4,0},{1,5},{5,1},{2,6},{6,2},{3,7},{7,3},{8,12},{12,8},{9,1... | collective-permute-start | bytes 786440 | tf_op jit(solution)/shard_map/ppermute | solution.py:455
  42.9 0.0 copy-start.1
  42.9 1.2 %copy-done.1 = bf16[2048,256]{1,0:T(8,128)(2,1)S(1)} copy-done((bf16[2048,256]{1,0:T(8,128)(2,1)S(1)}, bf16[2048,256]{1,0:T(8,128)(2,1)}, u32[]{:S(2)}) %copy-start.1) | copy-done | bytes 1048600
  44.1 0.0 copy-start.4
  44.1 0.0 copy-start.5
  44.1 0.3 project_first.1
  44.4 0.0 collective-permute-done.blocks_ref
  44.4 0.2 project_second.1
  44.6 10.3 %all_to_all.27.parts_ref = bf16[4,128,256]{2,1,0:T(8,128)(2,1)S(1)} all-to-all(bf16[4,128,256]{2,1,0:T(8,128)(2,1)S(1)} %project_second.1), channel_id=1, replica_groups=mesh['seq_0'=4,'seq_1'=4,'seq_2'=2,'head'=4] {'head'}, dimensions={0} | all-to-all | bytes 524288 | tf_op jit(solution)/shard_map/all_to_all | solution.py:451
  54.9 0.0 copy-done.3
  54.9 0.0 copy-done.2
  54.9 0.1 stream.1
  55.0 17.8 %all_to_all.28.blocks_ref = bf16[16,128,256]{2,1,0:T(8,128)(2,1)S(1)} all-to-all(bf16[16,128,256]{2,1,0:T(8,128)(2,1)S(1)} %stream.1), channel_id=1, replica_groups=mesh['seq_0'=4,'seq_1'=4,'seq_2'=2,'head'=4] {'seq_0','seq_1'}, dimensions={0} | all-to-all | bytes 2097152 | tf_op jit(solution)/shard_map/all_to_all | solution.py:451
  72.8 3.4 %collective-permute-start.1 = (bf16[16,128,256]{2,1,0:T(8,128)(2,1)S(1)}, bf16[16,128,256]{2,1,0:T(8,128)(2,1)S(1)}, u32[]{:S(2)}, u32[]{:S(2)}) collective-permute-start(bf16[16,128,256]{2,1,0:T(8,128)(2,1)S(1)} %all_to_all.28.blocks_ref), channel_id=1, source_target_pairs={{0,4},{4,0},{1,5},{5,1},{2,6},{6,2},{3,7},{7,3},{8,12},{12,8},{9,1... | collective-permute-start | bytes 3145736 | tf_op jit(solution)/shard_map/ppermute | solution.py:455
  76.2 0.0 copy-done
  76.2 0.7 logits_first.1
  77.0 1.6 %collective-permute-done.1.blocks_ref = bf16[16,128,256]{2,1,0:T(8,128)(2,1)S(1)} collective-permute-done((bf16[16,128,256]{2,1,0:T(8,128)(2,1)S(1)}, bf16[16,128,256]{2,1,0:T(8,128)(2,1)S(1)}, u32[]{:S(2)}, u32[]{:S(2)}) %collective-permute-start.1) | collective-permute-done | bytes 1048608 | tf_op jit(solution)/shard_map/ppermute | solution.py:455
  78.5 0.0 copy-done.4
  78.5 0.0 copy-done.5
  78.5 1.9 %logits_second.1 = (f32[6,2,512]{2,1,0:T(2,128)}, f32[128,2,128]{2,1,0:T(2,128)S(1)}) custom-call(s32[2,6]{1,0:T(2,128)S(1)} %copy-done.4, bf16[16,128,256]{2,1,0:T(8,128)(2,1)S(1)} %collective-permute-done.1.blocks_ref, bf16[32,72,128]{2,1,0:T(8,128)(2,1)S(1)} %all_to_all.25.parts_ref.shares_ref, bf16[8192,512]{1,0:T(8,128)(2,1)S(1)} %copy-done, ...), custom_call_target="tpu_custom_call" | custom-call | tf_op jit(solution)/shard_map/logits_second/pallas_call | solution.py:417
  80.5 14.0 %all_to_all.29.stats_ref = f32[128,2,128]{2,1,0:T(2,128)S(1)} all-to-all(f32[128,2,128]{2,1,0:T(2,128)S(1)} %get-tuple-element.13), channel_id=1, replica_groups=mesh['seq_0'=4,'seq_1'=4,'seq_2'=2,'head'=4] {'seq_0','seq_1','seq_2','h..., dimensions={0} | all-to-all | bytes 262144 | tf_op jit(solution)/shard_map/all_to_all | solution.py:451
  94.4 0.8 final.1
Async XLA Ops:
  0.6 54.3 %copy-start.3 = (bf16[256]{0:T(256)(128)(2,1)S(1)}, bf16[256]{0:T(256)(128)(2,1)}, u32[]{:S(2)}) copy-start(bf16[256]{0:T(256)(128)(2,1)} %gain_ref.1) | copy-start | bytes 1540
  0.6 54.3 %copy-start.2 = (bf16[2,64,256]{2,1,0:T(8,128)(2,1)S(1)}, bf16[2,64,256]{2,1,0:T(8,128)(2,1)}, u32[]{:S(2)}) copy-start(bf16[2,64,256]{2,1,0:T(8,128)(2,1)} %param.22) | copy-start | bytes 196612
  7.0 69.3 %copy-start = (bf16[8192,512]{1,0:T(8,128)(2,1)S(1)}, bf16[8192,512]{1,0:T(8,128)(2,1)}, u32[]{:S(2)}) copy-start(bf16[8192,512]{1,0:T(8,128)(2,1)} %weight_ref.5) | copy-start | bytes 25165828
  41.0 3.3 %collective-permute-start = (bf16[16,64,128]{2,1,0:T(8,128)(2,1)S(1)}, bf16[16,64,128]{2,1,0:T(8,128)(2,1)S(1)}, u32[]{:S(2)}, u32[]{:S(2)}) collective-permute-start(bf16[16,64,128]{2,1,0:T(8,128)(2,1)S(1)} %all_to_all.26.blocks_ref), channel_id=1, source_target_pairs={{0,4},{4,0},{1,5},{5,1},{2,6},{6,2},{3,7},{7,3},{8,12},{12,8},{9,1... | collective-permute-start | bytes 786440 | tf_op jit(solution)/shard_map/ppermute | solution.py:455
  42.9 1.2 %copy-start.1 = (bf16[2048,256]{1,0:T(8,128)(2,1)S(1)}, bf16[2048,256]{1,0:T(8,128)(2,1)}, u32[]{:S(2)}) copy-start(bf16[2048,256]{1,0:T(8,128)(2,1)} %weight_ref.3) | copy-start | bytes 3145732
  44.1 34.4 %copy-start.4 = (s32[2,6]{1,0:T(2,128)S(1)}, s32[2,6]{1,0:T(2,128)}, u32[]{:S(2)}) copy-start(s32[2,6]{1,0:T(2,128)} %path_ref.1) | copy-start | bytes 148
  44.1 34.4 %copy-start.5 = (s32[2,64]{1,0:T(2,128)S(1)}, s32[2,64]{1,0:T(2,128)}, u32[]{:S(2)}) copy-start(s32[2,64]{1,0:T(2,128)} %tokens_ref.1) | copy-start | bytes 1540
  72.8 5.7 %collective-permute-start.1 = (bf16[16,128,256]{2,1,0:T(8,128)(2,1)S(1)}, bf16[16,128,256]{2,1,0:T(8,128)(2,1)S(1)}, u32[]{:S(2)}, u32[]{:S(2)}) collective-permute-start(bf16[16,128,256]{2,1,0:T(8,128)(2,1)S(1)} %all_to_all.28.blocks_ref), channel_id=1, source_target_pairs={{0,4},{4,0},{1,5},{5,1},{2,6},{6,2},{3,7},{7,3},{8,12},{12,8},{9,1... | collective-permute-start | bytes 3145736 | tf_op jit(solution)/shard_map/ppermute | solution.py:455

commit v5 on v4

--- a/solution.py
+++ b/solution.py
@@ -10,7 +10,7 @@
 
 D = 8192
 SEQ = ("seq_0", "seq_1", "seq_2")
-CHIPS = ("seq_0", "seq_1")
+CHIPS = ("seq_1", "seq_0")
 SEQ_HEAD = ("seq_0", "seq_1", "seq_2", "head")
 
 HIDDEN = -1e30
@@ -27,6 +27,10 @@
     return lax.dot_general(a, b, (((1,), (1,)), ((), ())), preferred_element_type=f32)
 
 
+def place_of(chip, side=4):
+    return chip % side * side + chip // side
+
+
 def plain_dot(a, b):
     return lax.dot_general(a, b, (((1,), (0,)), ((), ())), preferred_element_type=f32)
 
@@ -37,6 +41,10 @@
 
 def rows_dot(a, b):
     return lax.dot_general(a, b, (((1,), (1,)), ((), ())), preferred_element_type=f32)
+
+
+def place_of(chip, side=4):
+    return chip % side * side + chip // side
 
 
 def plain_dot(a, b):
@@ -264,7 +272,8 @@
 def head_lines(blocks_ref):
     half = blocks_ref.shape[0] // 2
     lines = [
-        jnp.concatenate([blocks_ref[b * half + k] for k in range(half)], axis=1) for b in range(2)
+        jnp.concatenate([blocks_ref[place_of(b * half + k)] for k in range(half)], axis=1)
+        for b in range(2)
     ]
     return jnp.concatenate(lines, axis=0)
 
@@ -340,7 +349,7 @@
     for k in range(chips):
         block = blocks_ref[k]
         blocks.append(block)
-        source = 2 * k + core
+        source = 2 * place_of(k) + core
         sections.append(weight_ref[pl.ds(pl.multiple_of(source * columns, columns), columns)])
         gains = shares_ref[source, nodes:].astype(f32)
         for n in range(2):

time: 95.6 us -> 95 us (level)
  starting transfers between devices: 5.26 us -> 3.66 us
  blocking collectives: 75.5 us -> 76.5 us
    ppermute x2, starting transfers between devices: 5.26 us -> 3.66 us  [across(): return lax.ppermute(x, 'seq_2', [(0, 1), (1, 0)])]
    all_to_all x5, blocking collectives: 75.5 us -> 76.5 us  [to_each(): return lax.all_to_all(x, axes, 0, 0, tiled=True)]
where the time goes in v5:
time: 95 us; the launch traced here: 94.7 us
  blocking collectives  76.5 us (81%)
  Pallas kernels  11 us (12%)
  starting transfers between devices  3.66 us (4%)
  waiting for transfers between devices  1.56 us (2%)
  local copies, waits for them, and re-layouts  1.25 us (1%)
    all_to_all x5, blocking collectives, to_each(): return lax.all_to_all(x, axes, 0, 0, tiled=True)  76.5 us
    pallas_call x1, Pallas kernels, local_attention(): pl.pallas_call(attention_kernel, in_specs=[pl.BlockSpec(memory_space=pltp...  6.33 us
    ppermute x2, starting transfers between devices, across(): return lax.ppermute(x, 'seq_2', [(0, 1), (1, 0)])  3.66 us
    pallas_call x1, Pallas kernels, second_half(): pl.pallas_call(second_kernel, in_specs=[pl.BlockSpec(memory_space=pltpu.S...  1.93 us
  transfers between devices with their start and end apart: 2, of which 1 were waited for; matrix products, arithmetic and copies ran while one was open for 0% of the time, Pallas kernels for 1%

profile of v5, /device:TPU:1, one launch (start us, length us, event | category | flops | bytes accessed | tf_op | source)
XLA Modules:
  0.0 94.7 jit_solution(3826865739825241188)
XLA Ops:
  0.6 0.0 copy-start.3
  0.6 0.0 copy-start.2
  0.7 6.3 %attend.1 = bf16[32,72,128]{2,1,0:T(8,128)(2,1)} custom-call(s32[2]{0:T(128)} %lengths_hbm.1, s32[2,64]{1,0:T(2,128)} %parents_hbm.1, bf16[2,16,64,128]{3,2,1,0:T(8,128)(2,1)} %q_hbm.1, bf16[2,2,1024,128]{3,2,1,0:T(8,128)(2,1)} %k_hbm.1, bf16[2,2,1024,128]{3,2,1,0:T(8,128)(2,1)} %v_hbm.1, bf16[2,2,64,128]{3,2,1,0:T(8,128)(2,1)} %nk_hbm.1, ...), custom_call_target="tpu_custom_call" | custom-call | tf_op jit(solution)/shard_map/attend/pallas_call | solution.py:231
  7.0 0.0 copy-start
  7.0 22.9 %all_to_all.25.parts_ref.shares_ref = bf16[32,72,128]{2,1,0:T(8,128)(2,1)S(1)} all-to-all(bf16[32,72,128]{2,1,0:T(8,128)(2,1)} %attend.1), channel_id=1, replica_groups=mesh['seq_0'=4,'seq_1'=4,'seq_2'=2,'head'=4] {'seq_0','seq_1','seq_2'}, dimensions={0} | all-to-all | bytes 1179648 | tf_op jit(solution)/shard_map/all_to_all | solution.py:460
  30.0 0.6 join.1
  30.5 11.1 %all_to_all.26.blocks_ref = bf16[16,64,128]{2,1,0:T(8,128)(2,1)S(1)} all-to-all(bf16[16,64,128]{2,1,0:T(8,128)(2,1)S(1)} %join.1), channel_id=1, replica_groups=mesh['seq_0'=4,'seq_1'=4,'seq_2'=2,'head'=4] {'seq_1','seq_0'}, dimensions={0} | all-to-all | bytes 524288 | tf_op jit(solution)/shard_map/all_to_all | solution.py:460
  41.6 1.4 %collective-permute-start = (bf16[16,64,128]{2,1,0:T(8,128)(2,1)S(1)}, bf16[16,64,128]{2,1,0:T(8,128)(2,1)S(1)}, u32[]{:S(2)}, u32[]{:S(2)}) collective-permute-start(bf16[16,64,128]{2,1,0:T(8,128)(2,1)S(1)} %all_to_all.26.blocks_ref), channel_id=1, source_target_pairs={{0,4},{4,0},{1,5},{5,1},{2,6},{6,2},{3,7},{7,3},{8,12},{12,8},{9,1... | collective-permute-start | bytes 786440 | tf_op jit(solution)/shard_map/ppermute | solution.py:464
  43.0 0.0 copy-start.1
  43.0 1.2 %copy-done.1 = bf16[2048,256]{1,0:T(8,128)(2,1)S(1)} copy-done((bf16[2048,256]{1,0:T(8,128)(2,1)S(1)}, bf16[2048,256]{1,0:T(8,128)(2,1)}, u32[]{:S(2)}) %copy-start.1) | copy-done | bytes 1048600
  44.3 0.0 copy-start.4
  44.3 0.0 copy-start.5
  44.3 0.3 project_first.1
  44.5 0.0 collective-permute-done.blocks_ref
  44.5 0.2 project_second.1
  44.8 10.3 %all_to_all.27.parts_ref = bf16[4,128,256]{2,1,0:T(8,128)(2,1)S(1)} all-to-all(bf16[4,128,256]{2,1,0:T(8,128)(2,1)S(1)} %project_second.1), channel_id=1, replica_groups=mesh['seq_0'=4,'seq_1'=4,'seq_2'=2,'head'=4] {'head'}, dimensions={0} | all-to-all | bytes 524288 | tf_op jit(solution)/shard_map/all_to_all | solution.py:460
  55.1 0.0 copy-done.3
  55.1 0.0 copy-done.2
  55.1 0.1 stream.1
  55.2 18.5 %all_to_all.28.blocks_ref = bf16[16,128,256]{2,1,0:T(8,128)(2,1)S(1)} all-to-all(bf16[16,128,256]{2,1,0:T(8,128)(2,1)S(1)} %stream.1), channel_id=1, replica_groups=mesh['seq_0'=4,'seq_1'=4,'seq_2'=2,'head'=4] {'seq_1','seq_0'}, dimensions={0} | all-to-all | bytes 2097152 | tf_op jit(solution)/shard_map/all_to_all | solution.py:460
  73.7 2.2 %collective-permute-start.1 = (bf16[16,128,256]{2,1,0:T(8,128)(2,1)S(1)}, bf16[16,128,256]{2,1,0:T(8,128)(2,1)S(1)}, u32[]{:S(2)}, u32[]{:S(2)}) collective-permute-start(bf16[16,128,256]{2,1,0:T(8,128)(2,1)S(1)} %all_to_all.28.blocks_ref), channel_id=1, source_target_pairs={{0,4},{4,0},{1,5},{5,1},{2,6},{6,2},{3,7},{7,3},{8,12},{12,8},{9,1... | collective-permute-start | bytes 3145736 | tf_op jit(solution)/shard_map/ppermute | solution.py:464
  75.9 0.0 copy-done
  75.9 0.7 logits_first.1
  76.7 1.6 %collective-permute-done.1.blocks_ref = bf16[16,128,256]{2,1,0:T(8,128)(2,1)S(1)} collective-permute-done((bf16[16,128,256]{2,1,0:T(8,128)(2,1)S(1)}, bf16[16,128,256]{2,1,0:T(8,128)(2,1)S(1)}, u32[]{:S(2)}, u32[]{:S(2)}) %collective-permute-start.1) | collective-permute-done | bytes 1048608 | tf_op jit(solution)/shard_map/ppermute | solution.py:464
  78.2 0.0 copy-done.4
  78.2 0.0 copy-done.5
  78.2 1.9 %logits_second.1 = (f32[6,2,512]{2,1,0:T(2,128)}, f32[128,2,128]{2,1,0:T(2,128)S(1)}) custom-call(s32[2,6]{1,0:T(2,128)S(1)} %copy-done.4, bf16[16,128,256]{2,1,0:T(8,128)(2,1)S(1)} %collective-permute-done.1.blocks_ref, bf16[32,72,128]{2,1,0:T(8,128)(2,1)S(1)} %all_to_all.25.parts_ref.shares_ref, bf16[8192,512]{1,0:T(8,128)(2,1)S(1)} %copy-done, ...), custom_call_target="tpu_custom_call" | custom-call | tf_op jit(solution)/shard_map/logits_second/pallas_call | solution.py:426
  80.2 13.7 %all_to_all.29.stats_ref = f32[128,2,128]{2,1,0:T(2,128)S(1)} all-to-all(f32[128,2,128]{2,1,0:T(2,128)S(1)} %get-tuple-element.13), channel_id=1, replica_groups=mesh['seq_0'=4,'seq_1'=4,'seq_2'=2,'head'=4] {'seq_0','seq_1','seq_2','h..., dimensions={0} | all-to-all | bytes 262144 | tf_op jit(solution)/shard_map/all_to_all | solution.py:460
  93.8 0.8 final.1
Async XLA Ops:
  0.6 54.4 %copy-start.3 = (bf16[256]{0:T(256)(128)(2,1)S(1)}, bf16[256]{0:T(256)(128)(2,1)}, u32[]{:S(2)}) copy-start(bf16[256]{0:T(256)(128)(2,1)} %gain_ref.1) | copy-start | bytes 1540
  0.6 54.4 %copy-start.2 = (bf16[2,64,256]{2,1,0:T(8,128)(2,1)S(1)}, bf16[2,64,256]{2,1,0:T(8,128)(2,1)}, u32[]{:S(2)}) copy-start(bf16[2,64,256]{2,1,0:T(8,128)(2,1)} %param.22) | copy-start | bytes 196612
  7.0 68.9 %copy-start = (bf16[8192,512]{1,0:T(8,128)(2,1)S(1)}, bf16[8192,512]{1,0:T(8,128)(2,1)}, u32[]{:S(2)}) copy-start(bf16[8192,512]{1,0:T(8,128)(2,1)} %weight_ref.5) | copy-start | bytes 25165828
  41.6 2.9 %collective-permute-start = (bf16[16,64,128]{2,1,0:T(8,128)(2,1)S(1)}, bf16[16,64,128]{2,1,0:T(8,128)(2,1)S(1)}, u32[]{:S(2)}, u32[]{:S(2)}) collective-permute-start(bf16[16,64,128]{2,1,0:T(8,128)(2,1)S(1)} %all_to_all.26.blocks_ref), channel_id=1, source_target_pairs={{0,4},{4,0},{1,5},{5,1},{2,6},{6,2},{3,7},{7,3},{8,12},{12,8},{9,1... | collective-permute-start | bytes 786440 | tf_op jit(solution)/shard_map/ppermute | solution.py:464
  43.0 1.2 %copy-start.1 = (bf16[2048,256]{1,0:T(8,128)(2,1)S(1)}, bf16[2048,256]{1,0:T(8,128)(2,1)}, u32[]{:S(2)}) copy-start(bf16[2048,256]{1,0:T(8,128)(2,1)} %weight_ref.3) | copy-start | bytes 3145732
  44.3 34.0 %copy-start.4 = (s32[2,6]{1,0:T(2,128)S(1)}, s32[2,6]{1,0:T(2,128)}, u32[]{:S(2)}) copy-start(s32[2,6]{1,0:T(2,128)} %path_ref.1) | copy-start | bytes 148
  44.3 34.0 %copy-start.5 = (s32[2,64]{1,0:T(2,128)S(1)}, s32[2,64]{1,0:T(2,128)}, u32[]{:S(2)}) copy-start(s32[2,64]{1,0:T(2,128)} %tokens_ref.1) | copy-start | bytes 1540
  73.7 4.5 %collective-permute-start.1 = (bf16[16,128,256]{2,1,0:T(8,128)(2,1)S(1)}, bf16[16,128,256]{2,1,0:T(8,128)(2,1)S(1)}, u32[]{:S(2)}, u32[]{:S(2)}) collective-permute-start(bf16[16,128,256]{2,1,0:T(8,128)(2,1)S(1)} %all_to_all.28.blocks_ref), channel_id=1, source_target_pairs={{0,4},{4,0},{1,5},{5,1},{2,6},{6,2},{3,7},{7,3},{8,12},{12,8},{9,1... | collective-permute-start | bytes 3145736 | tf_op jit(solution)/shard_map/ppermute | solution.py:464

commit v6 on v5

--- a/solution.py
+++ b/solution.py
@@ -387,16 +387,7 @@
 
 
 def second_kernel(
-    path_ref,
-    blocks_ref,
-    shares_ref,
-    weight_ref,
-    product_ref,
-    squares_ref,
-    tokens_ref,
-    picked_ref,
-    stats_ref,
-    logits_ref,
+    blocks_ref, shares_ref, weight_ref, product_ref, squares_ref, tokens_ref, logits_ref, stats_ref
 ):
     rows, width = product_ref.shape
     core = 1 - lax.axis_index("seq_2")
@@ -412,48 +403,55 @@
     tokens = jnp.transpose(line)[:, 0:1].astype(jnp.int32)
     hit = jnp.sum(jnp.where(ids == tokens, logits, 0.0), axis=1, keepdims=True)
     lane = lax.broadcasted_iota(jnp.int32, (rows, 128), 1)
-    pair = jnp.transpose(jnp.where(lane == 0, top + jnp.log(sums), hit))[:2]
-    for k in range(stats_ref.shape[0]):
-        stats_ref[k] = pair
-    for b in range(path_ref.shape[0]):
+    turned = jnp.transpose(jnp.where(lane % 2 == 0, top + jnp.log(sums), hit))[:8]
+    for k in range(stats_ref.shape[0] // 8):
+        stats_ref[k * 8 : k * 8 + 8] = turned
+
+
+def second_half(blocks, shares, weight, product, squares, tokens, copies):
+    return pl.pallas_call(
+        second_kernel,
+        out_shape=[
+            jax.ShapeDtypeStruct(product.shape, f32),
+            jax.ShapeDtypeStruct((copies * 2, 128), f32),
+        ],
+        compiler_params=room(16),
+        name="logits_second",
+    )(blocks, shares, weight, product, squares, tokens)
+
+
+def final_kernel(path_ref, stats_ref, logits_ref, picked_ref, out_ref):
+    batch, nodes = out_ref.shape
+    for b in range(batch):
         for k in range(path_ref.shape[1]):
-            n = path_ref[b, k] + b * (rows // path_ref.shape[0])
-            picked_ref[k, b : b + 1] = logits_ref[pl.ds(n, 1)]
-
-
-def second_half(blocks, shares, weight, product, squares, path, tokens, copies):
-    rows, width = product.shape
-    return pl.pallas_call(
-        second_kernel,
-        in_specs=[pl.BlockSpec(memory_space=pltpu.SMEM)]
-        + [pl.BlockSpec(memory_space=pltpu.VMEM)] * 6,
+            picked_ref[k, b : b + 1] = logits_ref[pl.ds(path_ref[b, k] + b * nodes, 1)]
+    stats = stats_ref[...]
+    is_sum = lax.broadcasted_iota(jnp.int32, stats.shape, 0) % 2 == 0
+    sums = jnp.where(is_sum, stats, HIDDEN)
+    top = jnp.max(sums, axis=0, keepdims=True)
+    total = top + jnp.log(jnp.sum(jnp.exp(sums - top), axis=0, keepdims=True))
+    result = jnp.sum(jnp.where(is_sum, 0.0, stats), axis=0, keepdims=True) - total
+    for b in range(batch):
+        out_ref[b : b + 1] = result[:, b * nodes : (b + 1) * nodes]
+
+
+def final_join(path, stats, logits):
+    batch = path.shape[0]
+    rows, width = logits.shape
+    return pl.pallas_call(
+        final_kernel,
+        in_specs=[
+            pl.BlockSpec(memory_space=pltpu.SMEM),
+            pl.BlockSpec(memory_space=pltpu.VMEM),
+            pl.BlockSpec(memory_space=pltpu.VMEM),
+        ],
         out_shape=[
             jax.ShapeDtypeStruct((*path.shape[::-1], width), f32),
-            jax.ShapeDtypeStruct((copies, 2, 128), f32),
+            jax.ShapeDtypeStruct((batch, rows // batch), f32),
         ],
-        scratch_shapes=[pltpu.VMEM((rows, width), f32)],
-        compiler_params=room(16),
-        name="logits_second",
-    )(path, blocks, shares, weight, product, squares, tokens)
-
-
-def final_kernel(stats_ref, out_ref):
-    stats = stats_ref[...]
-    top = jnp.max(stats, axis=0)
-    total = top + jnp.log(jnp.sum(jnp.exp(stats - top[None]), axis=0))
-    result = jnp.sum(stats, axis=0)[1:2] - total[0:1]
-    nodes = out_ref.shape[1]
-    for b in range(out_ref.shape[0]):
-        out_ref[b : b + 1] = result[:, b * nodes : (b + 1) * nodes]
-
-
-def log_probabilities(stats, batch):
-    return pl.pallas_call(
-        final_kernel,
-        out_shape=jax.ShapeDtypeStruct((batch, stats.shape[2] // batch), f32),
         compiler_params=room(4),
         name="final",
-    )(stats)
+    )(path, stats, logits)
 
 
 def to_each(x, axes):
@@ -479,8 +477,7 @@
     norm_gain,
     vocab_weight,
 ):
-    batch, nodes = parents.shape
-    rows = batch * nodes
+    rows = parents.size
     chips = lax.axis_size(CHIPS)
     shares = local_attention(
         queries, cache_keys, cache_values, new_keys, new_values, parents, lengths, norm_gain
@@ -496,11 +493,11 @@
     other = across(mine)
     product, squares = first_half(mine, shares, vocab_weight)
     copies = lax.axis_size(SEQ_HEAD)
-    path_logits, stats = second_half(
-        other, shares, vocab_weight, product, squares, path, draft_tokens, copies
+    logits, stats = second_half(
+        other, shares, vocab_weight, product, squares, draft_tokens, copies
     )
-    stats = to_each(stats, SEQ_HEAD)
-    logprob = log_probabilities(stats, batch)
+    stats = to_each(stats.reshape(copies, 2, 128), SEQ_HEAD).reshape(copies * 2, 128)
+    path_logits, logprob = final_join(path, stats, logits)
     return (jnp.transpose(path_logits, (1, 0, 2)), logprob)
 
 

time: 95 us -> 94.7 us (level)
  no operation moved by 1% of the time
where the time goes in v6:
time: 94.7 us; the launch traced here: 94.3 us
  blocking collectives  76.5 us (81%)
  Pallas kernels  10.8 us (11%)
  starting transfers between devices  3.67 us (4%)
  waiting for transfers between devices  1.46 us (2%)
  local copies, waits for them, and re-layouts  1.25 us (1%)
    all_to_all x5, blocking collectives, to_each(): return lax.all_to_all(x, axes, 0, 0, tiled=True)  76.5 us
    pallas_call x1, Pallas kernels, local_attention(): pl.pallas_call(attention_kernel, in_specs=[pl.BlockSpec(memory_space=pltp...  6.32 us
    ppermute x2, starting transfers between devices, across(): return lax.ppermute(x, 'seq_2', [(0, 1), (1, 0)])  3.67 us
  transfers between devices with their start and end apart: 2, of which 1 were waited for; matrix products, arithmetic and copies ran while one was open for 0% of the time, Pallas kernels for 1%

profile of v6, /device:TPU:1, one launch (start us, length us, event | category | flops | bytes accessed | tf_op | source)
XLA Modules:
  0.0 94.3 jit_solution(7491001227156015035)
XLA Ops:
  0.6 0.0 copy-start.3
  0.6 0.0 copy-start.2
  0.7 6.3 %attend.1 = bf16[32,72,128]{2,1,0:T(8,128)(2,1)} custom-call(s32[2]{0:T(128)} %lengths_hbm.1, s32[2,64]{1,0:T(2,128)} %parents_hbm.1, bf16[2,16,64,128]{3,2,1,0:T(8,128)(2,1)} %q_hbm.1, bf16[2,2,1024,128]{3,2,1,0:T(8,128)(2,1)} %k_hbm.1, bf16[2,2,1024,128]{3,2,1,0:T(8,128)(2,1)} %v_hbm.1, bf16[2,2,64,128]{3,2,1,0:T(8,128)(2,1)} %nk_hbm.1, ...), custom_call_target="tpu_custom_call" | custom-call | tf_op jit(solution)/shard_map/attend/pallas_call | solution.py:231
  7.0 0.0 copy-start
  7.0 22.9 %all_to_all.25.parts_ref.shares_ref = bf16[32,72,128]{2,1,0:T(8,128)(2,1)S(1)} all-to-all(bf16[32,72,128]{2,1,0:T(8,128)(2,1)} %attend.1), channel_id=1, replica_groups=mesh['seq_0'=4,'seq_1'=4,'seq_2'=2,'head'=4] {'seq_0','seq_1','seq_2'}, dimensions={0} | all-to-all | bytes 1179648 | tf_op jit(solution)/shard_map/all_to_all | solution.py:458
  29.9 0.6 join.1
  30.5 11.1 %all_to_all.26.blocks_ref = bf16[16,64,128]{2,1,0:T(8,128)(2,1)S(1)} all-to-all(bf16[16,64,128]{2,1,0:T(8,128)(2,1)S(1)} %join.1), channel_id=1, replica_groups=mesh['seq_0'=4,'seq_1'=4,'seq_2'=2,'head'=4] {'seq_1','seq_0'}, dimensions={0} | all-to-all | bytes 524288 | tf_op jit(solution)/shard_map/all_to_all | solution.py:458
  41.6 1.4 %collective-permute-start = (bf16[16,64,128]{2,1,0:T(8,128)(2,1)S(1)}, bf16[16,64,128]{2,1,0:T(8,128)(2,1)S(1)}, u32[]{:S(2)}, u32[]{:S(2)}) collective-permute-start(bf16[16,64,128]{2,1,0:T(8,128)(2,1)S(1)} %all_to_all.26.blocks_ref), channel_id=1, source_target_pairs={{0,4},{4,0},{1,5},{5,1},{2,6},{6,2},{3,7},{7,3},{8,12},{12,8},{9,1... | collective-permute-start | bytes 786440 | tf_op jit(solution)/shard_map/ppermute | solution.py:462
  43.0 0.0 copy-start.1
  43.0 1.2 %copy-done.1 = bf16[2048,256]{1,0:T(8,128)(2,1)S(1)} copy-done((bf16[2048,256]{1,0:T(8,128)(2,1)S(1)}, bf16[2048,256]{1,0:T(8,128)(2,1)}, u32[]{:S(2)}) %copy-start.1) | copy-done | bytes 1048600
  44.3 0.0 copy-start.5
  44.3 0.3 project_first.1
  44.5 0.0 collective-permute-done.blocks_ref
  44.5 0.2 project_second.1
  44.8 10.3 %all_to_all.27.parts_ref = bf16[4,128,256]{2,1,0:T(8,128)(2,1)S(1)} all-to-all(bf16[4,128,256]{2,1,0:T(8,128)(2,1)S(1)} %project_second.1), channel_id=1, replica_groups=mesh['seq_0'=4,'seq_1'=4,'seq_2'=2,'head'=4] {'head'}, dimensions={0} | all-to-all | bytes 524288 | tf_op jit(solution)/shard_map/all_to_all | solution.py:458
  55.1 0.0 copy-done.3
  55.1 0.0 copy-done.2
  55.1 0.1 stream.1
  55.2 18.5 %all_to_all.28.blocks_ref = bf16[16,128,256]{2,1,0:T(8,128)(2,1)S(1)} all-to-all(bf16[16,128,256]{2,1,0:T(8,128)(2,1)S(1)} %stream.1), channel_id=1, replica_groups=mesh['seq_0'=4,'seq_1'=4,'seq_2'=2,'head'=4] {'seq_1','seq_0'}, dimensions={0} | all-to-all | bytes 2097152 | tf_op jit(solution)/shard_map/all_to_all | solution.py:458
  73.7 0.0 copy-start.4
  73.7 2.2 %collective-permute-start.1 = (bf16[16,128,256]{2,1,0:T(8,128)(2,1)S(1)}, bf16[16,128,256]{2,1,0:T(8,128)(2,1)S(1)}, u32[]{:S(2)}, u32[]{:S(2)}) collective-permute-start(bf16[16,128,256]{2,1,0:T(8,128)(2,1)S(1)} %all_to_all.28.blocks_ref), channel_id=1, source_target_pairs={{0,4},{4,0},{1,5},{5,1},{2,6},{6,2},{3,7},{7,3},{8,12},{12,8},{9,1... | collective-permute-start | bytes 3145736 | tf_op jit(solution)/shard_map/ppermute | solution.py:462
  75.9 0.0 copy-done
  75.9 0.8 logits_first.1
  76.8 1.5 %collective-permute-done.1.blocks_ref = bf16[16,128,256]{2,1,0:T(8,128)(2,1)S(1)} collective-permute-done((bf16[16,128,256]{2,1,0:T(8,128)(2,1)S(1)}, bf16[16,128,256]{2,1,0:T(8,128)(2,1)S(1)}, u32[]{:S(2)}, u32[]{:S(2)}) %collective-permute-start.1) | collective-permute-done | bytes 1048608 | tf_op jit(solution)/shard_map/ppermute | solution.py:462
  78.2 0.0 copy-done.5
  78.2 1.2 %logits_second.1 = (f32[128,512]{1,0:T(8,128)S(1)}, f32[256,128]{1,0:T(8,128)S(1)}) custom-call(bf16[16,128,256]{2,1,0:T(8,128)(2,1)S(1)} %collective-permute-done.1.blocks_ref, bf16[32,72,128]{2,1,0:T(8,128)(2,1)S(1)} %all_to_all.25.parts_ref.shares_ref, bf16[8192,512]{1,0:T(8,128)(2,1)S(1)} %copy-done, f32[128,512]{1,0:T(8,128)S(1)} %get-tuple-element.12.product_ref, ...), custom_call_target="tpu_custom_call" | custom-call | tf_op jit(solution)/shard_map/logits_second/pallas_call | solution.py:412
  79.4 13.7 %all_to_all.29 = f32[128,2,128]{2,1,0:T(2,128)S(1)} all-to-all(f32[128,2,128]{2,1,0:T(2,128)S(1)} %bitcast.5), channel_id=1, replica_groups=mesh['seq_0'=4,'seq_1'=4,'seq_2'=2,'head'=4] {'seq_0','seq_1','seq_2','h..., dimensions={0} | all-to-all | bytes 262144 | tf_op jit(solution)/shard_map/all_to_all | solution.py:458
  93.1 0.0 copy-done.4
  93.1 1.3 %final.1 = (f32[6,2,512]{2,1,0:T(2,128)}, f32[2,64]{1,0:T(2,128)}) custom-call(s32[2,6]{1,0:T(2,128)S(1)} %copy-done.4, f32[256,128]{1,0:T(8,128)S(1)} %bitcast.4, f32[128,512]{1,0:T(8,128)S(1)} %get-tuple-element.15.logits_ref), custom_call_target="tpu_custom_call" | custom-call | tf_op jit(solution)/shard_map/final/pallas_call | solution.py:441
Async XLA Ops:
  0.6 54.4 %copy-start.3 = (bf16[256]{0:T(256)(128)(2,1)S(1)}, bf16[256]{0:T(256)(128)(2,1)}, u32[]{:S(2)}) copy-start(bf16[256]{0:T(256)(128)(2,1)} %gain_ref.1) | copy-start | bytes 1540
  0.6 54.4 %copy-start.2 = (bf16[2,64,256]{2,1,0:T(8,128)(2,1)S(1)}, bf16[2,64,256]{2,1,0:T(8,128)(2,1)}, u32[]{:S(2)}) copy-start(bf16[2,64,256]{2,1,0:T(8,128)(2,1)} %param.22) | copy-start | bytes 196612
  7.0 68.9 %copy-start = (bf16[8192,512]{1,0:T(8,128)(2,1)S(1)}, bf16[8192,512]{1,0:T(8,128)(2,1)}, u32[]{:S(2)}) copy-start(bf16[8192,512]{1,0:T(8,128)(2,1)} %weight_ref.5) | copy-start | bytes 25165828
  41.6 2.9 %collective-permute-start = (bf16[16,64,128]{2,1,0:T(8,128)(2,1)S(1)}, bf16[16,64,128]{2,1,0:T(8,128)(2,1)S(1)}, u32[]{:S(2)}, u32[]{:S(2)}) collective-permute-start(bf16[16,64,128]{2,1,0:T(8,128)(2,1)S(1)} %all_to_all.26.blocks_ref), channel_id=1, source_target_pairs={{0,4},{4,0},{1,5},{5,1},{2,6},{6,2},{3,7},{7,3},{8,12},{12,8},{9,1... | collective-permute-start | bytes 786440 | tf_op jit(solution)/shard_map/ppermute | solution.py:462
  43.0 1.2 %copy-start.1 = (bf16[2048,256]{1,0:T(8,128)(2,1)S(1)}, bf16[2048,256]{1,0:T(8,128)(2,1)}, u32[]{:S(2)}) copy-start(bf16[2048,256]{1,0:T(8,128)(2,1)} %weight_ref.3) | copy-start | bytes 3145732
  44.3 34.0 %copy-start.5 = (s32[2,64]{1,0:T(2,128)S(1)}, s32[2,64]{1,0:T(2,128)}, u32[]{:S(2)}) copy-start(s32[2,64]{1,0:T(2,128)} %tokens_ref.1) | copy-start | bytes 1540
  73.7 19.4 %copy-start.4 = (s32[2,6]{1,0:T(2,128)S(1)}, s32[2,6]{1,0:T(2,128)}, u32[]{:S(2)}) copy-start(s32[2,6]{1,0:T(2,128)} %path_ref.1) | copy-start | bytes 148
  73.7 4.5 %collective-permute-start.1 = (bf16[16,128,256]{2,1,0:T(8,128)(2,1)S(1)}, bf16[16,128,256]{2,1,0:T(8,128)(2,1)S(1)}, u32[]{:S(2)}, u32[]{:S(2)}) collective-permute-start(bf16[16,128,256]{2,1,0:T(8,128)(2,1)S(1)} %all_to_all.28.blocks_ref), channel_id=1, source_target_pairs={{0,4},{4,0},{1,5},{5,1},{2,6},{6,2},{3,7},{7,3},{8,12},{12,8},{9,1... | collective-permute-start | bytes 3145736 | tf_op jit(solution)/shard_map/ppermute | solution.py:462

commit v7 on v6

--- a/solution.py
+++ b/solution.py
@@ -342,58 +342,71 @@
     )(parts, residual, gain)
 
 
-def gathered_product(blocks_ref, shares_ref, weight_ref, core):
+def gathered_product(blocks_ref, weight_ref):
     chips, rows, columns = blocks_ref.shape
+    core = lax.axis_index("seq_2")
+    blocks, sections = [], []
+    for k in range(chips):
+        start = pl.multiple_of((2 * place_of(k) + core) * columns, columns)
+        blocks.append(blocks_ref[k])
+        sections.append(weight_ref[pl.ds(start, columns)])
+    return plain_dot(jnp.concatenate(blocks, axis=1), jnp.concatenate(sections, axis=0))
+
+
+def sent_kernel(blocks_ref, shares_ref, weight_ref, out_ref):
+    chips = blocks_ref.shape[0]
+    width = weight_ref.shape[1]
     nodes = shares_ref.shape[1] - 8
-    blocks, sections, squares = [], [], 0.0
+    core = lax.axis_index("seq_2")
+    squares = 0.0
     for k in range(chips):
-        block = blocks_ref[k]
-        blocks.append(block)
-        source = 2 * place_of(k) + core
-        sections.append(weight_ref[pl.ds(pl.multiple_of(source * columns, columns), columns)])
-        gains = shares_ref[source, nodes:].astype(f32)
+        gains = shares_ref[2 * place_of(k) + core, nodes:].astype(f32)
         for n in range(2):
             inverse = 1.0 / gains[3 + n : 4 + n]
-            plain = block[:, n * 128 : (n + 1) * 128].astype(f32) * inverse
+            plain = blocks_ref[k, :, n * 128 : (n + 1) * 128].astype(f32) * inverse
             squares = squares + plain * plain
-    product = plain_dot(jnp.concatenate(blocks, axis=1), jnp.concatenate(sections, axis=0))
-    return product, squares
-
-
-def first_kernel(blocks_ref, shares_ref, weight_ref, product_ref, squares_ref):
-    core = lax.axis_index("seq_2")
-    product_ref[...], squares_ref[...] = gathered_product(
-        blocks_ref, shares_ref, weight_ref, core
+    out_ref[:, :width] = gathered_product(blocks_ref, weight_ref)
+    out_ref[:, width:] = squares
+
+
+def kept_kernel(blocks_ref, weight_ref, out_ref):
+    out_ref[...] = gathered_product(blocks_ref, weight_ref)
+
+
+def product_cost(blocks, weight):
+    chips, rows, columns = blocks.shape
+    return pl.CostEstimate(
+        flops=2 * blocks.size * weight.shape[1],
+        bytes_accessed=2 * chips * columns * (rows + weight.shape[1]),
+        transcendentals=0,
     )
 
 
-def first_half(blocks, shares, weight):
-    chips, rows, columns = blocks.shape
-    width = weight.shape[1]
-    return pl.pallas_call(
-        first_kernel,
-        out_shape=[
-            jax.ShapeDtypeStruct((rows, width), f32),
-            jax.ShapeDtypeStruct((rows, 128), f32),
-        ],
-        cost_estimate=pl.CostEstimate(
-            flops=2 * rows * chips * columns * width,
-            bytes_accessed=2 * chips * columns * (rows + width),
-            transcendentals=0,
-        ),
+def sent_product(blocks, shares, weight):
+    return pl.pallas_call(
+        sent_kernel,
+        out_shape=jax.ShapeDtypeStruct((blocks.shape[1], weight.shape[1] + 128), f32),
+        cost_estimate=product_cost(blocks, weight),
         compiler_params=room(16),
-        name="logits_first",
+        name="logits_sent",
     )(blocks, shares, weight)
 
 
-def second_kernel(
-    blocks_ref, shares_ref, weight_ref, product_ref, squares_ref, tokens_ref, logits_ref, stats_ref
-):
-    rows, width = product_ref.shape
-    core = 1 - lax.axis_index("seq_2")
-    product, squares = gathered_product(blocks_ref, shares_ref, weight_ref, core)
-    total = jnp.sum(squares + squares_ref[...], axis=1, keepdims=True)
-    logits = (product + product_ref[...]) * lax.rsqrt(total / D + EPSILON)
+def kept_product(blocks, weight):
+    return pl.pallas_call(
+        kept_kernel,
+        out_shape=jax.ShapeDtypeStruct((blocks.shape[1], weight.shape[1]), f32),
+        cost_estimate=product_cost(blocks, weight),
+        compiler_params=room(16),
+        name="logits_kept",
+    )(blocks, weight)
+
+
+def statistics_kernel(kept_ref, sent_ref, received_ref, tokens_ref, logits_ref, stats_ref):
+    rows, width = kept_ref.shape
+    squares = sent_ref[:, width:] + received_ref[:, width:]
+    total = jnp.sum(squares, axis=1, keepdims=True)
+    logits = (kept_ref[...] + received_ref[:, :width]) * lax.rsqrt(total / D + EPSILON)
     logits_ref[...] = logits
     top = jnp.max(logits, axis=1, keepdims=True)
     sums = jnp.sum(jnp.exp(logits - top), axis=1, keepdims=True)
@@ -408,16 +421,16 @@
         stats_ref[k * 8 : k * 8 + 8] = turned
 
 
-def second_half(blocks, shares, weight, product, squares, tokens, copies):
-    return pl.pallas_call(
-        second_kernel,
+def logit_statistics(kept, sent, received, tokens, copies):
+    return pl.pallas_call(
+        statistics_kernel,
         out_shape=[
-            jax.ShapeDtypeStruct(product.shape, f32),
+            jax.ShapeDtypeStruct(kept.shape, f32),
             jax.ShapeDtypeStruct((copies * 2, 128), f32),
         ],
-        compiler_params=room(16),
-        name="logits_second",
-    )(blocks, shares, weight, product, squares, tokens)
+        compiler_params=room(8),
+        name="logits_statistics",
+    )(kept, sent, received, tokens)
 
 
 def final_kernel(path_ref, stats_ref, logits_ref, picked_ref, out_ref):
@@ -482,20 +495,22 @@
     shares = local_attention(
         queries, cache_keys, cache_values, new_keys, new_values, parents, lengths, norm_gain
     )
+    shares, own_weight = lax.optimization_barrier((shares, vocab_weight))
+    other_weight = across(own_weight)
     shares = to_each(shares, SEQ)
     heads = to_each(join_shares(shares, chips), CHIPS)
     other_heads = across(heads)
     partial, rest = project_first(heads, out_weight)
     partial = project_second(other_heads, rest, partial, lax.axis_size("head"))
+    partial, other_weight = lax.optimization_barrier((partial, other_weight))
     partial = to_each(partial, "head")
     stream = make_stream(partial, residual.reshape(rows, -1), norm_gain, chips)
     mine = to_each(stream, CHIPS)
-    other = across(mine)
-    product, squares = first_half(mine, shares, vocab_weight)
+    sent = sent_product(mine, shares, other_weight)
+    received = across(sent)
+    kept = kept_product(mine, own_weight)
     copies = lax.axis_size(SEQ_HEAD)
-    logits, stats = second_half(
-        other, shares, vocab_weight, product, squares, draft_tokens, copies
-    )
+    logits, stats = logit_statistics(kept, sent, received, draft_tokens, copies)
     stats = to_each(stats.reshape(copies, 2, 128), SEQ_HEAD).reshape(copies * 2, 128)
     path_logits, logprob = final_join(path, stats, logits)
     return (jnp.transpose(path_logits, (1, 0, 2)), logprob)

time: 94.7 us -> 94.3 us (level)
  starting transfers between devices: 3.67 us -> 5.33 us
  blocking collectives: 76.5 us -> 75.3 us
    ppermute x2 -> x3, starting transfers between devices: 3.67 us -> 5.33 us  [across(): return lax.ppermute(x, 'seq_2', [(0, 1), (1, 0)])]
    all_to_all x5, blocking collectives: 76.5 us -> 75.3 us  [to_each(): return lax.all_to_all(x, axes, 0, 0, tiled=True)]
    pallas_call x2 -> x3, Pallas kernels: 1.98 us -> 1.97 us  [the longest x1 0.81 us: sent_product(): pl.pallas_call(sent_kernel, out_shape=jax.ShapeDtypeStruct((blocks.shape[...]
  transfers between devices with their start and end apart: 2 -> 3, of which waited for: 1 -> 1; matrix products, arithmetic and copies ran while one was open for 0% -> 0% of each run, Pallas kernels for 1% -> 2%
where the time goes in v7:
time: 94.3 us; the launch traced here: 94 us
  blocking collectives  75.3 us (80%)
  Pallas kernels  10.8 us (11%)
  starting transfers between devices  5.33 us (6%)
  local copies, waits for them, and re-layouts  1.25 us (1%)
    all_to_all x5, blocking collectives, to_each(): return lax.all_to_all(x, axes, 0, 0, tiled=True)  75.3 us
    pallas_call x1, Pallas kernels, local_attention(): pl.pallas_call(attention_kernel, in_specs=[pl.BlockSpec(memory_space=pltp...  6.34 us
    ppermute x3, starting transfers between devices, across(): return lax.ppermute(x, 'seq_2', [(0, 1), (1, 0)])  5.33 us
  transfers between devices with their start and end apart: 3, of which 1 were waited for; matrix products, arithmetic and copies ran while one was open for 0% of the time, Pallas kernels for 2%

profile of v7, /device:TPU:1, one launch (start us, length us, event | category | flops | bytes accessed | tf_op | source)
XLA Modules:
  0.0 94.0 jit_solution(14010655652460549100)
XLA Ops:
  0.6 0.0 copy-start.2
  0.6 0.0 copy-start.1
  0.7 6.3 %attend.1 = bf16[32,72,128]{2,1,0:T(8,128)(2,1)} custom-call(s32[2]{0:T(128)} %lengths_hbm.1, s32[2,64]{1,0:T(2,128)} %parents_hbm.1, bf16[2,16,64,128]{3,2,1,0:T(8,128)(2,1)} %q_hbm.1, bf16[2,2,1024,128]{3,2,1,0:T(8,128)(2,1)} %k_hbm.1, bf16[2,2,1024,128]{3,2,1,0:T(8,128)(2,1)} %v_hbm.1, bf16[2,2,64,128]{3,2,1,0:T(8,128)(2,1)} %nk_hbm.1, ...), custom_call_target="tpu_custom_call" | custom-call | tf_op jit(solution)/shard_map/attend/pallas_call | solution.py:231
  7.0 1.5 %collective-permute-start.1 = (bf16[8192,512]{1,0:T(8,128)(2,1)}, bf16[8192,512]{1,0:T(8,128)(2,1)S(1)}, u32[]{:S(2)}, u32[]{:S(2)}) collective-permute-start(bf16[8192,512]{1,0:T(8,128)(2,1)} %weight_ref.2), channel_id=1, source_target_pairs={{0,4},{4,0},{1,5},{5,1},{2,6},{6,2},{3,7},{7,3},{8,12},{12,8},{9,1... | collective-permute-start | bytes 25165832 | tf_op jit(solution)/shard_map/ppermute | solution.py:475
  8.5 21.7 %all_to_all.25.parts_ref.shares_ref = bf16[32,72,128]{2,1,0:T(8,128)(2,1)S(1)} all-to-all(bf16[32,72,128]{2,1,0:T(8,128)(2,1)} %attend.1), channel_id=1, replica_groups=mesh['seq_0'=4,'seq_1'=4,'seq_2'=2,'head'=4] {'seq_0','seq_1','seq_2'}, dimensions={0} | all-to-all | bytes 1179648 | tf_op jit(solution)/shard_map/all_to_all | solution.py:471
  30.1 0.6 join.1
  30.7 11.1 %all_to_all.26.blocks_ref = bf16[16,64,128]{2,1,0:T(8,128)(2,1)S(1)} all-to-all(bf16[16,64,128]{2,1,0:T(8,128)(2,1)S(1)} %join.1), channel_id=1, replica_groups=mesh['seq_0'=4,'seq_1'=4,'seq_2'=2,'head'=4] {'seq_1','seq_0'}, dimensions={0} | all-to-all | bytes 524288 | tf_op jit(solution)/shard_map/all_to_all | solution.py:471
  41.8 0.0 slice-start
  41.8 1.4 %collective-permute-start = (bf16[16,64,128]{2,1,0:T(8,128)(2,1)S(1)}, bf16[16,64,128]{2,1,0:T(8,128)(2,1)S(1)}, u32[]{:S(2)}, u32[]{:S(2)}) collective-permute-start(bf16[16,64,128]{2,1,0:T(8,128)(2,1)S(1)} %all_to_all.26.blocks_ref), channel_id=1, source_target_pairs={{0,4},{4,0},{1,5},{5,1},{2,6},{6,2},{3,7},{7,3},{8,12},{12,8},{9,1... | collective-permute-start | bytes 786440 | tf_op jit(solution)/shard_map/ppermute | solution.py:475
  43.2 0.0 copy-start
  43.2 1.2 %copy-done = bf16[2048,256]{1,0:T(8,128)(2,1)S(1)} copy-done((bf16[2048,256]{1,0:T(8,128)(2,1)S(1)}, bf16[2048,256]{1,0:T(8,128)(2,1)}, u32[]{:S(2)}) %copy-start) | copy-done | bytes 1048600
  44.5 0.3 project_first.1
  44.7 0.0 collective-permute-done.blocks_ref
  44.7 0.2 project_second.1
  45.0 0.0 collective-permute-done.1.weight_ref
  45.0 10.2 %all_to_all.27.parts_ref = bf16[4,128,256]{2,1,0:T(8,128)(2,1)S(1)} all-to-all(bf16[4,128,256]{2,1,0:T(8,128)(2,1)S(1)} %project_second.1), channel_id=1, replica_groups=mesh['seq_0'=4,'seq_1'=4,'seq_2'=2,'head'=4] {'head'}, dimensions={0} | all-to-all | bytes 524288 | tf_op jit(solution)/shard_map/all_to_all | solution.py:471
  55.1 0.0 copy-done.2
  55.2 0.0 copy-done.1
  55.2 0.1 stream.1
  55.3 18.4 %all_to_all.28.blocks_ref = bf16[16,128,256]{2,1,0:T(8,128)(2,1)S(1)} all-to-all(bf16[16,128,256]{2,1,0:T(8,128)(2,1)S(1)} %stream.1), channel_id=1, replica_groups=mesh['seq_0'=4,'seq_1'=4,'seq_2'=2,'head'=4] {'seq_1','seq_0'}, dimensions={0} | all-to-all | bytes 2097152 | tf_op jit(solution)/shard_map/all_to_all | solution.py:471
  73.6 0.0 slice-start.1
  73.6 0.0 copy-start.4
  73.6 0.0 copy-start.3
  73.6 0.8 logits_sent.1.sent_ref
  74.5 2.4 %collective-permute-start.2 = (f32[128,640]{1,0:T(8,128)S(1)}, f32[128,640]{1,0:T(8,128)S(1)}, u32[]{:S(2)}, u32[]{:S(2)}) collective-permute-start(f32[128,640]{1,0:T(8,128)S(1)} %logits_sent.1.sent_ref), channel_id=1, source_target_pairs={{0,4},{4,0},{1,5},{5,1},{2,6},{6,2},{3,7},{7,3},{8,12},{12,8},{9,1... | collective-permute-start | bytes 983048 | tf_op jit(solution)/shard_map/ppermute | solution.py:475
  76.9 0.0 slice-done
  76.9 0.0 slice-done.1
  76.9 0.7 logits_kept.1.kept_ref
  77.6 0.5 collective-permute-done.2.received_ref
  78.2 0.0 copy-done.4
  78.2 0.5 logits_statistics.1
  78.6 14.1 %all_to_all.29 = f32[128,2,128]{2,1,0:T(2,128)S(1)} all-to-all(f32[128,2,128]{2,1,0:T(2,128)S(1)} %bitcast.7), channel_id=1, replica_groups=mesh['seq_0'=4,'seq_1'=4,'seq_2'=2,'head'=4] {'seq_0','seq_1','seq_2','h..., dimensions={0} | all-to-all | bytes 262144 | tf_op jit(solution)/shard_map/all_to_all | solution.py:471
  92.7 0.0 copy-done.3
  92.7 1.3 %final.1 = (f32[6,2,512]{2,1,0:T(2,128)}, f32[2,64]{1,0:T(2,128)}) custom-call(s32[2,6]{1,0:T(2,128)S(1)} %copy-done.3, f32[256,128]{1,0:T(8,128)S(1)} %bitcast.6, f32[128,512]{1,0:T(8,128)S(1)} %get-tuple-element.19.logits_ref), custom_call_target="tpu_custom_call" | custom-call | tf_op jit(solution)/shard_map/final/pallas_call | solution.py:454
  (1 shorter events, 0.0 us)
Async XLA Ops:
  0.6 54.5 %copy-start.2 = (bf16[256]{0:T(256)(128)(2,1)S(1)}, bf16[256]{0:T(256)(128)(2,1)}, u32[]{:S(2)}) copy-start(bf16[256]{0:T(256)(128)(2,1)} %gain_ref.1) | copy-start | bytes 1540
  0.6 54.5 %copy-start.1 = (bf16[2,64,256]{2,1,0:T(8,128)(2,1)S(1)}, bf16[2,64,256]{2,1,0:T(8,128)(2,1)}, u32[]{:S(2)}) copy-start(bf16[2,64,256]{2,1,0:T(8,128)(2,1)} %param.22) | copy-start | bytes 196612
  7.0 38.0 %collective-permute-start.1 = (bf16[8192,512]{1,0:T(8,128)(2,1)}, bf16[8192,512]{1,0:T(8,128)(2,1)S(1)}, u32[]{:S(2)}, u32[]{:S(2)}) collective-permute-start(bf16[8192,512]{1,0:T(8,128)(2,1)} %weight_ref.2), channel_id=1, source_target_pairs={{0,4},{4,0},{1,5},{5,1},{2,6},{6,2},{3,7},{7,3},{8,12},{12,8},{9,1... | collective-permute-start | bytes 25165832 | tf_op jit(solution)/shard_map/ppermute | solution.py:475
  41.8 35.1 %slice-start = ((s8[8388608]{0:T(1024)(128)(4,1)}), s8[4194304]{0:T(1024)(128)(4,1)S(1)}, s32[]{:S(2)}) async-start(s8[8388608]{0:T(1024)(128)(4,1)} %bitcast.4), calls=%async_computation.5 | async-start | bytes 8388608
  41.8 2.9 %collective-permute-start = (bf16[16,64,128]{2,1,0:T(8,128)(2,1)S(1)}, bf16[16,64,128]{2,1,0:T(8,128)(2,1)S(1)}, u32[]{:S(2)}, u32[]{:S(2)}) collective-permute-start(bf16[16,64,128]{2,1,0:T(8,128)(2,1)S(1)} %all_to_all.26.blocks_ref), channel_id=1, source_target_pairs={{0,4},{4,0},{1,5},{5,1},{2,6},{6,2},{3,7},{7,3},{8,12},{12,8},{9,1... | collective-permute-start | bytes 786440 | tf_op jit(solution)/shard_map/ppermute | solution.py:475
  43.2 1.2 %copy-start = (bf16[2048,256]{1,0:T(8,128)(2,1)S(1)}, bf16[2048,256]{1,0:T(8,128)(2,1)}, u32[]{:S(2)}) copy-start(bf16[2048,256]{1,0:T(8,128)(2,1)} %weight_ref.1) | copy-start | bytes 3145732
  73.6 3.3 %slice-start.1 = ((s8[8388608]{0:T(1024)(128)(4,1)}), s8[4194304]{0:T(1024)(128)(4,1)S(1)}, s32[]{:S(2)}) async-start(s8[8388608]{0:T(1024)(128)(4,1)} %bitcast.4), calls=%async_computation.6 | async-start | bytes 8388608
  73.6 4.5 %copy-start.4 = (s32[2,64]{1,0:T(2,128)S(1)}, s32[2,64]{1,0:T(2,128)}, u32[]{:S(2)}) copy-start(s32[2,64]{1,0:T(2,128)} %tokens_ref.1) | copy-start | bytes 1540
  73.6 19.0 %copy-start.3 = (s32[2,6]{1,0:T(2,128)S(1)}, s32[2,6]{1,0:T(2,128)}, u32[]{:S(2)}) copy-start(s32[2,6]{1,0:T(2,128)} %path_ref.1) | copy-start | bytes 148
  74.5 3.7 %collective-permute-start.2 = (f32[128,640]{1,0:T(8,128)S(1)}, f32[128,640]{1,0:T(8,128)S(1)}, u32[]{:S(2)}, u32[]{:S(2)}) collective-permute-start(f32[128,640]{1,0:T(8,128)S(1)} %logits_sent.1.sent_ref), channel_id=1, source_target_pairs={{0,4},{4,0},{1,5},{5,1},{2,6},{6,2},{3,7},{7,3},{8,12},{12,8},{9,1... | collective-permute-start | bytes 983048 | tf_op jit(solution)/shard_map/ppermute | solution.py:475

commit v8 on v7

--- a/solution.py
+++ b/solution.py
@@ -495,14 +495,13 @@
     shares = local_attention(
         queries, cache_keys, cache_values, new_keys, new_values, parents, lengths, norm_gain
     )
-    shares, own_weight = lax.optimization_barrier((shares, vocab_weight))
-    other_weight = across(own_weight)
     shares = to_each(shares, SEQ)
     heads = to_each(join_shares(shares, chips), CHIPS)
     other_heads = across(heads)
     partial, rest = project_first(heads, out_weight)
     partial = project_second(other_heads, rest, partial, lax.axis_size("head"))
-    partial, other_weight = lax.optimization_barrier((partial, other_weight))
+    partial, own_weight = lax.optimization_barrier((partial, vocab_weight))
+    other_weight = across(own_weight)
     partial = to_each(partial, "head")
     stream = make_stream(partial, residual.reshape(rows, -1), norm_gain, chips)
     mine = to_each(stream, CHIPS)

time: 94.3 us -> 93.7 us (level)
  transfers between devices with their start and end apart: 3 -> 3, of which waited for: 1 -> 1; matrix products, arithmetic and copies ran while one was open for 0% -> 0% of each run, Pallas kernels for 2% -> 1%
where the time goes in v8:
time: 93.7 us; the launch traced here: 93.4 us
  blocking collectives  75.2 us (80%)
  Pallas kernels  11 us (12%)
  starting transfers between devices  4.65 us (5%)
  local copies, waits for them, and re-layouts  1.25 us (1%)
    all_to_all x5, blocking collectives, to_each(): return lax.all_to_all(x, axes, 0, 0, tiled=True)  75.2 us
    pallas_call x1, Pallas kernels, local_attention(): pl.pallas_call(attention_kernel, in_specs=[pl.BlockSpec(memory_space=pltp...  6.49 us
    ppermute x3, starting transfers between devices, across(): return lax.ppermute(x, 'seq_2', [(0, 1), (1, 0)])  4.65 us
  transfers between devices with their start and end apart: 3, of which 1 were waited for; matrix products, arithmetic and copies ran while one was open for 0% of the time, Pallas kernels for 1%

profile of v8, /device:TPU:1, one launch (start us, length us, event | category | flops | bytes accessed | tf_op | source)
XLA Modules:
  0.0 93.4 jit_solution(2815848384925860393)
XLA Ops:
  0.6 0.0 copy-start.2
  0.6 0.0 copy-start.1
  0.7 6.5 %attend.1 = bf16[32,72,128]{2,1,0:T(8,128)(2,1)} custom-call(s32[2]{0:T(128)} %lengths_hbm.1, s32[2,64]{1,0:T(2,128)} %parents_hbm.1, bf16[2,16,64,128]{3,2,1,0:T(8,128)(2,1)} %q_hbm.1, bf16[2,2,1024,128]{3,2,1,0:T(8,128)(2,1)} %k_hbm.1, bf16[2,2,1024,128]{3,2,1,0:T(8,128)(2,1)} %v_hbm.1, bf16[2,2,64,128]{3,2,1,0:T(8,128)(2,1)} %nk_hbm.1, ...), custom_call_target="tpu_custom_call" | custom-call | tf_op jit(solution)/shard_map/attend/pallas_call | solution.py:231
  7.2 22.6 %all_to_all.25.parts_ref.shares_ref = bf16[32,72,128]{2,1,0:T(8,128)(2,1)S(1)} all-to-all(bf16[32,72,128]{2,1,0:T(8,128)(2,1)} %attend.1), channel_id=1, replica_groups=mesh['seq_0'=4,'seq_1'=4,'seq_2'=2,'head'=4] {'seq_0','seq_1','seq_2'}, dimensions={0} | all-to-all | bytes 1179648 | tf_op jit(solution)/shard_map/all_to_all | solution.py:471
  29.7 0.6 join.1
  30.3 11.1 %all_to_all.26.blocks_ref = bf16[16,64,128]{2,1,0:T(8,128)(2,1)S(1)} all-to-all(bf16[16,64,128]{2,1,0:T(8,128)(2,1)S(1)} %join.1), channel_id=1, replica_groups=mesh['seq_0'=4,'seq_1'=4,'seq_2'=2,'head'=4] {'seq_1','seq_0'}, dimensions={0} | all-to-all | bytes 524288 | tf_op jit(solution)/shard_map/all_to_all | solution.py:471
  41.4 0.0 slice-start
  41.4 1.4 %collective-permute-start = (bf16[16,64,128]{2,1,0:T(8,128)(2,1)S(1)}, bf16[16,64,128]{2,1,0:T(8,128)(2,1)S(1)}, u32[]{:S(2)}, u32[]{:S(2)}) collective-permute-start(bf16[16,64,128]{2,1,0:T(8,128)(2,1)S(1)} %all_to_all.26.blocks_ref), channel_id=1, source_target_pairs={{0,4},{4,0},{1,5},{5,1},{2,6},{6,2},{3,7},{7,3},{8,12},{12,8},{9,1... | collective-permute-start | bytes 786440 | tf_op jit(solution)/shard_map/ppermute | solution.py:475
  42.8 0.0 copy-start
  42.8 1.2 %copy-done = bf16[2048,256]{1,0:T(8,128)(2,1)S(1)} copy-done((bf16[2048,256]{1,0:T(8,128)(2,1)S(1)}, bf16[2048,256]{1,0:T(8,128)(2,1)}, u32[]{:S(2)}) %copy-start) | copy-done | bytes 1048600
  44.1 0.3 project_first.1
  44.3 0.0 collective-permute-done.blocks_ref
  44.3 0.2 project_second.1
  44.6 0.2 collective-permute-start.1
  44.8 9.6 %all_to_all.27.parts_ref = bf16[4,128,256]{2,1,0:T(8,128)(2,1)S(1)} all-to-all(bf16[4,128,256]{2,1,0:T(8,128)(2,1)S(1)} %project_second.1), channel_id=1, replica_groups=mesh['seq_0'=4,'seq_1'=4,'seq_2'=2,'head'=4] {'head'}, dimensions={0} | all-to-all | bytes 524288 | tf_op jit(solution)/shard_map/all_to_all | solution.py:471
  54.5 0.0 copy-done.2
  54.5 0.0 copy-done.1
  54.5 0.1 stream.1
  54.6 18.0 %all_to_all.28.blocks_ref = bf16[16,128,256]{2,1,0:T(8,128)(2,1)S(1)} all-to-all(bf16[16,128,256]{2,1,0:T(8,128)(2,1)S(1)} %stream.1), channel_id=1, replica_groups=mesh['seq_0'=4,'seq_1'=4,'seq_2'=2,'head'=4] {'seq_1','seq_0'}, dimensions={0} | all-to-all | bytes 2097152 | tf_op jit(solution)/shard_map/all_to_all | solution.py:471
  72.5 0.0 slice-start.1
  72.5 0.0 copy-start.4
  72.5 0.0 copy-start.3
  72.5 0.0 collective-permute-done.1.weight_ref
  72.6 0.8 logits_sent.1.sent_ref
  73.4 3.0 %collective-permute-start.2 = (f32[128,640]{1,0:T(8,128)S(1)}, f32[128,640]{1,0:T(8,128)S(1)}, u32[]{:S(2)}, u32[]{:S(2)}) collective-permute-start(f32[128,640]{1,0:T(8,128)S(1)} %logits_sent.1.sent_ref), channel_id=1, source_target_pairs={{0,4},{4,0},{1,5},{5,1},{2,6},{6,2},{3,7},{7,3},{8,12},{12,8},{9,1... | collective-permute-start | bytes 983048 | tf_op jit(solution)/shard_map/ppermute | solution.py:475
  76.4 0.0 slice-done
  76.4 0.0 slice-done.1
  76.4 0.7 logits_kept.1.kept_ref
  77.1 0.5 collective-permute-done.2.received_ref
  77.7 0.0 copy-done.4
  77.7 0.5 logits_statistics.1
  78.1 13.9 %all_to_all.29 = f32[128,2,128]{2,1,0:T(2,128)S(1)} all-to-all(f32[128,2,128]{2,1,0:T(2,128)S(1)} %bitcast.7), channel_id=1, replica_groups=mesh['seq_0'=4,'seq_1'=4,'seq_2'=2,'head'=4] {'seq_0','seq_1','seq_2','h..., dimensions={0} | all-to-all | bytes 262144 | tf_op jit(solution)/shard_map/all_to_all | solution.py:471
  92.1 0.0 copy-done.3
  92.1 1.3 %final.1 = (f32[6,2,512]{2,1,0:T(2,128)}, f32[2,64]{1,0:T(2,128)}) custom-call(s32[2,6]{1,0:T(2,128)S(1)} %copy-done.3, f32[256,128]{1,0:T(8,128)S(1)} %bitcast.6, f32[128,512]{1,0:T(8,128)S(1)} %get-tuple-element.15.logits_ref), custom_call_target="tpu_custom_call" | custom-call | tf_op jit(solution)/shard_map/final/pallas_call | solution.py:454
  (1 shorter events, 0.0 us)
Async XLA Ops:
  0.6 53.8 %copy-start.2 = (bf16[256]{0:T(256)(128)(2,1)S(1)}, bf16[256]{0:T(256)(128)(2,1)}, u32[]{:S(2)}) copy-start(bf16[256]{0:T(256)(128)(2,1)} %gain_ref.1) | copy-start | bytes 1540
  0.6 53.8 %copy-start.1 = (bf16[2,64,256]{2,1,0:T(8,128)(2,1)S(1)}, bf16[2,64,256]{2,1,0:T(8,128)(2,1)}, u32[]{:S(2)}) copy-start(bf16[2,64,256]{2,1,0:T(8,128)(2,1)} %param.22) | copy-start | bytes 196612
  41.4 35.0 %slice-start = ((s8[8388608]{0:T(1024)(128)(4,1)}), s8[4194304]{0:T(1024)(128)(4,1)S(1)}, s32[]{:S(2)}) async-start(s8[8388608]{0:T(1024)(128)(4,1)} %bitcast.4), calls=%async_computation.5 | async-start | bytes 8388608
  41.4 2.9 %collective-permute-start = (bf16[16,64,128]{2,1,0:T(8,128)(2,1)S(1)}, bf16[16,64,128]{2,1,0:T(8,128)(2,1)S(1)}, u32[]{:S(2)}, u32[]{:S(2)}) collective-permute-start(bf16[16,64,128]{2,1,0:T(8,128)(2,1)S(1)} %all_to_all.26.blocks_ref), channel_id=1, source_target_pairs={{0,4},{4,0},{1,5},{5,1},{2,6},{6,2},{3,7},{7,3},{8,12},{12,8},{9,1... | collective-permute-start | bytes 786440 | tf_op jit(solution)/shard_map/ppermute | solution.py:475
  42.8 1.2 %copy-start = (bf16[2048,256]{1,0:T(8,128)(2,1)S(1)}, bf16[2048,256]{1,0:T(8,128)(2,1)}, u32[]{:S(2)}) copy-start(bf16[2048,256]{1,0:T(8,128)(2,1)} %weight_ref.1) | copy-start | bytes 3145732
  44.6 28.0 %collective-permute-start.1 = (bf16[8192,512]{1,0:T(8,128)(2,1)}, bf16[8192,512]{1,0:T(8,128)(2,1)S(1)}, u32[]{:S(2)}, u32[]{:S(2)}) collective-permute-start(bf16[8192,512]{1,0:T(8,128)(2,1)} %weight_ref.2), channel_id=1, source_target_pairs={{0,4},{4,0},{1,5},{5,1},{2,6},{6,2},{3,7},{7,3},{8,12},{12,8},{9,1... | collective-permute-start | bytes 25165832 | tf_op jit(solution)/shard_map/ppermute | solution.py:475
  72.5 3.9 %slice-start.1 = ((s8[8388608]{0:T(1024)(128)(4,1)}), s8[4194304]{0:T(1024)(128)(4,1)S(1)}, s32[]{:S(2)}) async-start(s8[8388608]{0:T(1024)(128)(4,1)} %bitcast.4), calls=%async_computation.6 | async-start | bytes 8388608
  72.5 5.1 %copy-start.4 = (s32[2,64]{1,0:T(2,128)S(1)}, s32[2,64]{1,0:T(2,128)}, u32[]{:S(2)}) copy-start(s32[2,64]{1,0:T(2,128)} %tokens_ref.1) | copy-start | bytes 1540
  72.5 19.5 %copy-start.3 = (s32[2,6]{1,0:T(2,128)S(1)}, s32[2,6]{1,0:T(2,128)}, u32[]{:S(2)}) copy-start(s32[2,6]{1,0:T(2,128)} %path_ref.1) | copy-start | bytes 148
  73.4 4.3 %collective-permute-start.2 = (f32[128,640]{1,0:T(8,128)S(1)}, f32[128,640]{1,0:T(8,128)S(1)}, u32[]{:S(2)}, u32[]{:S(2)}) collective-permute-start(f32[128,640]{1,0:T(8,128)S(1)} %logits_sent.1.sent_ref), channel_id=1, source_target_pairs={{0,4},{4,0},{1,5},{5,1},{2,6},{6,2},{3,7},{7,3},{8,12},{12,8},{9,1... | collective-permute-start | bytes 983048 | tf_op jit(solution)/shard_map/ppermute | solution.py:475

commit v9 on v8

--- a/solution.py
+++ b/solution.py
@@ -433,11 +433,13 @@
     )(kept, sent, received, tokens)
 
 
-def final_kernel(path_ref, stats_ref, logits_ref, picked_ref, out_ref):
+def final_kernel(path_ref, stats_ref, logits_ref, picked_hbm, out_ref, picked_ref, sem):
     batch, nodes = out_ref.shape
     for b in range(batch):
         for k in range(path_ref.shape[1]):
             picked_ref[k, b : b + 1] = logits_ref[pl.ds(path_ref[b, k] + b * nodes, 1)]
+    copy = pltpu.make_async_copy(picked_ref, picked_hbm, sem)
+    copy.start()
     stats = stats_ref[...]
     is_sum = lax.broadcasted_iota(jnp.int32, stats.shape, 0) % 2 == 0
     sums = jnp.where(is_sum, stats, HIDDEN)
@@ -446,6 +448,7 @@
     result = jnp.sum(jnp.where(is_sum, 0.0, stats), axis=0, keepdims=True) - total
     for b in range(batch):
         out_ref[b : b + 1] = result[:, b * nodes : (b + 1) * nodes]
+    copy.wait()
 
 
 def final_join(path, stats, logits):
@@ -461,6 +464,14 @@
         out_shape=[
             jax.ShapeDtypeStruct((*path.shape[::-1], width), f32),
             jax.ShapeDtypeStruct((batch, rows // batch), f32),
+        ],
+        out_specs=[
+            pl.BlockSpec(memory_space=pltpu.HBM),
+            pl.BlockSpec(memory_space=pltpu.VMEM),
+        ],
+        scratch_shapes=[
+            pltpu.VMEM((*path.shape[::-1], width), f32),
+            pltpu.SemaphoreType.DMA,
         ],
         compiler_params=room(4),
         name="final",

time: 93.7 us -> 94.3 us (level)
  no operation moved by 1% of the time
where the time goes in v9:
time: 94.3 us; the launch traced here: 93.9 us
  blocking collectives  75.2 us (80%)
  Pallas kernels  11.5 us (12%)
  starting transfers between devices  4.65 us (5%)
  local copies, waits for them, and re-layouts  1.25 us (1%)
    all_to_all x5, blocking collectives, to_each(): return lax.all_to_all(x, axes, 0, 0, tiled=True)  75.2 us
    pallas_call x1, Pallas kernels, local_attention(): pl.pallas_call(attention_kernel, in_specs=[pl.BlockSpec(memory_space=pltp...  6.49 us
    ppermute x3, starting transfers between devices, across(): return lax.ppermute(x, 'seq_2', [(0, 1), (1, 0)])  4.65 us
  transfers between devices with their start and end apart: 3, of which 1 were waited for; matrix products, arithmetic and copies ran while one was open for 0% of the time, Pallas kernels for 1%

profile of v9, /device:TPU:1, one launch (start us, length us, event | category | flops | bytes accessed | tf_op | source)
XLA Modules:
  0.0 93.9 jit_solution(2514645568262670269)
XLA Ops:
  0.6 0.0 copy-start.2
  0.6 0.0 copy-start.1
  0.7 6.5 %attend.1 = bf16[32,72,128]{2,1,0:T(8,128)(2,1)} custom-call(s32[2]{0:T(128)} %lengths_hbm.1, s32[2,64]{1,0:T(2,128)} %parents_hbm.1, bf16[2,16,64,128]{3,2,1,0:T(8,128)(2,1)} %q_hbm.1, bf16[2,2,1024,128]{3,2,1,0:T(8,128)(2,1)} %k_hbm.1, bf16[2,2,1024,128]{3,2,1,0:T(8,128)(2,1)} %v_hbm.1, bf16[2,2,64,128]{3,2,1,0:T(8,128)(2,1)} %nk_hbm.1, ...), custom_call_target="tpu_custom_call" | custom-call | tf_op jit(solution)/shard_map/attend/pallas_call | solution.py:231
  7.2 22.6 %all_to_all.25.parts_ref.shares_ref = bf16[32,72,128]{2,1,0:T(8,128)(2,1)S(1)} all-to-all(bf16[32,72,128]{2,1,0:T(8,128)(2,1)} %attend.1), channel_id=1, replica_groups=mesh['seq_0'=4,'seq_1'=4,'seq_2'=2,'head'=4] {'seq_0','seq_1','seq_2'}, dimensions={0} | all-to-all | bytes 1179648 | tf_op jit(solution)/shard_map/all_to_all | solution.py:482
  29.7 0.6 join.1
  30.3 11.1 %all_to_all.26.blocks_ref = bf16[16,64,128]{2,1,0:T(8,128)(2,1)S(1)} all-to-all(bf16[16,64,128]{2,1,0:T(8,128)(2,1)S(1)} %join.1), channel_id=1, replica_groups=mesh['seq_0'=4,'seq_1'=4,'seq_2'=2,'head'=4] {'seq_1','seq_0'}, dimensions={0} | all-to-all | bytes 524288 | tf_op jit(solution)/shard_map/all_to_all | solution.py:482
  41.4 0.0 slice-start
  41.4 1.4 %collective-permute-start = (bf16[16,64,128]{2,1,0:T(8,128)(2,1)S(1)}, bf16[16,64,128]{2,1,0:T(8,128)(2,1)S(1)}, u32[]{:S(2)}, u32[]{:S(2)}) collective-permute-start(bf16[16,64,128]{2,1,0:T(8,128)(2,1)S(1)} %all_to_all.26.blocks_ref), channel_id=1, source_target_pairs={{0,4},{4,0},{1,5},{5,1},{2,6},{6,2},{3,7},{7,3},{8,12},{12,8},{9,1... | collective-permute-start | bytes 786440 | tf_op jit(solution)/shard_map/ppermute | solution.py:486
  42.8 0.0 copy-start
  42.8 1.2 %copy-done = bf16[2048,256]{1,0:T(8,128)(2,1)S(1)} copy-done((bf16[2048,256]{1,0:T(8,128)(2,1)S(1)}, bf16[2048,256]{1,0:T(8,128)(2,1)}, u32[]{:S(2)}) %copy-start) | copy-done | bytes 1048600
  44.1 0.3 project_first.1
  44.3 0.0 collective-permute-done.blocks_ref
  44.3 0.2 project_second.1
  44.6 0.2 collective-permute-start.1
  44.8 9.6 %all_to_all.27.parts_ref = bf16[4,128,256]{2,1,0:T(8,128)(2,1)S(1)} all-to-all(bf16[4,128,256]{2,1,0:T(8,128)(2,1)S(1)} %project_second.1), channel_id=1, replica_groups=mesh['seq_0'=4,'seq_1'=4,'seq_2'=2,'head'=4] {'head'}, dimensions={0} | all-to-all | bytes 524288 | tf_op jit(solution)/shard_map/all_to_all | solution.py:482
  54.5 0.0 copy-done.2
  54.5 0.0 copy-done.1
  54.5 0.1 stream.1
  54.6 18.0 %all_to_all.28.blocks_ref = bf16[16,128,256]{2,1,0:T(8,128)(2,1)S(1)} all-to-all(bf16[16,128,256]{2,1,0:T(8,128)(2,1)S(1)} %stream.1), channel_id=1, replica_groups=mesh['seq_0'=4,'seq_1'=4,'seq_2'=2,'head'=4] {'seq_1','seq_0'}, dimensions={0} | all-to-all | bytes 2097152 | tf_op jit(solution)/shard_map/all_to_all | solution.py:482
  72.5 0.0 slice-start.1
  72.5 0.0 copy-start.4
  72.5 0.0 copy-start.3
  72.5 0.0 collective-permute-done.1.weight_ref
  72.6 0.8 logits_sent.1.sent_ref
  73.4 3.0 %collective-permute-start.2 = (f32[128,640]{1,0:T(8,128)S(1)}, f32[128,640]{1,0:T(8,128)S(1)}, u32[]{:S(2)}, u32[]{:S(2)}) collective-permute-start(f32[128,640]{1,0:T(8,128)S(1)} %logits_sent.1.sent_ref), channel_id=1, source_target_pairs={{0,4},{4,0},{1,5},{5,1},{2,6},{6,2},{3,7},{7,3},{8,12},{12,8},{9,1... | collective-permute-start | bytes 983048 | tf_op jit(solution)/shard_map/ppermute | solution.py:486
  76.4 0.0 slice-done
  76.4 0.0 slice-done.1
  76.4 0.7 logits_kept.1.kept_ref
  77.1 0.5 collective-permute-done.2.received_ref
  77.7 0.0 copy-done.4
  77.7 0.5 logits_statistics.1
  78.1 13.9 %all_to_all.29 = f32[128,2,128]{2,1,0:T(2,128)S(1)} all-to-all(f32[128,2,128]{2,1,0:T(2,128)S(1)} %bitcast.7), channel_id=1, replica_groups=mesh['seq_0'=4,'seq_1'=4,'seq_2'=2,'head'=4] {'seq_0','seq_1','seq_2','h..., dimensions={0} | all-to-all | bytes 262144 | tf_op jit(solution)/shard_map/all_to_all | solution.py:482
  92.1 0.0 copy-done.3
  92.1 1.8 %final.1 = (f32[6,2,512]{2,1,0:T(2,128)}, f32[2,64]{1,0:T(2,128)}) custom-call(s32[2,6]{1,0:T(2,128)S(1)} %copy-done.3, f32[256,128]{1,0:T(8,128)S(1)} %bitcast.6, f32[128,512]{1,0:T(8,128)S(1)} %get-tuple-element.15.logits_ref), custom_call_target="tpu_custom_call" | custom-call | tf_op jit(solution)/shard_map/final/pallas_call | solution.py:457
  (1 shorter events, 0.0 us)
Async XLA Ops:
  0.6 53.8 %copy-start.2 = (bf16[256]{0:T(256)(128)(2,1)S(1)}, bf16[256]{0:T(256)(128)(2,1)}, u32[]{:S(2)}) copy-start(bf16[256]{0:T(256)(128)(2,1)} %gain_ref.1) | copy-start | bytes 1540
  0.6 53.8 %copy-start.1 = (bf16[2,64,256]{2,1,0:T(8,128)(2,1)S(1)}, bf16[2,64,256]{2,1,0:T(8,128)(2,1)}, u32[]{:S(2)}) copy-start(bf16[2,64,256]{2,1,0:T(8,128)(2,1)} %param.22) | copy-start | bytes 196612
  41.4 35.0 %slice-start = ((s8[8388608]{0:T(1024)(128)(4,1)}), s8[4194304]{0:T(1024)(128)(4,1)S(1)}, s32[]{:S(2)}) async-start(s8[8388608]{0:T(1024)(128)(4,1)} %bitcast.4), calls=%async_computation.5 | async-start | bytes 8388608
  41.4 2.9 %collective-permute-start = (bf16[16,64,128]{2,1,0:T(8,128)(2,1)S(1)}, bf16[16,64,128]{2,1,0:T(8,128)(2,1)S(1)}, u32[]{:S(2)}, u32[]{:S(2)}) collective-permute-start(bf16[16,64,128]{2,1,0:T(8,128)(2,1)S(1)} %all_to_all.26.blocks_ref), channel_id=1, source_target_pairs={{0,4},{4,0},{1,5},{5,1},{2,6},{6,2},{3,7},{7,3},{8,12},{12,8},{9,1... | collective-permute-start | bytes 786440 | tf_op jit(solution)/shard_map/ppermute | solution.py:486
  42.8 1.2 %copy-start = (bf16[2048,256]{1,0:T(8,128)(2,1)S(1)}, bf16[2048,256]{1,0:T(8,128)(2,1)}, u32[]{:S(2)}) copy-start(bf16[2048,256]{1,0:T(8,128)(2,1)} %weight_ref.1) | copy-start | bytes 3145732
  44.6 28.0 %collective-permute-start.1 = (bf16[8192,512]{1,0:T(8,128)(2,1)}, bf16[8192,512]{1,0:T(8,128)(2,1)S(1)}, u32[]{:S(2)}, u32[]{:S(2)}) collective-permute-start(bf16[8192,512]{1,0:T(8,128)(2,1)} %weight_ref.2), channel_id=1, source_target_pairs={{0,4},{4,0},{1,5},{5,1},{2,6},{6,2},{3,7},{7,3},{8,12},{12,8},{9,1... | collective-permute-start | bytes 25165832 | tf_op jit(solution)/shard_map/ppermute | solution.py:486
  72.5 3.9 %slice-start.1 = ((s8[8388608]{0:T(1024)(128)(4,1)}), s8[4194304]{0:T(1024)(128)(4,1)S(1)}, s32[]{:S(2)}) async-start(s8[8388608]{0:T(1024)(128)(4,1)} %bitcast.4), calls=%async_computation.6 | async-start | bytes 8388608
  72.5 5.1 %copy-start.4 = (s32[2,64]{1,0:T(2,128)S(1)}, s32[2,64]{1,0:T(2,128)}, u32[]{:S(2)}) copy-start(s32[2,64]{1,0:T(2,128)} %tokens_ref.1) | copy-start | bytes 1540
  72.5 19.5 %copy-start.3 = (s32[2,6]{1,0:T(2,128)S(1)}, s32[2,6]{1,0:T(2,128)}, u32[]{:S(2)}) copy-start(s32[2,6]{1,0:T(2,128)} %path_ref.1) | copy-start | bytes 148
  73.4 4.3 %collective-permute-start.2 = (f32[128,640]{1,0:T(8,128)S(1)}, f32[128,640]{1,0:T(8,128)S(1)}, u32[]{:S(2)}, u32[]{:S(2)}) collective-permute-start(f32[128,640]{1,0:T(8,128)S(1)} %logits_sent.1.sent_ref), channel_id=1, source_target_pairs={{0,4},{4,0},{1,5},{5,1},{2,6},{6,2},{3,7},{7,3},{8,12},{12,8},{9,1... | collective-permute-start | bytes 983048 | tf_op jit(solution)/shard_map/ppermute | solution.py:486

commit v10 on v8

--- a/solution.py
+++ b/solution.py
@@ -17,7 +17,7 @@
 FLOOR = -1e25
 EPSILON = 1e-5
 LOG2E = 1.4426950408889634
-ROWS = 256
+ROWS = 128
 
 f32 = jnp.float32
 bf16 = jnp.bfloat16

time: 93.7 us -> 93.6 us (level)
  no operation moved by 1% of the time
where the time goes in v10:
time: 93.6 us; the launch traced here: 93.2 us
  blocking collectives  75 us (80%)
  Pallas kernels  11.1 us (12%)
  starting transfers between devices  4.66 us (5%)
  local copies, waits for them, and re-layouts  1.25 us (1%)
    all_to_all x5, blocking collectives, to_each(): return lax.all_to_all(x, axes, 0, 0, tiled=True)  75 us
    pallas_call x1, Pallas kernels, local_attention(): pl.pallas_call(attention_kernel, in_specs=[pl.BlockSpec(memory_space=pltp...  6.58 us
    ppermute x3, starting transfers between devices, across(): return lax.ppermute(x, 'seq_2', [(0, 1), (1, 0)])  4.66 us
  transfers between devices with their start and end apart: 3, of which 1 were waited for; matrix products, arithmetic and copies ran while one was open for 0% of the time, Pallas kernels for 1%

profile of v10, /device:TPU:1, one launch (start us, length us, event | category | flops | bytes accessed | tf_op | source)
XLA Modules:
  0.0 93.2 jit_solution(8404350678615598616)
XLA Ops:
  0.6 0.0 copy-start.2
  0.6 0.0 copy-start.1
  0.7 6.6 %attend.1 = bf16[32,72,128]{2,1,0:T(8,128)(2,1)} custom-call(s32[2]{0:T(128)} %lengths_hbm.1, s32[2,64]{1,0:T(2,128)} %parents_hbm.1, bf16[2,16,64,128]{3,2,1,0:T(8,128)(2,1)} %q_hbm.1, bf16[2,2,1024,128]{3,2,1,0:T(8,128)(2,1)} %k_hbm.1, bf16[2,2,1024,128]{3,2,1,0:T(8,128)(2,1)} %v_hbm.1, bf16[2,2,64,128]{3,2,1,0:T(8,128)(2,1)} %nk_hbm.1, ...), custom_call_target="tpu_custom_call" | custom-call | tf_op jit(solution)/shard_map/attend/pallas_call | solution.py:231
  7.2 22.4 %all_to_all.25.parts_ref.shares_ref = bf16[32,72,128]{2,1,0:T(8,128)(2,1)S(1)} all-to-all(bf16[32,72,128]{2,1,0:T(8,128)(2,1)} %attend.1), channel_id=1, replica_groups=mesh['seq_0'=4,'seq_1'=4,'seq_2'=2,'head'=4] {'seq_0','seq_1','seq_2'}, dimensions={0} | all-to-all | bytes 1179648 | tf_op jit(solution)/shard_map/all_to_all | solution.py:471
  29.6 0.6 join.1
  30.2 11.1 %all_to_all.26.blocks_ref = bf16[16,64,128]{2,1,0:T(8,128)(2,1)S(1)} all-to-all(bf16[16,64,128]{2,1,0:T(8,128)(2,1)S(1)} %join.1), channel_id=1, replica_groups=mesh['seq_0'=4,'seq_1'=4,'seq_2'=2,'head'=4] {'seq_1','seq_0'}, dimensions={0} | all-to-all | bytes 524288 | tf_op jit(solution)/shard_map/all_to_all | solution.py:471
  41.3 0.0 slice-start
  41.3 1.4 %collective-permute-start = (bf16[16,64,128]{2,1,0:T(8,128)(2,1)S(1)}, bf16[16,64,128]{2,1,0:T(8,128)(2,1)S(1)}, u32[]{:S(2)}, u32[]{:S(2)}) collective-permute-start(bf16[16,64,128]{2,1,0:T(8,128)(2,1)S(1)} %all_to_all.26.blocks_ref), channel_id=1, source_target_pairs={{0,4},{4,0},{1,5},{5,1},{2,6},{6,2},{3,7},{7,3},{8,12},{12,8},{9,1... | collective-permute-start | bytes 786440 | tf_op jit(solution)/shard_map/ppermute | solution.py:475
  42.7 0.0 copy-start
  42.7 1.2 %copy-done = bf16[2048,256]{1,0:T(8,128)(2,1)S(1)} copy-done((bf16[2048,256]{1,0:T(8,128)(2,1)S(1)}, bf16[2048,256]{1,0:T(8,128)(2,1)}, u32[]{:S(2)}) %copy-start) | copy-done | bytes 1048600
  43.9 0.3 project_first.1
  44.2 0.0 collective-permute-done.blocks_ref
  44.2 0.2 project_second.1
  44.5 0.2 collective-permute-start.1
  44.7 9.6 %all_to_all.27.parts_ref = bf16[4,128,256]{2,1,0:T(8,128)(2,1)S(1)} all-to-all(bf16[4,128,256]{2,1,0:T(8,128)(2,1)S(1)} %project_second.1), channel_id=1, replica_groups=mesh['seq_0'=4,'seq_1'=4,'seq_2'=2,'head'=4] {'head'}, dimensions={0} | all-to-all | bytes 524288 | tf_op jit(solution)/shard_map/all_to_all | solution.py:471
  54.3 0.0 copy-done.2
  54.3 0.0 copy-done.1
  54.4 0.1 stream.1
  54.5 18.0 %all_to_all.28.blocks_ref = bf16[16,128,256]{2,1,0:T(8,128)(2,1)S(1)} all-to-all(bf16[16,128,256]{2,1,0:T(8,128)(2,1)S(1)} %stream.1), channel_id=1, replica_groups=mesh['seq_0'=4,'seq_1'=4,'seq_2'=2,'head'=4] {'seq_1','seq_0'}, dimensions={0} | all-to-all | bytes 2097152 | tf_op jit(solution)/shard_map/all_to_all | solution.py:471
  72.4 0.0 slice-start.1
  72.4 0.0 copy-start.4
  72.4 0.0 copy-start.3
  72.4 0.0 collective-permute-done.1.weight_ref
  72.4 0.8 logits_sent.1.sent_ref
  73.3 3.0 %collective-permute-start.2 = (f32[128,640]{1,0:T(8,128)S(1)}, f32[128,640]{1,0:T(8,128)S(1)}, u32[]{:S(2)}, u32[]{:S(2)}) collective-permute-start(f32[128,640]{1,0:T(8,128)S(1)} %logits_sent.1.sent_ref), channel_id=1, source_target_pairs={{0,4},{4,0},{1,5},{5,1},{2,6},{6,2},{3,7},{7,3},{8,12},{12,8},{9,1... | collective-permute-start | bytes 983048 | tf_op jit(solution)/shard_map/ppermute | solution.py:475
  76.3 0.0 slice-done
  76.3 0.0 slice-done.1
  76.3 0.7 logits_kept.1.kept_ref
  77.0 0.5 collective-permute-done.2.received_ref
  77.5 0.0 copy-done.4
  77.5 0.5 logits_statistics.1
  78.0 13.9 %all_to_all.29 = f32[128,2,128]{2,1,0:T(2,128)S(1)} all-to-all(f32[128,2,128]{2,1,0:T(2,128)S(1)} %bitcast.7), channel_id=1, replica_groups=mesh['seq_0'=4,'seq_1'=4,'seq_2'=2,'head'=4] {'seq_0','seq_1','seq_2','h..., dimensions={0} | all-to-all | bytes 262144 | tf_op jit(solution)/shard_map/all_to_all | solution.py:471
  91.9 0.0 copy-done.3
  92.0 1.3 %final.1 = (f32[6,2,512]{2,1,0:T(2,128)}, f32[2,64]{1,0:T(2,128)}) custom-call(s32[2,6]{1,0:T(2,128)S(1)} %copy-done.3, f32[256,128]{1,0:T(8,128)S(1)} %bitcast.6, f32[128,512]{1,0:T(8,128)S(1)} %get-tuple-element.15.logits_ref), custom_call_target="tpu_custom_call" | custom-call | tf_op jit(solution)/shard_map/final/pallas_call | solution.py:454
  (1 shorter events, 0.0 us)
Async XLA Ops:
  0.6 53.7 %copy-start.2 = (bf16[256]{0:T(256)(128)(2,1)S(1)}, bf16[256]{0:T(256)(128)(2,1)}, u32[]{:S(2)}) copy-start(bf16[256]{0:T(256)(128)(2,1)} %gain_ref.1) | copy-start | bytes 1540
  0.6 53.7 %copy-start.1 = (bf16[2,64,256]{2,1,0:T(8,128)(2,1)S(1)}, bf16[2,64,256]{2,1,0:T(8,128)(2,1)}, u32[]{:S(2)}) copy-start(bf16[2,64,256]{2,1,0:T(8,128)(2,1)} %param.22) | copy-start | bytes 196612
  41.3 35.0 %slice-start = ((s8[8388608]{0:T(1024)(128)(4,1)}), s8[4194304]{0:T(1024)(128)(4,1)S(1)}, s32[]{:S(2)}) async-start(s8[8388608]{0:T(1024)(128)(4,1)} %bitcast.4), calls=%async_computation.5 | async-start | bytes 8388608
  41.3 2.9 %collective-permute-start = (bf16[16,64,128]{2,1,0:T(8,128)(2,1)S(1)}, bf16[16,64,128]{2,1,0:T(8,128)(2,1)S(1)}, u32[]{:S(2)}, u32[]{:S(2)}) collective-permute-start(bf16[16,64,128]{2,1,0:T(8,128)(2,1)S(1)} %all_to_all.26.blocks_ref), channel_id=1, source_target_pairs={{0,4},{4,0},{1,5},{5,1},{2,6},{6,2},{3,7},{7,3},{8,12},{12,8},{9,1... | collective-permute-start | bytes 786440 | tf_op jit(solution)/shard_map/ppermute | solution.py:475
  42.7 1.2 %copy-start = (bf16[2048,256]{1,0:T(8,128)(2,1)S(1)}, bf16[2048,256]{1,0:T(8,128)(2,1)}, u32[]{:S(2)}) copy-start(bf16[2048,256]{1,0:T(8,128)(2,1)} %weight_ref.1) | copy-start | bytes 3145732
  44.5 28.0 %collective-permute-start.1 = (bf16[8192,512]{1,0:T(8,128)(2,1)}, bf16[8192,512]{1,0:T(8,128)(2,1)S(1)}, u32[]{:S(2)}, u32[]{:S(2)}) collective-permute-start(bf16[8192,512]{1,0:T(8,128)(2,1)} %weight_ref.2), channel_id=1, source_target_pairs={{0,4},{4,0},{1,5},{5,1},{2,6},{6,2},{3,7},{7,3},{8,12},{12,8},{9,1... | collective-permute-start | bytes 25165832 | tf_op jit(solution)/shard_map/ppermute | solution.py:475
  72.4 3.9 %slice-start.1 = ((s8[8388608]{0:T(1024)(128)(4,1)}), s8[4194304]{0:T(1024)(128)(4,1)S(1)}, s32[]{:S(2)}) async-start(s8[8388608]{0:T(1024)(128)(4,1)} %bitcast.4), calls=%async_computation.6 | async-start | bytes 8388608
  72.4 5.1 %copy-start.4 = (s32[2,64]{1,0:T(2,128)S(1)}, s32[2,64]{1,0:T(2,128)}, u32[]{:S(2)}) copy-start(s32[2,64]{1,0:T(2,128)} %tokens_ref.1) | copy-start | bytes 1540
  72.4 19.5 %copy-start.3 = (s32[2,6]{1,0:T(2,128)S(1)}, s32[2,6]{1,0:T(2,128)}, u32[]{:S(2)}) copy-start(s32[2,6]{1,0:T(2,128)} %path_ref.1) | copy-start | bytes 148
  73.3 4.3 %collective-permute-start.2 = (f32[128,640]{1,0:T(8,128)S(1)}, f32[128,640]{1,0:T(8,128)S(1)}, u32[]{:S(2)}, u32[]{:S(2)}) collective-permute-start(f32[128,640]{1,0:T(8,128)S(1)} %logits_sent.1.sent_ref), channel_id=1, source_target_pairs={{0,4},{4,0},{1,5},{5,1},{2,6},{6,2},{3,7},{7,3},{8,12},{12,8},{9,1... | collective-permute-start | bytes 983048 | tf_op jit(solution)/shard_map/ppermute | solution.py:475
